TPU v7x, 8 devices: a whole 2x2x1 slice. The times are simulated.
8 devices in a mesh: fsdp: 8 (over z, y, x, core).
Axes of the slice: x: 2, y: 2, z: 1, core: 2. Of those that a mesh axis runs over, the one named last changes fastest.
Arguments:
- hidden: bfloat16 [24, 512, 2048], P('fsdp')
- positions: int32 [24, 512], P('fsdp')
- grad_y: bfloat16 [24, 512, 2048], P('fsdp')
- attn_gain: bfloat16 [2048], P('fsdp')
- w_qkv: bfloat16 [2048, 2560], P('fsdp')
- b_qkv: bfloat16 [2560], P('fsdp')
- w_out: bfloat16 [2048, 2048], P('fsdp')
- mlp_gain: bfloat16 [2048], P('fsdp')
- w_up: bfloat16 [2048, 22016], P('fsdp')
- w_down: bfloat16 [11008, 2048], P('fsdp')
Outputs:
- output 1: bfloat16 [24, 512, 2048], P('fsdp')
- output 2: bfloat16 [24, 512, 2048], P('fsdp')
- output 3: float32 [2048], P('fsdp')
- output 4: float32 [2048, 2560], P('fsdp')
- output 5: float32 [2560], P('fsdp')
- output 6: float32 [2048, 2048], P('fsdp')
- output 7: float32 [2048], P('fsdp')
- output 8: float32 [2048, 22016], P('fsdp')
- output 9: float32 [11008, 2048], P('fsdp')
All inputs are finite; a program needn't handle non-finite values.
Results may differ from a plain program's by a relative error of at most 0.0161931.
Values are sent between devices in bfloat16 or wider.
A program may use at most 1 GiB of HBM per device.

v0:
```python
import functools

import jax
import jax.numpy as jnp
from jax import lax
from jax.experimental import pallas as pl
from jax.experimental.pallas import tpu as pltpu
from jax.sharding import PartitionSpec as P


HEAD_DIM = 128
ROT_DIM = 64
ROPE_BASE = 10000.0
EPS = 1e-5

NT_DIMS = (((1,), (1,)), ((), ()))
TN_DIMS = (((0,), (0,)), ((), ()))
NN_DIMS = (((1,), (0,)), ((), ()))
F32 = jnp.float32
BF16 = jnp.bfloat16
SCALE = HEAD_DIM ** -0.5
MASKED = -1e30
Q_BLOCK = 256


def mm(a, b, dims):
    return lax.dot_general(a, b, dims, preferred_element_type=F32)


def after(*vals):
    return lax.optimization_barrier(vals)


def norm_scale(rows_in):
    return lax.rsqrt(jnp.mean(rows_in * rows_in, axis=-1, keepdims=True) + EPS)


def rope_tables(positions):
    lane = jnp.arange(HEAD_DIM, dtype=jnp.int32)
    pair = (lane - lane % 2).astype(F32)
    inv_freq = 1.0 / (ROPE_BASE ** (pair / ROT_DIM))
    angles = positions.astype(F32).reshape(-1, 1) * inv_freq
    turned = lane < ROT_DIM
    sines = jnp.sin(angles)
    return jnp.where(turned, jnp.cos(angles), 1.0), jnp.where(turned, jnp.where(lane % 2 == 0, -sines, sines), 0.0)


def swap_pairs(v):
    lane = lax.broadcasted_iota(jnp.int32, v.shape, 1)
    return jnp.where(lane % 2 == 0, pltpu.roll(v, HEAD_DIM - 1, 1), pltpu.roll(v, 1, 1))


def causal_probs(q, k, row0):
    s = mm(q, k, NT_DIMS) * SCALE
    row = lax.broadcasted_iota(jnp.int32, s.shape, 0) + row0
    col = lax.broadcasted_iota(jnp.int32, s.shape, 1)
    s = jnp.where(row >= col, s, MASKED)
    e = jnp.exp(s - jnp.max(s, axis=1, keepdims=True))
    return e * (1.0 / jnp.sum(e, axis=1, keepdims=True))


def attend_kernel(heads, kv_heads, z_ref, cos_ref, sin_ref, qkv_ref, ctx_ref):
    seq_len = z_ref.shape[0]
    group = heads // kv_heads
    cos_t, sin_t = cos_ref[...], sin_ref[...]

    def cols(i):
        return pl.ds(pl.multiple_of(i * HEAD_DIM, HEAD_DIM), HEAD_DIM)

    for g in range(kv_heads):
        kc, vc = cols(heads + g), cols(heads + kv_heads + g)
        zk = z_ref[:, kc]
        qkv_ref[:, kc] = (zk * cos_t + swap_pairs(zk) * sin_t).astype(BF16)
        qkv_ref[:, vc] = z_ref[:, vc].astype(BF16)

        @pl.loop(0, group)
        def _(h):
            hc = cols(g * group + h)
            zq = z_ref[:, hc]
            q = (zq * cos_t + swap_pairs(zq) * sin_t).astype(BF16)
            qkv_ref[:, hc] = q
            for r in range(0, seq_len, Q_BLOCK):
                n = r + Q_BLOCK
                p = causal_probs(q[r:n], qkv_ref[:n, kc], r).astype(BF16)
                ctx_ref[r:n, hc] = mm(p, qkv_ref[:n, vc], NN_DIMS).astype(BF16)


def attend_back_kernel(heads, kv_heads, qkv_ref, dctx_ref, cos_ref, sin_ref, dz_ref, sum_ref, dk_ref, dv_ref):
    seq_len = qkv_ref.shape[0]
    group = heads // kv_heads
    cos_t, sin_t = cos_ref[...], sin_ref[...]

    def cols(i):
        return pl.ds(pl.multiple_of(i * HEAD_DIM, HEAD_DIM), HEAD_DIM)

    @pl.when(pl.program_id(0) == 0)
    def _():
        sum_ref[...] = jnp.zeros_like(sum_ref)

    def put(c, d):
        dz_ref[:, c] = d.astype(BF16)
        sum_ref[:, c] += jnp.sum(d, axis=0, keepdims=True)

    for g in range(kv_heads):
        kc, vc = cols(heads + g), cols(heads + kv_heads + g)
        dk_ref[...] = jnp.zeros_like(dk_ref)
        dv_ref[...] = jnp.zeros_like(dv_ref)

        @pl.loop(0, group)
        def _(h):
            hc = cols(g * group + h)
            dq = []
            for r in range(0, seq_len, Q_BLOCK):
                n = r + Q_BLOCK
                q, k, v, d = qkv_ref[r:n, hc], qkv_ref[:n, kc], qkv_ref[:n, vc], dctx_ref[r:n, hc]
                p = causal_probs(q, k, r)
                dp = mm(d, v, NT_DIMS)
                dv_ref[:n] += mm(p.astype(BF16), d, TN_DIMS)
                ds = (p * (dp - jnp.sum(p * dp, axis=1, keepdims=True)) * SCALE).astype(BF16)
                dq.append(mm(ds, k, NN_DIMS))
                dk_ref[:n] += mm(ds, q, TN_DIMS)
            dq = jnp.concatenate(dq, axis=0)
            put(hc, dq * cos_t - swap_pairs(dq) * sin_t)

        dk = dk_ref[...]
        put(kc, dk * cos_t - swap_pairs(dk) * sin_t)
        put(vc, dv_ref[...])


def attend(z, cos_t, sin_t, batch, heads, kv_heads):
    tokens, width = z.shape
    seq_len = tokens // batch
    row = lambda b: (b, 0)
    flops = 4 * tokens * seq_len * heads * HEAD_DIM
    return pl.pallas_call(
        functools.partial(attend_kernel, heads, kv_heads),
        grid=(batch,),
        in_specs=[pl.BlockSpec((seq_len, width), row), pl.BlockSpec((seq_len, HEAD_DIM), row), pl.BlockSpec((seq_len, HEAD_DIM), row)],
        out_specs=[pl.BlockSpec((seq_len, width), row), pl.BlockSpec((seq_len, heads * HEAD_DIM), row)],
        out_shape=[jax.ShapeDtypeStruct((tokens, width), BF16), jax.ShapeDtypeStruct((tokens, heads * HEAD_DIM), BF16)],
        compiler_params=pltpu.CompilerParams(dimension_semantics=("arbitrary",), vmem_limit_bytes=48 * 2 ** 20),
        cost_estimate=pl.CostEstimate(flops=3 * flops, bytes_accessed=tokens * width * 8, transcendentals=tokens * seq_len * heads),
        name="attend",
    )(z, cos_t, sin_t)


def attend_back(qkv, d_ctx, cos_t, sin_t, batch, heads, kv_heads):
    tokens, width = qkv.shape
    seq_len = tokens // batch
    row = lambda b: (b, 0)
    flops = 10 * tokens * seq_len * heads * HEAD_DIM
    return pl.pallas_call(
        functools.partial(attend_back_kernel, heads, kv_heads),
        grid=(batch,),
        in_specs=[pl.BlockSpec((seq_len, width), row), pl.BlockSpec((seq_len, heads * HEAD_DIM), row), pl.BlockSpec((seq_len, HEAD_DIM), row), pl.BlockSpec((seq_len, HEAD_DIM), row)],
        out_specs=[pl.BlockSpec((seq_len, width), row), pl.BlockSpec((1, width), lambda b: (0, 0))],
        out_shape=[jax.ShapeDtypeStruct((tokens, width), BF16), jax.ShapeDtypeStruct((1, width), F32)],
        scratch_shapes=[pltpu.VMEM((seq_len, HEAD_DIM), F32), pltpu.VMEM((seq_len, HEAD_DIM), F32)],
        compiler_params=pltpu.CompilerParams(dimension_semantics=("arbitrary",), vmem_limit_bytes=48 * 2 ** 20),
        cost_estimate=pl.CostEstimate(flops=3 * flops, bytes_accessed=tokens * width * 8, transcendentals=tokens * seq_len * heads),
        name="attend_back",
    )(qkv, d_ctx, cos_t, sin_t)


def solution(mesh):
    ax = mesh.axis_names[0]
    n_dev = mesh.shape[ax]
    group = n_dev // 2

    def hop(v, k):
        return lax.ppermute(v, ax, [(i, i ^ k) for i in range(n_dev)])

    def gather_rows(shard):
        return lax.all_gather(shard, ax, axis=0, tiled=True)

    def scatter_rows(full):
        return lax.psum_scatter(full, ax, scatter_dimension=0, tiled=True)

    def spread(v):
        rows, cols = v.shape
        out = jnp.zeros((group * rows, cols), v.dtype)
        parts = [v, hop(v, 1), hop(v, 2)]
        parts.append(hop(parts[2], 1))
        for k in range(group):
            out = lax.dynamic_update_slice(out, parts[k], (k * rows, 0))
        return out

    def layer(hidden, positions, grad_y, attn_gain, w_qkv, b_qkv, w_out, mlp_gain, w_up, w_down):
        batch, seq_len, width = hidden.shape
        tokens = batch * seq_len
        h_loc = w_up.shape[0]
        h_chip = 2 * h_loc
        f_loc = w_down.shape[0]
        pad = -(2 * f_loc) % 256
        f_pad = 2 * f_loc + pad
        q_loc = b_qkv.shape[0]
        me = lax.axis_index(ax)
        rank = lax.rem(me, group)
        side = lax.div(me, group)
        core = lax.rem(me, 2)
        chip = lax.div(me, 2)

        wqkv = gather_rows(w_qkv)
        wout = gather_rows(w_out)
        small = gather_rows(jnp.concatenate([attn_gain, b_qkv, mlp_gain])[None])
        small, w_up, w_down, grad_y = lax.optimization_barrier((small, w_up, w_down, grad_y))
        gain_one = small[:, :h_loc].reshape(1, width).astype(F32)
        bias = small[:, h_loc:h_loc + q_loc].reshape(1, n_dev * q_loc).astype(F32)
        gain_two = small[:, h_loc + q_loc:].reshape(1, width).astype(F32)

        blank = jnp.zeros((h_loc, pad), BF16)
        up_blocks = [w_up[:, j * f_loc:(j + 1) * f_loc] for j in range(2 * n_dev)]
        up_for = jnp.stack([jnp.concatenate([up_blocks[q], up_blocks[group + q], blank, up_blocks[n_dev + q], up_blocks[n_dev + group + q], blank], axis=1) for q in range(group)])
        up_part = [lax.dynamic_index_in_dim(up_for, rank ^ k, 0, keepdims=False) for k in range(group)]
        up_near = [up_part[0]] + [hop(up_part[k], k) for k in (1, 2, 3)]
        up_far = [hop(v, group) for v in up_near]
        w_all = jnp.zeros((width, 2 * f_pad), BF16)
        for k in range(group):
            w_all = lax.dynamic_update_slice(w_all, up_near[k], ((me ^ k) * h_loc, 0))
            w_all = lax.dynamic_update_slice(w_all, up_far[k], ((me ^ group ^ k) * h_loc, 0))
        down_far = hop(w_down, group)
        first = side == 0
        wd_all = jnp.concatenate([jnp.where(first, w_down, down_far), jnp.where(first, down_far, w_down), jnp.zeros((pad, width), BF16)], axis=0)
        dy = grad_y.reshape(tokens, width)
        dy_all = spread(dy)

        hid_wide = hidden.astype(F32).reshape(tokens, width)
        inv_one = norm_scale(hid_wide)
        normed = (hid_wide * inv_one * gain_one).astype(BF16)
        q_width = wout.shape[0]
        kv_width = (wqkv.shape[1] - q_width) // 2
        kv_heads = kv_width // HEAD_DIM
        heads = q_width // HEAD_DIM
        cos_t, sin_t = rope_tables(positions)
        z = mm(normed, wqkv, NN_DIMS) + bias
        qkv, context = attend(z, cos_t, sin_t, batch, heads, kv_heads)
        mid = (hid_wide + mm(context, wout, NN_DIMS)).astype(BF16)
        mid_wide = mid.astype(F32)
        inv_two = norm_scale(mid_wide)
        mlp_in = (mid_wide * inv_two * gain_two).astype(BF16)
        m_all = spread(mlp_in)

        gate_low = mm(m_all, w_all[:, :f_pad], NN_DIMS).astype(BF16)
        lin_low = mm(m_all, w_all[:, f_pad:], NN_DIMS).astype(BF16)
        gate = gate_low.astype(F32)
        act = (gate * jax.nn.sigmoid(gate) * lin_low.astype(F32)).astype(BF16)
        gate_low, lin_low, act = after(gate_low, lin_low, act)

        def block(rows, k, w, dims):
            return mm(rows[k * tokens:(k + 1) * tokens], w, dims)

        half = width // 2

        def down_grad(a, j):
            return mm(a, dy_all[:, j * half:(j + 1) * half], TN_DIMS)

        def send_down(g_full):
            return hop(lax.dynamic_slice(g_full, ((1 - side) * f_loc, 0), (f_loc, half)), group)

        def up_grad(m, d_up, chip_id):
            cols = lax.dynamic_slice(m, (0, chip_id * h_chip), (group * tokens, h_chip))
            return mm(cols, d_up, TN_DIMS)

        y3 = block(act, 3, wd_all, NN_DIMS)
        act, y3 = after(act, y3)
        y3 = hop(y3, 1)
        dwd0 = down_grad(act, 0)
        act, dwd0 = after(act, dwd0)
        dwd0_far = send_down(dwd0)
        y2 = block(act, 2, wd_all, NN_DIMS) + y3
        act, y2 = after(act, y2)
        y2 = hop(y2, 2)
        dwd1 = down_grad(act, 1)
        dwd1, act, gate_low, lin_low = after(dwd1, act, gate_low, lin_low)
        dwd1_far = send_down(dwd1)

        gate, lin = gate_low.astype(F32), lin_low.astype(F32)
        sig = jax.nn.sigmoid(gate)
        d_act = mm(dy_all, wd_all, NT_DIMS)
        d_gate = (d_act * lin * sig * (1.0 + gate * (1.0 - sig))).astype(BF16)
        d_lin = (d_act * gate * sig).astype(BF16)
        d_up = jnp.concatenate([d_gate, d_lin], axis=1)
        dm3 = block(d_up, 3, w_all, NT_DIMS)
        d_gate, d_lin, dm3 = after(d_gate, d_lin, dm3)
        dm3 = hop(dm3, 1)
        d_up = jnp.concatenate([d_gate, d_lin], axis=1)
        dm1 = block(d_up, 1, w_all, NT_DIMS)
        d_gate, d_lin, dm1 = after(d_gate, d_lin, dm1)
        dm1 = hop(dm1, 1)
        d_up = jnp.concatenate([d_gate, d_lin], axis=1)
        dm2 = block(d_up, 2, w_all, NT_DIMS) + dm3
        d_gate, d_lin, dm2 = after(d_gate, d_lin, dm2)
        dm2 = hop(dm2, 2)

        d_up = jnp.concatenate([d_gate, d_lin], axis=1)
        far_a = up_grad(m_all, d_up, chip ^ 3)
        d_gate, d_lin, far_a = after(d_gate, d_lin, far_a)
        far_a = hop(far_a, group)
        d_up = jnp.concatenate([d_gate, d_lin], axis=1)
        far_b = up_grad(m_all, d_up, chip ^ 2)
        d_gate, d_lin, act, far_b = after(d_gate, d_lin, act, far_b)
        far_b = hop(far_b, group)
        y1 = block(act, 1, wd_all, NN_DIMS)
        act, d_gate, d_lin, y1 = after(act, d_gate, d_lin, y1)
        y1 = hop(y1, 1)
        d_up = jnp.concatenate([d_gate, d_lin], axis=1)
        dm0 = block(d_up, 0, w_all, NT_DIMS)
        d_gate, d_lin, dm0, act = after(d_gate, d_lin, dm0, act)
        y0 = block(act, 0, wd_all, NN_DIMS)
        d_gate, d_lin, y0 = after(d_gate, d_lin, y0)
        d_up = jnp.concatenate([d_gate, d_lin], axis=1)
        near_a = up_grad(m_all, d_up, chip ^ 1)
        d_gate, d_lin, near_a = after(d_gate, d_lin, near_a)
        d_up = jnp.concatenate([d_gate, d_lin], axis=1)
        near_b = up_grad(m_all, d_up, chip)
        near_b, dm2 = after(near_b, dm2)

        grad_w_down = jnp.concatenate([lax.dynamic_slice(g, (side * f_loc, 0), (f_loc, half)) + far for g, far in ((dwd0, dwd0_far), (dwd1, dwd1_far))], axis=1)

        def rows_of(c, *parts):
            return sum(lax.dynamic_slice(v, (c * h_loc, 0), (h_loc, 2 * f_pad)) for v in parts)

        pieces = [
            rows_of(core, near_b, far_b),
            hop(rows_of(1 - core, near_b, far_b), 1),
            hop(rows_of(core, near_a, far_a), 2),
            hop(rows_of(1 - core, near_a, far_a), 3),
        ]
        stacked = jnp.stack(pieces)
        by_rank = [lax.dynamic_index_in_dim(stacked, rank ^ q, 0, keepdims=False) for q in range(group)]
        cols = [v[:, lo:lo + f_loc] for lo in (0, f_loc, f_pad, f_pad + f_loc) for v in by_rank]
        grad_w_up = jnp.concatenate(cols, axis=1)

        d_m = dm0 + dm1 + dm2
        grad_mlp_gain = jnp.sum(d_m * mid_wide * inv_two, axis=0)
        scaled_two = d_m * gain_two
        d_mid = dy.astype(F32) + inv_two * (scaled_two - mid_wide * inv_two * inv_two * jnp.mean(scaled_two * mid_wide, axis=-1, keepdims=True))
        d_mid_low = d_mid.astype(BF16)
        grad_w_out = scatter_rows(mm(context, d_mid_low, TN_DIMS))
        d_context = mm(d_mid_low, wout, NT_DIMS).astype(BF16)
        d_proj, grad_b_qkv = attend_back(qkv, d_context, cos_t, sin_t, batch, heads, kv_heads)
        grad_w_qkv = scatter_rows(mm(normed, d_proj, TN_DIMS))
        d_normed = mm(d_proj, wqkv, NT_DIMS)
        y0, y1, y2, mid_late, d_normed = after(y0, y1, y2, mid, d_normed)
        output = (mid_late.astype(F32) + (y0 + y1 + y2)).astype(BF16)
        grad_attn_gain = jnp.sum(d_normed * hid_wide * inv_one, axis=0)
        scaled_one = d_normed * gain_one
        grad_hidden = (d_mid + inv_one * (scaled_one - hid_wide * inv_one * inv_one * jnp.mean(scaled_one * hid_wide, axis=-1, keepdims=True))).astype(BF16)
        small_grads = scatter_rows(jnp.concatenate([grad_attn_gain.reshape(n_dev, h_loc), grad_b_qkv.reshape(n_dev, q_loc), grad_mlp_gain.reshape(n_dev, h_loc)], axis=1)).reshape(-1)
        return (output.reshape(hidden.shape), grad_hidden.reshape(hidden.shape), small_grads[:h_loc], grad_w_qkv, small_grads[h_loc:h_loc + q_loc], grad_w_out, small_grads[h_loc + q_loc:], grad_w_up, grad_w_down)

    row_spec = P(ax)
    return jax.shard_map(layer, mesh=mesh, in_specs=(row_spec,) * 10, out_specs=(row_spec,) * 9, check_vma=False)
```

profile of v0, /device:TPU:0, one launch (start us, length us, event | category | flops | bytes accessed | tf_op | source)
XLA Modules:
  0.0 3183.4 jit_solution(2447170593055925720)
XLA Ops:
  9.7 26.1 all-reduce.2
  35.9 11.0 fusion.101
  105.0 22.6 convolution_add_fusion.z_ref
  127.6 62.5 %attend.1 = (bf16[1536,2560]{1,0:T(8,128)(2,1)}, bf16[1536,2048]{1,0:T(8,128)(2,1)}) custom-call(f32[1536,2560]{1,0:T(8,128)} %convolution_add_fusion.z_ref, f32[1536,128]{1,0:T(8,128)S(1)} %get-tuple-element.184.cos_ref, f32[1536,128]{1,0:T(8,128)S(1)} %get-tuple-element.183.sin_ref), custom_call_target="tpu_custom_call" | custom-call | flops 19327352832 | bytes 31457280 | tf_op jit(solution)/shard_map/attend/pallas_call | solution.py:135
  190.0 19.1 fusion.44
  230.8 185.8 %collective-permute-done.10 = bf16[256,5632]{1,0:T(8,128)(2,1)} collective-permute-done((bf16[256,5632]{1,0:T(8,128)(2,1)}, bf16[256,5632]{1,0:T(8,128)(2,1)}, u32[]{:S(2)}, u32[]{:S(2)}) %collective-permute-start.10) | collective-permute-done | bytes 2883616 | tf_op jit(solution)/shard_map/ppermute | solution.py:171
  416.6 59.4 %collective-permute-done.12 = bf16[256,5632]{1,0:T(8,128)(2,1)} collective-permute-done((bf16[256,5632]{1,0:T(8,128)(2,1)}, bf16[256,5632]{1,0:T(8,128)(2,1)}, u32[]{:S(2)}, u32[]{:S(2)}) %collective-permute-start.12) | collective-permute-done | bytes 2883616 | tf_op jit(solution)/shard_map/ppermute | solution.py:171
  485.6 9.2 broadcast_select_fusion.1
  503.6 47.4 %collective-permute-done.11 = bf16[256,5632]{1,0:T(8,128)(2,1)} collective-permute-done((bf16[256,5632]{1,0:T(8,128)(2,1)}, bf16[256,5632]{1,0:T(8,128)(2,1)}, u32[]{:S(2)}, u32[]{:S(2)}) %collective-permute-start.11) | collective-permute-done | bytes 2883616 | tf_op jit(solution)/shard_map/ppermute | solution.py:171
  558.1 53.5 %collective-permute-done.13 = bf16[256,5632]{1,0:T(8,128)(2,1)S(1)} collective-permute-done((bf16[256,5632]{1,0:T(8,128)(2,1)}, bf16[256,5632]{1,0:T(8,128)(2,1)S(1)}, u32[]{:S(2)}, u32[]{:S(2)}) %collective-permute-start.13) | collective-permute-done | bytes 2883616 | tf_op jit(solution)/shard_map/ppermute | solution.py:171
  613.4 12.5 dynamic_update_slice.52
  645.6 80.8 %convolution_convert_fusion.1 = bf16[6144,2816]{0,1:T(8,128)(2,1)} fusion(bf16[6144,2048]{1,0:T(8,128)(2,1)} %constant_dynamic-update-slice_fusion.8, bf16[2048,5632]{1,0:T(8,128)(2,1)} %constant_dynamic-update-slice_fusion), kind=kOutput, calls=%fused_computation.35 | convolution fusion | flops 70884261888 | bytes 71303168 | tf_op jit(solution)/shard_map/dot_general | solution.py:27
  726.5 96.5 %fusion.28 = (bf16[6144,2816]{0,1:T(8,128)(2,1)}, bf16[6144,2816]{0,1:T(8,128)(2,1)}) fusion(bf16[6144,2816]{0,1:T(8,128)(2,1)} %convolution_convert_fusion.1, bf16[6144,2048]{1,0:T(8,128)(2,1)} %constant_dynamic-update-slice_fusion.8, bf16[2048,5632]{1,0:T(8,128)(2,1)} %constant_dynamic-update-slice_fusion), kind=kOutput, calls=%fused_computation.33 | convolution fusion | flops 71022673920 | bytes 140509184 | tf_op jit(solution)/shard_map/dot_general | solution.py:27
  823.0 25.4 fusion.72
  848.9 18.6 dynamic_update_slice.48
  887.2 44.9 %fusion.50 = f32[2816,1024]{1,0:T(8,128)} fusion(bf16[6144,2816]{0,1:T(8,128)(2,1)} %get-tuple-element.99, bf16[6144,2048]{1,0:T(8,128)(2,1)} %constant_dynamic-update-slice_fusion.11), kind=kOutput, calls=%fused_computation.67 | convolution fusion | flops 35433480192 | bytes 58720256 | tf_op jit(solution)/shard_map/dot_general | solution.py:27
  932.1 26.5 convolution_add_fusion.1
  958.5 45.0 %fusion.48 = f32[2816,1024]{1,0:T(8,128)} fusion(bf16[6144,2816]{0,1:T(8,128)(2,1)} %get-tuple-element.99, bf16[6144,2048]{1,0:T(8,128)(2,1)} %constant_dynamic-update-slice_fusion.11), kind=kOutput, calls=%fused_computation.65 | convolution fusion | flops 35433480192 | bytes 58720256 | tf_op jit(solution)/shard_map/dot_general | solution.py:27
  1003.5 152.0 %fusion.11 = (bf16[6144,2816]{0,1:T(8,128)(2,1)}, bf16[6144,2816]{0,1:T(8,128)(2,1)}) fusion(bf16[6144,2816]{0,1:T(8,128)(2,1)} %convolution_convert_fusion.1, bf16[6144,2816]{0,1:T(8,128)(2,1)} %get-tuple-element.79, bf16[6144,2048]{1,0:T(8,128)(2,1)} %constant_dynamic-update-slice_fusion.11, bf16[1376,2048]{1,0:T(8,128)(2,1)} %get-tuple-element.146, ...), kind=kOutput, calls=%fused_computation.16 | convolution fusion | flops 71161085952 | bytes 174855680 | tf_op jit(solution)/shard_map/dot_general | solution.py:27
  1155.5 46.9 %fusion.35 = f32[1536,2048]{1,0:T(8,128)} fusion(bf16[2048,5632]{1,0:T(8,128)(2,1)} %constant_dynamic-update-slice_fusion, bf16[6144,2816]{0,1:T(8,128)(2,1)} %get-tuple-element.109, bf16[6144,2816]{0,1:T(8,128)(2,1)} %get-tuple-element.108), kind=kOutput, calls=%fused_computation.51 | convolution fusion | flops 35468083200 | bytes 104857600 | tf_op jit(solution)/shard_map/dot_general | solution.py:27
  1202.5 58.2 %fusion.33 = f32[1536,2048]{1,0:T(8,128)} fusion(bf16[2048,5632]{1,0:T(8,128)(2,1)} %constant_dynamic-update-slice_fusion, bf16[6144,2816]{0,1:T(8,128)(2,1)} %get-tuple-element.109, bf16[6144,2816]{0,1:T(8,128)(2,1)} %get-tuple-element.108), kind=kOutput, calls=%fused_computation.48 | convolution fusion | flops 35468083200 | bytes 104857600 | tf_op jit(solution)/shard_map/dot_general | solution.py:27
  1261.2 64.1 %fusion.74 = f32[1536,2048]{1,0:T(8,128)} fusion(f32[1536,2048]{1,0:T(8,128)} %collective-permute-done.15, bf16[2048,5632]{1,0:T(8,128)(2,1)} %constant_dynamic-update-slice_fusion, bf16[6144,2816]{0,1:T(8,128)(2,1)} %get-tuple-element.109, bf16[6144,2816]{0,1:T(8,128)(2,1)} %get-tuple-element.108), kind=kOutput, calls=%fused_computation.102 | convolution fusion | flops 35471228928 | bytes 117440512 | tf_op jit(solution)/shard_map/dot_general | solution.py:27
  1325.2 46.6 %fusion.12 = f32[512,5632]{1,0:T(8,128)} fusion(bf16[6144,2816]{0,1:T(8,128)(2,1)} %get-tuple-element.109, bf16[6144,2816]{0,1:T(8,128)(2,1)} %get-tuple-element.108, bf16[6144,2048]{1,0:T(8,128)(2,1)} %constant_dynamic-update-slice_fusion.8, s32[]{:T(128)S(6)} %select_n.131), kind=kOutput, calls=%fused_computation.17 | convolution fusion | flops 35571892224 | bytes 87031808 | tf_op jit(solution)/shard_map/dot_general | solution.py:27
  1371.9 46.1 %fusion.16 = f32[512,5632]{1,0:T(8,128)} fusion(bf16[6144,2816]{0,1:T(8,128)(2,1)} %get-tuple-element.109, bf16[6144,2816]{0,1:T(8,128)(2,1)} %get-tuple-element.108, bf16[6144,2048]{1,0:T(8,128)(2,1)} %constant_dynamic-update-slice_fusion.8, s32[]{:T(128)S(6)} %select_n.132), kind=kOutput, calls=%fused_computation.21 | convolution fusion | flops 35571892224 | bytes 87031808 | tf_op jit(solution)/shard_map/dot_general | solution.py:27
  1418.0 24.9 fusion.69
  1442.9 53.2 %fusion.29 = f32[1536,2048]{1,0:T(8,128)} fusion(bf16[2048,5632]{1,0:T(8,128)(2,1)} %constant_dynamic-update-slice_fusion, bf16[6144,2816]{0,1:T(8,128)(2,1)} %get-tuple-element.109, bf16[6144,2816]{0,1:T(8,128)(2,1)} %get-tuple-element.108), kind=kOutput, calls=%fused_computation.42 | convolution fusion | flops 35468083200 | bytes 104857600 | tf_op jit(solution)/shard_map/dot_general | solution.py:27
  1496.5 24.6 fusion.67
  1521.1 46.3 %fusion.20 = f32[512,5632]{1,0:T(8,128)} fusion(bf16[6144,2816]{0,1:T(8,128)(2,1)} %get-tuple-element.109, bf16[6144,2816]{0,1:T(8,128)(2,1)} %get-tuple-element.108, bf16[6144,2048]{1,0:T(8,128)(2,1)} %constant_dynamic-update-slice_fusion.8, s32[]{:T(128)S(6)} %select_n.134), kind=kOutput, calls=%fused_computation.25 | convolution fusion | flops 35571892224 | bytes 87031808 | tf_op jit(solution)/shard_map/dot_general | solution.py:27
  1567.4 46.1 %fusion.24 = f32[512,5632]{1,0:T(8,128)} fusion(bf16[6144,2816]{0,1:T(8,128)(2,1)} %get-tuple-element.109, bf16[6144,2816]{0,1:T(8,128)(2,1)} %get-tuple-element.108, bf16[6144,2048]{1,0:T(8,128)(2,1)} %constant_dynamic-update-slice_fusion.8, s32[]{:T(128)S(6)} %select_n.133), kind=kOutput, calls=%fused_computation.29 | convolution fusion | flops 35571892224 | bytes 87031808 | tf_op jit(solution)/shard_map/dot_general | solution.py:27
  1613.5 155.2 %collective-permute-done.19 = f32[1536,2048]{1,0:T(8,128)} collective-permute-done((f32[1536,2048]{1,0:T(8,128)}, f32[1536,2048]{1,0:T(8,128)}, u32[]{:S(2)}, u32[]{:S(2)}) %collective-permute-start.19) | collective-permute-done | bytes 12582944 | tf_op jit(solution)/shard_map/ppermute | solution.py:171
  1768.8 19.4 fusion.47
  1788.2 13.4 fusion.43
  1801.6 22.0 fusion.79
  1823.6 20.8 convolution_convert_fusion.2.dctx_ref
  1844.4 80.1 %attend_back.1 = (bf16[1536,2560]{1,0:T(8,128)(2,1)}, f32[1,2560]{1,0:T(1,128)S(1)}) custom-call(bf16[1536,2560]{1,0:T(8,128)(2,1)} %get-tuple-element.103.qkv_ref, bf16[1536,2048]{1,0:T(8,128)(2,1)} %convolution_convert_fusion.2.dctx_ref, f32[1536,128]{1,0:T(8,128)S(1)} %get-tuple-element.184.cos_ref, f32[1536,128]{1,0:T(8,128)S(1)} %get-tuple-element.183.sin_ref), custom_call_target="tpu_custom_call" | custom-call | flops 48318382080 | bytes 31457280 | tf_op jit(solution)/shard_map/attend_back/pallas_call | solution.py:152
  1924.5 22.1 fusion.108
  1962.1 196.5 %collective-permute-done.25 = f32[1376,1024]{1,0:T(8,128)} collective-permute-done((f32[1376,1024]{1,0:T(8,128)S(1)}, f32[1376,1024]{1,0:T(8,128)}, u32[]{:S(2)}, u32[]{:S(2)}) %collective-permute-start.25) | collective-permute-done | bytes 5636128 | tf_op jit(solution)/shard_map/ppermute | solution.py:171
  2167.3 604.4 %collective-permute-done.26 = f32[1376,1024]{1,0:T(8,128)} collective-permute-done((f32[1376,1024]{1,0:T(8,128)}, f32[1376,1024]{1,0:T(8,128)}, u32[]{:S(2)}, u32[]{:S(2)}) %collective-permute-start.26) | collective-permute-done | bytes 5636128 | tf_op jit(solution)/shard_map/ppermute | solution.py:171
  2780.3 10.5 pad_maximum_fusion.10
  2790.8 12.8 dynamic-slice_add_fusion.1
  2803.7 13.0 add_bitcast_fusion
  2818.7 20.0 fusion.107
  2843.6 225.1 %all-reduce.3 = f32[8,832]{1,0:T(8,128)S(1)} all-reduce(f32[8,832]{1,0:T(8,128)S(1)} %pad_maximum_fusion.13), channel_id=3, replica_groups=mesh['fsdp'=8] {'fsdp'}, use_global_device_ids=true, to_apply=%region_6.7.clone | all-reduce | flops 6656 | bytes 53248
  3070.0 14.4 fusion.59
  3084.3 18.4 add_convert_fusion
  3102.8 15.3 pad_maximum_fusion
  3118.0 14.4 dynamic-slice_bitcast_fusion
  3147.6 28.7 concatenate.66
  (200 shorter events, 206.6 us)
Async XLA Ops:
  7.2 97.8 %all-gather.4.cloned.1.call-start = ((), (), s32[]{:S(2)}) async-start(), calls=%async_computation.2 | async-start | bytes 11796480 | tf_op jit(solution)/shard_map/all_gather | solution.py:174
  7.9 182.1 %all-gather.6.cloned.1.call-start = ((), (), s32[]{:S(2)}) async-start(), calls=%async_computation.3 | async-start | bytes 9437184 | tf_op jit(solution)/shard_map/all_gather | solution.py:174
  8.7 3167.6 %reduce-scatter.5.cloned.1.call-start = ((), (), s32[]{:S(2)}) async-start(), calls=%async_computation.5 | async-start | bytes 18874368 | tf_op jit(solution)/shard_map/reduce_scatter | solution.py:177
  90.7 134.5 %collective-permute-start.7 = (bf16[256,5632]{1,0:T(8,128)(2,1)}, bf16[256,5632]{1,0:T(8,128)(2,1)}, u32[]{:S(2)}, u32[]{:S(2)}) collective-permute-start(bf16[256,5632]{1,0:T(8,128)(2,1)} %get-tuple-element.131), channel_id=1, source_target_pairs={{0,4},{1,5},{2,6},{3,7},{4,0},{5,1},{6,2},{7,3}} | collective-permute-start | bytes 8650760 | tf_op jit(solution)/shard_map/ppermute | solution.py:171
  93.6 34.0 %copy-start.5 = (f32[1,2,8,128]{3,1,2,0:T(2,128)}, f32[1,2,8,128]{3,1,2,0:T(2,128)S(1)}, u32[]{:S(2)}) copy-start(f32[1,2,8,128]{3,1,2,0:T(2,128)S(1)} %copy.25) | copy-start | bytes 24580
  94.9 32.6 %copy-start.7 = (f32[1536]{0:T(1024)}, f32[1536]{0:T(1024)S(1)}, u32[]{:S(2)}) copy-start(f32[1536]{0:T(1024)S(1)} %rsqrt.20) | copy-start | bytes 18436
  95.0 114.2 %copy-start.9 = (f32[1,2,8,128]{3,1,2,0:T(2,128)}, f32[1,2,8,128]{3,1,2,0:T(2,128)S(1)}, u32[]{:S(2)}) copy-start(f32[1,2,8,128]{3,1,2,0:T(2,128)S(1)} %copy.26) | copy-start | bytes 24580
  216.0 269.6 %collective-permute-start.5 = (bf16[1536,2048]{1,0:T(8,128)(2,1)}, bf16[1536,2048]{1,0:T(8,128)(2,1)}, u32[]{:S(2)}, u32[]{:S(2)}) collective-permute-start(bf16[1536,2048]{1,0:T(8,128)(2,1)} %fusion.39), channel_id=1, source_target_pairs={{0,2},{1,3},{2,0},{3,1},{4,6},{5,7},{6,4},{7,5}} | collective-permute-start | bytes 18874376 | tf_op jit(solution)/shard_map/ppermute | solution.py:171
  216.2 269.1 %collective-permute-start.3 = (bf16[1376,2048]{1,0:T(8,128)(2,1)}, bf16[1376,2048]{1,0:T(8,128)(2,1)}, u32[]{:S(2)}, u32[]{:S(2)}) collective-permute-start(bf16[1376,2048]{1,0:T(8,128)(2,1)} %param.19), channel_id=1, source_target_pairs={{0,4},{1,5},{2,6},{3,7},{4,0},{5,1},{6,2},{7,3}} | collective-permute-start | bytes 16908296 | tf_op jit(solution)/shard_map/ppermute | solution.py:171
  225.1 5.6 collective-permute-start.8
  225.1 191.4 %collective-permute-start.10 = (bf16[256,5632]{1,0:T(8,128)(2,1)}, bf16[256,5632]{1,0:T(8,128)(2,1)}, u32[]{:S(2)}, u32[]{:S(2)}) collective-permute-start(bf16[256,5632]{1,0:T(8,128)(2,1)} %get-tuple-element.143), channel_id=1, source_target_pairs={{0,2},{1,3},{2,0},{3,1},{4,6},{5,7},{6,4},{7,5}} | collective-permute-start | bytes 8650760 | tf_op jit(solution)/shard_map/ppermute | solution.py:171
  225.2 250.8 %collective-permute-start.12 = (bf16[256,5632]{1,0:T(8,128)(2,1)}, bf16[256,5632]{1,0:T(8,128)(2,1)}, u32[]{:S(2)}, u32[]{:S(2)}) collective-permute-start(bf16[256,5632]{1,0:T(8,128)(2,1)} %get-tuple-element.142), channel_id=1, source_target_pairs={{0,3},{1,2},{2,1},{3,0},{4,7},{5,6},{6,5},{7,4}} | collective-permute-start | bytes 8650760 | tf_op jit(solution)/shard_map/ppermute | solution.py:171
  230.8 382.6 %collective-permute-start.1 = (bf16[1536,2048]{1,0:T(8,128)(2,1)}, bf16[1536,2048]{1,0:T(8,128)(2,1)}, u32[]{:S(2)}, u32[]{:S(2)}) collective-permute-start(bf16[1536,2048]{1,0:T(8,128)(2,1)} %bitcast.99), channel_id=1, source_target_pairs={{0,2},{1,3},{2,0},{3,1},{4,6},{5,7},{6,4},{7,5}} | collective-permute-start | bytes 18874376 | tf_op jit(solution)/shard_map/ppermute | solution.py:171
  416.5 78.3 %collective-permute-start.9 = (bf16[256,5632]{1,0:T(8,128)(2,1)}, bf16[256,5632]{1,0:T(8,128)(2,1)}, u32[]{:S(2)}, u32[]{:S(2)}) collective-permute-start(bf16[256,5632]{1,0:T(8,128)(2,1)} %collective-permute-done.8), channel_id=1, source_target_pairs={{0,4},{1,5},{2,6},{3,7},{4,0},{5,1},{6,2},{7,3}} | collective-permute-start | bytes 8650760 | tf_op jit(solution)/shard_map/ppermute | solution.py:171
  476.0 149.9 %collective-permute-start.4 = (bf16[1536,2048]{1,0:T(8,128)(2,1)}, bf16[1536,2048]{1,0:T(8,128)(2,1)}, u32[]{:S(2)}, u32[]{:S(2)}) collective-permute-start(bf16[1536,2048]{1,0:T(8,128)(2,1)} %fusion.39), channel_id=1, source_target_pairs={{0,1},{1,0},{2,3},{3,2},{4,5},{5,4},{6,7},{7,6}} | collective-permute-start | bytes 18874376 | tf_op jit(solution)/shard_map/ppermute | solution.py:171
  485.3 65.7 %collective-permute-start.11 = (bf16[256,5632]{1,0:T(8,128)(2,1)}, bf16[256,5632]{1,0:T(8,128)(2,1)}, u32[]{:S(2)}, u32[]{:S(2)}) collective-permute-start(bf16[256,5632]{1,0:T(8,128)(2,1)} %collective-permute-done.10), channel_id=1, source_target_pairs={{0,4},{1,5},{2,6},{3,7},{4,0},{5,1},{6,2},{7,3}} | collective-permute-start | bytes 8650760 | tf_op jit(solution)/shard_map/ppermute | solution.py:171
  485.6 153.4 %collective-permute-start.6 = (bf16[1536,2048]{1,0:T(8,128)(2,1)}, bf16[1536,2048]{1,0:T(8,128)(2,1)}, u32[]{:S(2)}, u32[]{:S(2)}) collective-permute-start(bf16[1536,2048]{1,0:T(8,128)(2,1)} %collective-permute-done.5), channel_id=1, source_target_pairs={{0,1},{1,0},{2,3},{3,2},{4,5},{5,4},{6,7},{7,6}} | collective-permute-start | bytes 18874376 | tf_op jit(solution)/shard_map/ppermute | solution.py:171
  494.8 116.9 %collective-permute-start.13 = (bf16[256,5632]{1,0:T(8,128)(2,1)}, bf16[256,5632]{1,0:T(8,128)(2,1)S(1)}, u32[]{:S(2)}, u32[]{:S(2)}) collective-permute-start(bf16[256,5632]{1,0:T(8,128)(2,1)} %collective-permute-done.12), channel_id=1, source_target_pairs={{0,4},{1,5},{2,6},{3,7},{4,0},{5,1},{6,2},{7,3}} | collective-permute-start | bytes 8650760 | tf_op jit(solution)/shard_map/ppermute | solution.py:171
  551.0 316.5 %collective-permute-start = (bf16[1536,2048]{1,0:T(8,128)(2,1)}, bf16[1536,2048]{1,0:T(8,128)(2,1)}, u32[]{:S(2)}, u32[]{:S(2)}) collective-permute-start(bf16[1536,2048]{1,0:T(8,128)(2,1)} %bitcast.100), channel_id=1, source_target_pairs={{0,1},{1,0},{2,3},{3,2},{4,5},{5,4},{6,7},{7,6}} | collective-permute-start | bytes 18874376 | tf_op jit(solution)/shard_map/ppermute | solution.py:171
  613.4 267.1 %collective-permute-start.2 = (bf16[1536,2048]{1,0:T(8,128)(2,1)}, bf16[1536,2048]{1,0:T(8,128)(2,1)}, u32[]{:S(2)}, u32[]{:S(2)}) collective-permute-start(bf16[1536,2048]{1,0:T(8,128)(2,1)} %collective-permute-done.1), channel_id=1, source_target_pairs={{0,1},{1,0},{2,3},{3,2},{4,5},{5,4},{6,7},{7,6}} | collective-permute-start | bytes 18874376 | tf_op jit(solution)/shard_map/ppermute | solution.py:171
  726.5 96.5 %copy-start.15 = (bf16[2816]{0:T(1024)(128)(2,1)S(1)}, bf16[2816]{0:T(1024)(128)(2,1)}, u32[]{:S(2)}) copy-start(bf16[2816]{0:T(1024)(128)(2,1)} %pad.33.clone) | copy-start | bytes 16900
  823.0 25.9 copy-start.3
  848.4 83.7 %collective-permute-start.14 = (f32[1536,2048]{1,0:T(8,128)}, f32[1536,2048]{1,0:T(8,128)}, u32[]{:S(2)}, u32[]{:S(2)}) collective-permute-start(f32[1536,2048]{1,0:T(8,128)} %fusion.72), channel_id=1, source_target_pairs={{0,1},{1,0},{2,3},{3,2},{4,5},{5,4},{6,7},{7,6}} | collective-permute-start | bytes 37748744 | tf_op jit(solution)/shard_map/ppermute | solution.py:171
  1202.4 58.7 %collective-permute-start.15 = (f32[1536,2048]{1,0:T(8,128)}, f32[1536,2048]{1,0:T(8,128)}, u32[]{:S(2)}, u32[]{:S(2)}) collective-permute-start(f32[1536,2048]{1,0:T(8,128)} %fusion.35), channel_id=1, source_target_pairs={{0,1},{1,0},{2,3},{3,2},{4,5},{5,4},{6,7},{7,6}} | collective-permute-start | bytes 37748744 | tf_op jit(solution)/shard_map/ppermute | solution.py:171
  1260.7 508.0 %collective-permute-start.18 = (f32[1536,2048]{1,0:T(8,128)}, f32[1536,2048]{1,0:T(8,128)}, u32[]{:S(2)}, u32[]{:S(2)}) collective-permute-start(f32[1536,2048]{1,0:T(8,128)} %fusion.33), channel_id=1, source_target_pairs={{0,1},{1,0},{2,3},{3,2},{4,5},{5,4},{6,7},{7,6}} | collective-permute-start | bytes 37748744 | tf_op jit(solution)/shard_map/ppermute | solution.py:171
  1325.2 92.7 %slice-start.12 = ((s8[5636096]{0:T(1024)(128)(4,1)}), s8[4194304]{0:T(1024)(128)(4,1)S(1)}, s32[]{:S(2)}) async-start(s8[5636096]{0:T(1024)(128)(4,1)} %bitcast.114), calls=%async_computation.18 | async-start | bytes 8388608
  1371.9 46.1 %slice-start.13 = ((s8[5636096]{0:T(1024)(128)(4,1)}), s8[1441792]{0:T(1024)(128)(4,1)S(1)}, s32[]{:S(2)}) async-start(s8[5636096]{0:T(1024)(128)(4,1)} %bitcast.114), calls=%async_computation.19 | async-start | bytes 2883584
  1371.9 46.1 %copy-start.16 = (bf16[2816]{0:T(1024)(128)(2,1)S(1)}, bf16[2816]{0:T(1024)(128)(2,1)}, u32[]{:S(2)}) copy-start(bf16[2816]{0:T(1024)(128)(2,1)} %pad.33.clone) | copy-start | bytes 16900
  1418.0 78.5 %slice-start.14 = ((s8[5636096]{0:T(1024)(128)(4,1)}), s8[4194304]{0:T(1024)(128)(4,1)S(1)}, s32[]{:S(2)}) async-start(s8[5636096]{0:T(1024)(128)(4,1)} %bitcast.116), calls=%async_computation.20 | async-start | bytes 8388608
  1442.9 53.6 %slice-start.15 = ((s8[5636096]{0:T(1024)(128)(4,1)}), s8[1441792]{0:T(1024)(128)(4,1)S(1)}, s32[]{:S(2)}) async-start(s8[5636096]{0:T(1024)(128)(4,1)} %bitcast.116), calls=%async_computation.21 | async-start | bytes 2883584
  1496.1 272.6 %collective-permute-start.19 = (f32[1536,2048]{1,0:T(8,128)}, f32[1536,2048]{1,0:T(8,128)}, u32[]{:S(2)}, u32[]{:S(2)}) collective-permute-start(f32[1536,2048]{1,0:T(8,128)} %fusion.74), channel_id=1, source_target_pairs={{0,2},{1,3},{2,0},{3,1},{4,6},{5,7},{6,4},{7,5}} | collective-permute-start | bytes 37748744 | tf_op jit(solution)/shard_map/ppermute | solution.py:171
  1521.1 247.7 %slice-start = ((s8[6291456]{0:T(1024)(128)(4,1)}), s8[4194304]{0:T(1024)(128)(4,1)S(1)}, s32[]{:S(2)}) async-start(s8[6291456]{0:T(1024)(128)(4,1)} %bitcast.93), calls=%async_computation.6 | async-start | bytes 8388608
  1567.4 201.3 %slice-start.1 = ((s8[6291456]{0:T(1024)(128)(4,1)}), s8[2097152]{0:T(1024)(128)(4,1)S(1)}, s32[]{:S(2)}) async-start(s8[6291456]{0:T(1024)(128)(4,1)} %bitcast.93), calls=%async_computation.7 | async-start | bytes 4194304
  1567.4 201.3 %copy-start.10 = (f32[1,2,8,128]{3,1,2,0:T(2,128)S(1)}, f32[1,2,8,128]{3,1,2,0:T(2,128)}, u32[]{:S(2)}) copy-start(f32[1,2,8,128]{3,1,2,0:T(2,128)} %copy-done.9) | copy-start | bytes 24580
  1567.4 201.3 %copy-start.12 = (f32[1536]{0:T(1024)S(1)}, f32[1536]{0:T(1024)}, u32[]{:S(2)}) copy-start(f32[1536]{0:T(1024)} %copy-done.11) | copy-start | bytes 18436
  1823.6 1352.8 %reduce-scatter.3.cloned.1.call-start = ((), (), s32[]{:S(2)}) async-start(), calls=%async_computation.4 | async-start | bytes 23592960 | tf_op jit(solution)/shard_map/reduce_scatter | solution.py:177
  1823.6 100.9 %slice-start.10 = ((s8[6291456]{0:T(1024)(128)(4,1)}), s8[2097152]{0:T(1024)(128)(4,1)S(1)}, s32[]{:S(2)}) async-start(s8[6291456]{0:T(1024)(128)(4,1)} %bitcast.112), calls=%async_computation.16 | async-start | bytes 4194304
  1844.4 80.1 %slice-start.11 = ((s8[6291456]{0:T(1024)(128)(4,1)}), s8[4194304]{0:T(1024)(128)(4,1)S(1)}, s32[]{:S(2)}) async-start(s8[6291456]{0:T(1024)(128)(4,1)} %bitcast.112), calls=%async_computation.17 | async-start | bytes 8388608
  1949.8 208.7 %collective-permute-start.25 = (f32[1376,1024]{1,0:T(8,128)S(1)}, f32[1376,1024]{1,0:T(8,128)}, u32[]{:S(2)}, u32[]{:S(2)}) collective-permute-start(f32[1376,1024]{1,0:T(8,128)S(1)} %constant_dynamic-slice_fusion.1), channel_id=1, source_target_pairs={{0,4},{1,5},{2,6},{3,7},{4,0},{5,1},{6,2},{7,3}} | collective-permute-start | bytes 16908296 | tf_op jit(solution)/shard_map/ppermute | solution.py:171
  1950.0 840.8 %collective-permute-start.22 = (f32[512,5632]{1,0:T(8,128)}, f32[512,5632]{1,0:T(8,128)}, u32[]{:S(2)}, u32[]{:S(2)}) collective-permute-start(f32[512,5632]{1,0:T(8,128)} %fusion.12), channel_id=1, source_target_pairs={{0,4},{1,5},{2,6},{3,7},{4,0},{5,1},{6,2},{7,3}} | collective-permute-start | bytes 34603016 | tf_op jit(solution)/shard_map/ppermute | solution.py:171
  1951.9 851.8 %collective-permute-start.20 = (f32[512,5632]{1,0:T(8,128)}, f32[512,5632]{1,0:T(8,128)}, u32[]{:S(2)}, u32[]{:S(2)}) collective-permute-start(f32[512,5632]{1,0:T(8,128)} %fusion.16), channel_id=1, source_target_pairs={{0,4},{1,5},{2,6},{3,7},{4,0},{5,1},{6,2},{7,3}} | collective-permute-start | bytes 34603016 | tf_op jit(solution)/shard_map/ppermute | solution.py:171
  1960.2 811.5 %collective-permute-start.26 = (f32[1376,1024]{1,0:T(8,128)}, f32[1376,1024]{1,0:T(8,128)}, u32[]{:S(2)}, u32[]{:S(2)}) collective-permute-start(f32[1376,1024]{1,0:T(8,128)} %constant_dynamic-slice_fusion), channel_id=1, source_target_pairs={{0,4},{1,5},{2,6},{3,7},{4,0},{5,1},{6,2},{7,3}} | collective-permute-start | bytes 16908296 | tf_op jit(solution)/shard_map/ppermute | solution.py:171
  1962.1 876.6 %collective-permute-start.17 = (f32[1536,2048]{1,0:T(8,128)}, f32[1536,2048]{1,0:T(8,128)}, u32[]{:S(2)}, u32[]{:S(2)}) collective-permute-start(f32[1536,2048]{1,0:T(8,128)} %convolution_add_fusion.1), channel_id=1, source_target_pairs={{0,2},{1,3},{2,0},{3,1},{4,6},{5,7},{6,4},{7,5}} | collective-permute-start | bytes 37748744 | tf_op jit(solution)/shard_map/ppermute | solution.py:171
  2158.6 680.2 %collective-permute-start.16 = (f32[1536,2048]{1,0:T(8,128)}, f32[1536,2048]{1,0:T(8,128)}, u32[]{:S(2)}, u32[]{:S(2)}) collective-permute-start(f32[1536,2048]{1,0:T(8,128)} %fusion.69), channel_id=1, source_target_pairs={{0,1},{1,0},{2,3},{3,2},{4,5},{5,4},{6,7},{7,6}} | collective-permute-start | bytes 37748744 | tf_op jit(solution)/shard_map/ppermute | solution.py:171
  2803.6 299.1 %collective-permute-start.23 = (f32[256,5632]{1,0:T(8,128)}, f32[256,5632]{1,0:T(8,128)}, u32[]{:S(2)}, u32[]{:S(2)}) collective-permute-start(f32[256,5632]{1,0:T(8,128)} %get-tuple-element.140), channel_id=1, source_target_pairs={{0,2},{1,3},{2,0},{3,1},{4,6},{5,7},{6,4},{7,5}} | collective-permute-start | bytes 17301512 | tf_op jit(solution)/shard_map/ppermute | solution.py:171
  2803.7 299.0 %collective-permute-start.24 = (f32[256,5632]{1,0:T(8,128)}, f32[256,5632]{1,0:T(8,128)}, u32[]{:S(2)}, u32[]{:S(2)}) collective-permute-start(f32[256,5632]{1,0:T(8,128)} %get-tuple-element.141), channel_id=1, source_target_pairs={{0,3},{1,2},{2,1},{3,0},{4,7},{5,6},{6,5},{7,4}} | collective-permute-start | bytes 17301512 | tf_op jit(solution)/shard_map/ppermute | solution.py:171
  2816.8 286.0 %collective-permute-start.21 = (f32[256,5632]{1,0:T(8,128)}, f32[256,5632]{1,0:T(8,128)}, u32[]{:S(2)}, u32[]{:S(2)}) collective-permute-start(f32[256,5632]{1,0:T(8,128)} %get-tuple-element.139), channel_id=1, source_target_pairs={{0,1},{1,0},{2,3},{3,2},{4,5},{5,4},{6,7},{7,6}} | collective-permute-start | bytes 17301512 | tf_op jit(solution)/shard_map/ppermute | solution.py:171
  3070.0 32.8 %slice-start.6 = ((s8[5767168]{0:T(1024)(128)(4,1)}), s8[4194304]{0:T(1024)(128)(4,1)S(1)}, s32[]{:S(2)}) async-start(s8[5767168]{0:T(1024)(128)(4,1)} %bitcast.102), calls=%async_computation.12 | async-start | bytes 8388608
  (18 other events, 244.4 us)
Sparse Core Ops, SparseCore 0:
  9.8 61.2 all-gather.3
  72.9 71.6 all-gather.5
  1823.7 107.9 reduce-scatter.4
  1946.8 212.4 reduce-scatter.2
where the time goes:
time: 3200 us; the launch traced here: 3180 us
  waiting for transfers between devices  1310 us (41%)
  matrix products  1050 us (33%)
  blocking collectives  251 us (8%)
  local copies, waits for them, and re-layouts  224 us (7%)
  other arithmetic  171 us (5%)
  Pallas kernels  143 us (4%)
    ppermute x27, waiting for transfers between devices, hop(): return lax.ppermute(v, ax, [(i, i ^ k) for i in range(n_dev)])  1310 us
    dot_general x23, matrix products, mm(): return lax.dot_general(a, b, dims, preferred_element_type=F32)  1050 us
    unnamed x2, blocking collectives  251 us
    pallas_call x1, Pallas kernels, attend_back(): pl.pallas_call(functools.partial(attend_back_kernel, heads, kv_heads), gr...  80.1 us
    dynamic_update_slice x8, local copies, waits for them, and re-layouts, spread(): out = lax.dynamic_update_slice(out, parts[k], (k * rows, 0))  70.5 us
  transfers between devices with their start and end apart: 31, of which 8 were waited for; matrix products, arithmetic and copies ran while one was open for 35% of the time, Pallas kernels for 4%

commit v1 on v0

--- a/solution.py
+++ b/solution.py
@@ -20,7 +20,11 @@
 BF16 = jnp.bfloat16
 SCALE = HEAD_DIM ** -0.5
 MASKED = -1e30
-Q_BLOCK = 256
+Q_BLOCK = 128
+T_BLOCK = 512
+F_BLOCK = 256
+LANES = 128
+LOG2_E = 1.4426950408889634
 
 
 def mm(a, b, dims):
@@ -50,12 +54,15 @@
     return jnp.where(lane % 2 == 0, pltpu.roll(v, HEAD_DIM - 1, 1), pltpu.roll(v, 1, 1))
 
 
-def causal_probs(q, k, row0):
-    s = mm(q, k, NT_DIMS) * SCALE
-    row = lax.broadcasted_iota(jnp.int32, s.shape, 0) + row0
-    col = lax.broadcasted_iota(jnp.int32, s.shape, 1)
-    s = jnp.where(row >= col, s, MASKED)
-    e = jnp.exp(s - jnp.max(s, axis=1, keepdims=True))
+def causal_probs(q, k):
+    n = q.shape[0]
+    full = k.shape[0] - n
+    s = mm(q, k, NT_DIMS)
+    row = lax.broadcasted_iota(jnp.int32, (n, n), 0)
+    col = lax.broadcasted_iota(jnp.int32, (n, n), 1)
+    own = jnp.where(row >= col, s[:, full:], MASKED)
+    s = own if full == 0 else jnp.concatenate([s[:, :full], own], axis=1)
+    e = jnp.exp2((s - jnp.max(s, axis=1, keepdims=True)) * (SCALE * LOG2_E))
     return e * (1.0 / jnp.sum(e, axis=1, keepdims=True))
 
 
@@ -81,7 +88,7 @@
             qkv_ref[:, hc] = q
             for r in range(0, seq_len, Q_BLOCK):
                 n = r + Q_BLOCK
-                p = causal_probs(q[r:n], qkv_ref[:n, kc], r).astype(BF16)
+                p = causal_probs(q[r:n], qkv_ref[:n, kc]).astype(BF16)
                 ctx_ref[r:n, hc] = mm(p, qkv_ref[:n, vc], NN_DIMS).astype(BF16)
 
 
@@ -113,7 +120,7 @@
             for r in range(0, seq_len, Q_BLOCK):
                 n = r + Q_BLOCK
                 q, k, v, d = qkv_ref[r:n, hc], qkv_ref[:n, kc], qkv_ref[:n, vc], dctx_ref[r:n, hc]
-                p = causal_probs(q, k, r)
+                p = causal_probs(q, k)
                 dp = mm(d, v, NT_DIMS)
                 dv_ref[:n] += mm(p.astype(BF16), d, TN_DIMS)
                 ds = (p * (dp - jnp.sum(p * dp, axis=1, keepdims=True)) * SCALE).astype(BF16)
@@ -162,6 +169,155 @@
     )(qkv, d_ctx, cos_t, sin_t)
 
 
+def up_kernel(m_ref, w_ref, g_ref, l_ref, a_ref):
+    f_pad = g_ref.shape[1]
+    for j in range(0, f_pad, F_BLOCK):
+        c = slice(j, j + F_BLOCK)
+        gate_low = mm(m_ref[...], w_ref[:, c], NN_DIMS).astype(BF16)
+        lin_low = mm(m_ref[...], w_ref[:, f_pad + j:f_pad + j + F_BLOCK], NN_DIMS).astype(BF16)
+        g_ref[:, c] = gate_low
+        l_ref[:, c] = lin_low
+        gate = gate_low.astype(F32)
+        a_ref[:, c] = (gate * (1.0 / (1.0 + jnp.exp(-gate))) * lin_low.astype(F32)).astype(BF16)
+
+
+def up_act(m, w):
+    tokens, width = m.shape
+    f_pad = w.shape[1] // 2
+    row = lambda i: (i, 0)
+    return pl.pallas_call(
+        up_kernel,
+        grid=(tokens // T_BLOCK,),
+        in_specs=[pl.BlockSpec((T_BLOCK, width), row), pl.BlockSpec(w.shape, lambda i: (0, 0), pipeline_mode=pl.Buffered(1))],
+        out_specs=[pl.BlockSpec((T_BLOCK, f_pad), row)] * 3,
+        out_shape=[jax.ShapeDtypeStruct((tokens, f_pad), BF16)] * 3,
+        compiler_params=pltpu.CompilerParams(dimension_semantics=("arbitrary",), vmem_limit_bytes=60 * 2 ** 20),
+        cost_estimate=pl.CostEstimate(flops=2 * tokens * width * 2 * f_pad, bytes_accessed=2 * (m.size + w.size + 3 * tokens * f_pad), transcendentals=2 * tokens * f_pad),
+        name="up_act",
+    )(m, w)
+
+
+def up_back_kernel(dy_ref, wd_ref, g_ref, l_ref, out_ref):
+    f_pad = g_ref.shape[1]
+    for j in range(0, f_pad, F_BLOCK):
+        c = slice(j, j + F_BLOCK)
+        d_act = mm(dy_ref[...], wd_ref[c, :], NT_DIMS)
+        gate, lin = g_ref[:, c].astype(F32), l_ref[:, c].astype(F32)
+        sig = 1.0 / (1.0 + jnp.exp(-gate))
+        gate_sig = gate * sig
+        out_ref[:, c] = (d_act * (lin * (sig + gate_sig * (1.0 - sig)))).astype(BF16)
+        out_ref[:, f_pad + j:f_pad + j + F_BLOCK] = (d_act * gate_sig).astype(BF16)
+
+
+def up_back(dy, wd, gate_low, lin_low):
+    tokens, width = dy.shape
+    f_pad = wd.shape[0]
+    row = lambda i: (i, 0)
+    return pl.pallas_call(
+        up_back_kernel,
+        grid=(tokens // T_BLOCK,),
+        in_specs=[pl.BlockSpec((T_BLOCK, width), row), pl.BlockSpec(wd.shape, lambda i: (0, 0), pipeline_mode=pl.Buffered(1)), pl.BlockSpec((T_BLOCK, f_pad), row), pl.BlockSpec((T_BLOCK, f_pad), row)],
+        out_specs=pl.BlockSpec((T_BLOCK, 2 * f_pad), row),
+        out_shape=jax.ShapeDtypeStruct((tokens, 2 * f_pad), BF16),
+        compiler_params=pltpu.CompilerParams(dimension_semantics=("arbitrary",), vmem_limit_bytes=60 * 2 ** 20),
+        cost_estimate=pl.CostEstimate(flops=2 * tokens * width * f_pad, bytes_accessed=2 * (dy.size + wd.size + 4 * tokens * f_pad), transcendentals=2 * tokens * f_pad),
+        name="up_back",
+    )(dy, wd, gate_low, lin_low)
+
+
+def shifted_tile(load, start, limit):
+    tile, phase = start // LANES, start % LANES
+    near = load(min(max(tile, 0), limit - 1))
+    if phase == 0:
+        return near
+    after_it = load(min(max(tile + 1, 0), limit - 1))
+    lane = lax.broadcasted_iota(jnp.int32, near.shape, 1)
+    return jnp.where(lane < LANES - phase, pltpu.roll(near, LANES - phase, 1), pltpu.roll(after_it, LANES - phase, 1))
+
+
+def gathered_tile(lo, segments, shape):
+    lane = lax.broadcasted_iota(jnp.int32, shape, 1)
+    out = jnp.zeros(shape, F32)
+    for first, length, load, there, limit in segments:
+        a, b = max(first, lo), min(first + length, lo + LANES)
+        if a < b:
+            part = shifted_tile(load, there + lo - first, limit)
+            inside = (lane >= a - lo) & (lane < b - lo)
+            out = part if b - a == LANES else jnp.where(inside, part, out)
+    return out
+
+
+def split_kernel(group, f_loc, rank_ref, w_ref, *out_refs):
+    rows, cols = w_ref.shape
+    f_pad = out_refs[0].shape[1] // 2
+
+    def load(t):
+        return w_ref[:, t * LANES:(t + 1) * LANES].astype(F32)
+
+    for r in range(group):
+        @pl.when(rank_ref[0] == r)
+        def _():
+            for q in range(group):
+                for h in range(2):
+                    segments = [(s * f_loc, f_loc, load, ((2 * h + s) * group + q) * f_loc, cols // LANES) for s in range(2)]
+                    for lo in range(0, f_pad, LANES):
+                        out_refs[r ^ q][:, h * f_pad + lo:h * f_pad + lo + LANES] = gathered_tile(lo, segments, (rows, LANES)).astype(BF16)
+
+
+def split_up(w_up, rank, group, f_loc, f_pad):
+    rows, cols = w_up.shape
+    step = 32
+    return pl.pallas_call(
+        functools.partial(split_kernel, group, f_loc),
+        grid_spec=pltpu.PrefetchScalarGridSpec(
+            num_scalar_prefetch=1,
+            grid=(rows // step,),
+            in_specs=[pl.BlockSpec((step, cols), lambda i, r: (i, 0))],
+            out_specs=[pl.BlockSpec((step, 2 * f_pad), lambda i, r: (i, 0))] * group,
+        ),
+        out_shape=[jax.ShapeDtypeStruct((rows, 2 * f_pad), BF16)] * group,
+        compiler_params=pltpu.CompilerParams(dimension_semantics=("arbitrary",)),
+        cost_estimate=pl.CostEstimate(flops=20 * rows * cols, bytes_accessed=4 * rows * cols, transcendentals=0),
+        name="split_up",
+    )(rank.reshape(1), w_up)
+
+
+def join_kernel(group, f_loc, rank_ref, *refs):
+    parts, out_ref = refs[:group], refs[group]
+    rows, cols = out_ref.shape
+    f_pad = parts[0].shape[1] // 2
+    half = cols // 2
+    for r in range(group):
+        @pl.when(rank_ref[0] == r)
+        def _():
+            def loader(ref):
+                return lambda t: ref[:, t * LANES:(t + 1) * LANES]
+
+            for h in range(2):
+                segments = [(b * f_loc, f_loc, loader(parts[r ^ (b % group)]), h * f_pad + b // group * f_loc, 2 * f_pad // LANES) for b in range(2 * group)]
+                for lo in range(0, half, LANES):
+                    out_ref[:, h * half + lo:h * half + lo + LANES] = gathered_tile(lo, segments, (rows, LANES))
+
+
+def join_up(parts, rank, group, f_loc):
+    rows, width = parts[0].shape
+    cols = 4 * group * f_loc
+    step = 32
+    return pl.pallas_call(
+        functools.partial(join_kernel, group, f_loc),
+        grid_spec=pltpu.PrefetchScalarGridSpec(
+            num_scalar_prefetch=1,
+            grid=(rows // step,),
+            in_specs=[pl.BlockSpec((step, width), lambda i, r: (i, 0))] * group,
+            out_specs=pl.BlockSpec((step, cols), lambda i, r: (i, 0)),
+        ),
+        out_shape=jax.ShapeDtypeStruct((rows, cols), F32),
+        compiler_params=pltpu.CompilerParams(dimension_semantics=("arbitrary",)),
+        cost_estimate=pl.CostEstimate(flops=20 * rows * cols, bytes_accessed=8 * rows * cols, transcendentals=0),
+        name="join_up",
+    )(rank.reshape(1), *parts)
+
+
 def solution(mesh):
     ax = mesh.axis_names[0]
     n_dev = mesh.shape[ax]
@@ -177,12 +333,14 @@
         return lax.psum_scatter(full, ax, scatter_dimension=0, tiled=True)
 
     def spread(v):
-        rows, cols = v.shape
-        out = jnp.zeros((group * rows, cols), v.dtype)
-        parts = [v, hop(v, 1), hop(v, 2)]
-        parts.append(hop(parts[2], 1))
-        for k in range(group):
-            out = lax.dynamic_update_slice(out, parts[k], (k * rows, 0))
+        v2 = hop(v, 2)
+        return [v, hop(v, 1), v2, hop(v2, 1)]
+
+    def joined(parts):
+        rows, cols = parts[0].shape
+        out = jnp.zeros((group * rows, cols), parts[0].dtype)
+        for k, v in enumerate(parts):
+            out = lax.dynamic_update_slice(out, v, (k * rows, 0))
         return out
 
     def layer(hidden, positions, grad_y, attn_gain, w_qkv, b_qkv, w_out, mlp_gain, w_up, w_down):
@@ -202,27 +360,21 @@
 
         wqkv = gather_rows(w_qkv)
         wout = gather_rows(w_out)
-        small = gather_rows(jnp.concatenate([attn_gain, b_qkv, mlp_gain])[None])
-        small, w_up, w_down, grad_y = lax.optimization_barrier((small, w_up, w_down, grad_y))
+        small = jnp.concatenate([attn_gain, b_qkv, mlp_gain])[None]
+        for k in (1, 2, group):
+            far = hop(small, k)
+            small = jnp.where((me & k) == 0, jnp.concatenate([small, far]), jnp.concatenate([far, small]))
+        up_part = split_up(w_up, rank, group, f_loc, f_pad)
+        small, *up_part, w_down, grad_y = after(small, *up_part, w_down, grad_y)
         gain_one = small[:, :h_loc].reshape(1, width).astype(F32)
         bias = small[:, h_loc:h_loc + q_loc].reshape(1, n_dev * q_loc).astype(F32)
         gain_two = small[:, h_loc + q_loc:].reshape(1, width).astype(F32)
 
-        blank = jnp.zeros((h_loc, pad), BF16)
-        up_blocks = [w_up[:, j * f_loc:(j + 1) * f_loc] for j in range(2 * n_dev)]
-        up_for = jnp.stack([jnp.concatenate([up_blocks[q], up_blocks[group + q], blank, up_blocks[n_dev + q], up_blocks[n_dev + group + q], blank], axis=1) for q in range(group)])
-        up_part = [lax.dynamic_index_in_dim(up_for, rank ^ k, 0, keepdims=False) for k in range(group)]
         up_near = [up_part[0]] + [hop(up_part[k], k) for k in (1, 2, 3)]
         up_far = [hop(v, group) for v in up_near]
-        w_all = jnp.zeros((width, 2 * f_pad), BF16)
-        for k in range(group):
-            w_all = lax.dynamic_update_slice(w_all, up_near[k], ((me ^ k) * h_loc, 0))
-            w_all = lax.dynamic_update_slice(w_all, up_far[k], ((me ^ group ^ k) * h_loc, 0))
         down_far = hop(w_down, group)
-        first = side == 0
-        wd_all = jnp.concatenate([jnp.where(first, w_down, down_far), jnp.where(first, down_far, w_down), jnp.zeros((pad, width), BF16)], axis=0)
         dy = grad_y.reshape(tokens, width)
-        dy_all = spread(dy)
+        dy_parts = [dy, hop(dy, 1), hop(dy, 2)]
 
         hid_wide = hidden.astype(F32).reshape(tokens, width)
         inv_one = norm_scale(hid_wide)
@@ -238,13 +390,26 @@
         mid_wide = mid.astype(F32)
         inv_two = norm_scale(mid_wide)
         mlp_in = (mid_wide * inv_two * gain_two).astype(BF16)
-        m_all = spread(mlp_in)
-
-        gate_low = mm(m_all, w_all[:, :f_pad], NN_DIMS).astype(BF16)
-        lin_low = mm(m_all, w_all[:, f_pad:], NN_DIMS).astype(BF16)
-        gate = gate_low.astype(F32)
-        act = (gate * jax.nn.sigmoid(gate) * lin_low.astype(F32)).astype(BF16)
-        gate_low, lin_low, act = after(gate_low, lin_low, act)
+        m_parts = spread(mlp_in)
+
+        w_all = jnp.zeros((width, 2 * f_pad), BF16)
+        for k in range(group):
+            w_all = lax.dynamic_update_slice(w_all, up_near[k], ((me ^ k) * h_loc, 0))
+        m_all = joined(m_parts[:2])
+        dy_all = joined(dy_parts[:2])
+        wd_all = lax.dynamic_update_slice(jnp.zeros((f_pad, width), BF16), w_down, (side * f_loc, 0))
+        m_all, dy_all, w_all, wd_all, up_far[2] = after(m_all, dy_all, w_all, wd_all, up_far[2])
+        for k in range(group):
+            w_all = lax.dynamic_update_slice(w_all, up_far[k], ((me ^ group ^ k) * h_loc, 0))
+        for k in (2, 3):
+            m_all = lax.dynamic_update_slice(m_all, m_parts[k], (k * tokens, 0))
+
+        gate_low, lin_low, act = up_act(m_all, w_all)
+        act, dy_far, down_far, dy_all = after(act, dy_parts[2], down_far, dy_all)
+        dy_parts[2:] = [dy_far, hop(dy_far, 1)]
+        for k in (2, 3):
+            dy_all = lax.dynamic_update_slice(dy_all, dy_parts[k], (k * tokens, 0))
+        wd_all = lax.dynamic_update_slice(wd_all, down_far, ((1 - side) * f_loc, 0))
 
         def block(rows, k, w, dims):
             return mm(rows[k * tokens:(k + 1) * tokens], w, dims)
@@ -274,62 +439,40 @@
         dwd1, act, gate_low, lin_low = after(dwd1, act, gate_low, lin_low)
         dwd1_far = send_down(dwd1)
 
-        gate, lin = gate_low.astype(F32), lin_low.astype(F32)
-        sig = jax.nn.sigmoid(gate)
-        d_act = mm(dy_all, wd_all, NT_DIMS)
-        d_gate = (d_act * lin * sig * (1.0 + gate * (1.0 - sig))).astype(BF16)
-        d_lin = (d_act * gate * sig).astype(BF16)
-        d_up = jnp.concatenate([d_gate, d_lin], axis=1)
+        d_up = up_back(dy_all, wd_all, gate_low, lin_low)
         dm3 = block(d_up, 3, w_all, NT_DIMS)
-        d_gate, d_lin, dm3 = after(d_gate, d_lin, dm3)
+        d_up, dm3 = after(d_up, dm3)
         dm3 = hop(dm3, 1)
-        d_up = jnp.concatenate([d_gate, d_lin], axis=1)
         dm1 = block(d_up, 1, w_all, NT_DIMS)
-        d_gate, d_lin, dm1 = after(d_gate, d_lin, dm1)
+        d_up, dm1 = after(d_up, dm1)
         dm1 = hop(dm1, 1)
-        d_up = jnp.concatenate([d_gate, d_lin], axis=1)
         dm2 = block(d_up, 2, w_all, NT_DIMS) + dm3
-        d_gate, d_lin, dm2 = after(d_gate, d_lin, dm2)
+        d_up, dm2 = after(d_up, dm2)
         dm2 = hop(dm2, 2)
 
-        d_up = jnp.concatenate([d_gate, d_lin], axis=1)
         far_a = up_grad(m_all, d_up, chip ^ 3)
-        d_gate, d_lin, far_a = after(d_gate, d_lin, far_a)
+        d_up, far_a = after(d_up, far_a)
         far_a = hop(far_a, group)
-        d_up = jnp.concatenate([d_gate, d_lin], axis=1)
         far_b = up_grad(m_all, d_up, chip ^ 2)
-        d_gate, d_lin, act, far_b = after(d_gate, d_lin, act, far_b)
+        d_up, act, far_b = after(d_up, act, far_b)
         far_b = hop(far_b, group)
         y1 = block(act, 1, wd_all, NN_DIMS)
-        act, d_gate, d_lin, y1 = after(act, d_gate, d_lin, y1)
+        act, d_up, y1 = after(act, d_up, y1)
         y1 = hop(y1, 1)
-        d_up = jnp.concatenate([d_gate, d_lin], axis=1)
         dm0 = block(d_up, 0, w_all, NT_DIMS)
-        d_gate, d_lin, dm0, act = after(d_gate, d_lin, dm0, act)
+        d_up, dm0, act = after(d_up, dm0, act)
         y0 = block(act, 0, wd_all, NN_DIMS)
-        d_gate, d_lin, y0 = after(d_gate, d_lin, y0)
-        d_up = jnp.concatenate([d_gate, d_lin], axis=1)
+        d_up, y0 = after(d_up, y0)
         near_a = up_grad(m_all, d_up, chip ^ 1)
-        d_gate, d_lin, near_a = after(d_gate, d_lin, near_a)
-        d_up = jnp.concatenate([d_gate, d_lin], axis=1)
-        near_b = up_grad(m_all, d_up, chip)
-        near_b, dm2 = after(near_b, dm2)
+        d_up, near_a, dm2 = after(d_up, near_a, dm2)
 
         grad_w_down = jnp.concatenate([lax.dynamic_slice(g, (side * f_loc, 0), (f_loc, half)) + far for g, far in ((dwd0, dwd0_far), (dwd1, dwd1_far))], axis=1)
 
         def rows_of(c, *parts):
             return sum(lax.dynamic_slice(v, (c * h_loc, 0), (h_loc, 2 * f_pad)) for v in parts)
 
-        pieces = [
-            rows_of(core, near_b, far_b),
-            hop(rows_of(1 - core, near_b, far_b), 1),
-            hop(rows_of(core, near_a, far_a), 2),
-            hop(rows_of(1 - core, near_a, far_a), 3),
-        ]
-        stacked = jnp.stack(pieces)
-        by_rank = [lax.dynamic_index_in_dim(stacked, rank ^ q, 0, keepdims=False) for q in range(group)]
-        cols = [v[:, lo:lo + f_loc] for lo in (0, f_loc, f_pad, f_pad + f_loc) for v in by_rank]
-        grad_w_up = jnp.concatenate(cols, axis=1)
+        piece2 = hop(rows_of(core, near_a, far_a), 2)
+        piece3 = hop(rows_of(1 - core, near_a, far_a), 3)
 
         d_m = dm0 + dm1 + dm2
         grad_mlp_gain = jnp.sum(d_m * mid_wide * inv_two, axis=0)
@@ -339,8 +482,16 @@
         grad_w_out = scatter_rows(mm(context, d_mid_low, TN_DIMS))
         d_context = mm(d_mid_low, wout, NT_DIMS).astype(BF16)
         d_proj, grad_b_qkv = attend_back(qkv, d_context, cos_t, sin_t, batch, heads, kv_heads)
-        grad_w_qkv = scatter_rows(mm(normed, d_proj, TN_DIMS))
+        grad_w_qkv = mm(normed, d_proj, TN_DIMS)
+        grad_w_qkv, d_proj = after(grad_w_qkv, d_proj)
+        grad_w_qkv = scatter_rows(grad_w_qkv)
         d_normed = mm(d_proj, wqkv, NT_DIMS)
+        d_normed, d_up = after(d_normed, d_up)
+        near_b = up_grad(m_all, d_up, chip)
+        near_b, d_normed = after(near_b, d_normed)
+        piece0 = rows_of(core, near_b, far_b)
+        piece1 = hop(rows_of(1 - core, near_b, far_b), 1)
+        grad_w_up = join_up([piece0, piece1, piece2, piece3], rank, group, f_loc)
         y0, y1, y2, mid_late, d_normed = after(y0, y1, y2, mid, d_normed)
         output = (mid_late.astype(F32) + (y0 + y1 + y2)).astype(BF16)
         grad_attn_gain = jnp.sum(d_normed * hid_wide * inv_one, axis=0)

time: 3200 us -> 2790 us (0.87)
  Pallas kernels: 143 us -> 508 us
  matrix products: 1050 us -> 687 us
  blocking collectives: 251 us -> 31.7 us
  local copies, waits for them, and re-layouts: 224 us -> 121 us
  waiting for transfers between devices: 1310 us -> 1260 us
    dot_general x23 -> x20, matrix products: 1050 us -> 687 us  [mm(): return lax.dot_general(a, b, dims, preferred_element_type=F32)]
    pallas_call x0 -> x4, Pallas kernels: none -> 312 us  [the longest x1 168 us: up_act(): pl.pallas_call(up_kernel, grid=(tokens // T_BLOCK,), in_specs=[pl.BlockSp...]
    unnamed x2 -> x1, blocking collectives: 251 us -> 31.7 us
    ppermute x27 -> x30, waiting for transfers between devices: 1310 us -> 1230 us  [hop(): return lax.ppermute(v, ax, [(i, i ^ k) for i in range(n_dev)])]
    concatenate x6 -> x0, local copies, waits for them, and re-layouts: 53.4 us -> none  [the longest x1 28.7 us: layer(): grad_w_up = jnp.concatenate(cols, axis=1)]
    another operation x3 -> x0, other arithmetic: 34.4 us -> none  [the longest x2 28.3 us: layer(): stacked = jnp.stack(pieces)]
    dynamic_update_slice x8 -> x10, local copies, waits for them, and re-layouts: 70.5 us -> 69.6 us  [the longest x4 38 us: joined(): out = lax.dynamic_update_slice(out, v, (k * rows, 0))]
  transfers between devices with their start and end apart: 31 -> 34, of which waited for: 8 -> 13; matrix products, arithmetic and copies ran while one was open for 35% -> 26% of each run, Pallas kernels for 4% -> 14%
where the time goes in v1:
time: 2790 us
  waiting for transfers between devices  1260 us (45%)
  matrix products  687 us (25%)
  Pallas kernels  508 us (18%)
  other arithmetic  149 us (5%)
  local copies, waits for them, and re-layouts  121 us (4%)
  blocking collectives  31.7 us (1%)
    ppermute x30, waiting for transfers between devices, hop(): return lax.ppermute(v, ax, [(i, i ^ k) for i in range(n_dev)])  1230 us
    dot_general x20, matrix products, mm(): return lax.dot_general(a, b, dims, preferred_element_type=F32)  687 us
    pallas_call x1, Pallas kernels, up_act(): pl.pallas_call(up_kernel, grid=(tokens // T_BLOCK,), in_specs=[pl.BlockSp...  168 us
    pallas_call x1, Pallas kernels, up_back(): pl.pallas_call(up_back_kernel, grid=(tokens // T_BLOCK,), in_specs=[pl.Bl...  110 us
    pallas_call x1, Pallas kernels, attend_back(): pl.pallas_call(functools.partial(attend_back_kernel, heads, kv_heads), gr...  109 us
    pallas_call x1, Pallas kernels, attend(): pl.pallas_call(functools.partial(attend_kernel, heads, kv_heads), grid=(b...  87.5 us
  transfers between devices with their start and end apart: 34, of which 13 were waited for; matrix products, arithmetic and copies ran while one was open for 26% of the time, Pallas kernels for 14%

profile of v1, /device:TPU:0, one launch (start us, length us, event | category | flops | bytes accessed | tf_op | source)
XLA Modules:
  0.0 2789.9 jit_solution(17044495340589162288)
XLA Ops:
  25.0 13.7 split_up.1
  46.5 23.8 all-gather.3.cloned.1.call-done
  70.3 22.4 convolution_add_fusion.z_ref
  92.7 87.5 %attend.1 = (bf16[1536,2560]{1,0:T(8,128)(2,1)}, bf16[1536,2048]{1,0:T(8,128)(2,1)}) custom-call(f32[1536,2560]{1,0:T(8,128)} %convolution_add_fusion.z_ref, f32[1536,128]{1,0:T(8,128)S(1)} %get-tuple-element.163.cos_ref, f32[1536,128]{1,0:T(8,128)S(1)} %get-tuple-element.162.sin_ref), custom_call_target="tpu_custom_call" | custom-call | flops 19327352832 | bytes 31457280 | tf_op jit(solution)/shard_map/attend/pallas_call | solution.py:142
  180.2 18.9 fusion.15
  213.7 12.2 dynamic_update_slice.56
  247.4 159.5 %collective-permute-done.6 = bf16[256,5632]{1,0:T(8,128)(2,1)} collective-permute-done((bf16[256,5632]{1,0:T(8,128)(2,1)}, bf16[256,5632]{1,0:T(8,128)(2,1)}, u32[]{:S(2)}, u32[]{:S(2)}) %collective-permute-start.6) | collective-permute-done | bytes 2883616 | tf_op jit(solution)/shard_map/ppermute | solution.py:327
  410.7 56.3 %collective-permute-done.7 = bf16[256,5632]{1,0:T(8,128)(2,1)} collective-permute-done((bf16[256,5632]{1,0:T(8,128)(2,1)}, bf16[256,5632]{1,0:T(8,128)(2,1)}, u32[]{:S(2)}, u32[]{:S(2)}) %collective-permute-start.7) | collective-permute-done | bytes 2883616 | tf_op jit(solution)/shard_map/ppermute | solution.py:327
  483.3 12.8 dynamic_update_slice.54
  510.8 21.5 collective-permute-done.11
  534.6 59.5 %collective-permute-done.12 = bf16[256,5632]{1,0:T(8,128)(2,1)S(1)} collective-permute-done((bf16[256,5632]{1,0:T(8,128)(2,1)}, bf16[256,5632]{1,0:T(8,128)(2,1)S(1)}, u32[]{:S(2)}, u32[]{:S(2)}) %collective-permute-start.12) | collective-permute-done | bytes 2883616 | tf_op jit(solution)/shard_map/ppermute | solution.py:327
  597.7 58.4 %collective-permute-done.13 = bf16[256,5632]{1,0:T(8,128)(2,1)} collective-permute-done((bf16[256,5632]{1,0:T(8,128)(2,1)}, bf16[256,5632]{1,0:T(8,128)(2,1)}, u32[]{:S(2)}, u32[]{:S(2)}) %collective-permute-start.13) | collective-permute-done | bytes 2883616 | tf_op jit(solution)/shard_map/ppermute | solution.py:327
  662.8 167.8 %up_act.1 = (bf16[6144,2816]{1,0:T(8,128)(2,1)}, bf16[6144,2816]{1,0:T(8,128)(2,1)}, bf16[6144,2816]{1,0:T(8,128)(2,1)}) custom-call(bf16[6144,2048]{1,0:T(8,128)(2,1)} %constant_dynamic-update-slice_fusion.7.m_ref, bf16[2048,5632]{1,0:T(8,128)(2,1)} %constant_dynamic-update-slice_fusion.3.w_ref), custom_call_target="tpu_custom_call" | custom-call | flops 141733920768 | bytes 152043520 | tf_op jit(solution)/shard_map/up_act/pallas_call | solution.py:188
  836.6 24.7 fusion.41
  868.3 21.4 collective-permute-done.16
  892.9 44.8 %fusion.21 = f32[2816,1024]{1,0:T(8,128)} fusion(bf16[6144,2816]{1,0:T(8,128)(2,1)} %get-tuple-element.120, bf16[6144,2048]{1,0:T(8,128)(2,1)} %constant_dynamic-update-slice_fusion.1.dy_ref), kind=kOutput, calls=%fused_computation.26 | convolution fusion | flops 35433480192 | bytes 58720256 | tf_op jit(solution)/shard_map/dot_general | solution.py:31
  937.7 25.7 convolution_add_fusion.1
  963.4 44.8 %fusion.19 = f32[2816,1024]{1,0:T(8,128)} fusion(bf16[6144,2816]{1,0:T(8,128)(2,1)} %get-tuple-element.120, bf16[6144,2048]{1,0:T(8,128)(2,1)} %constant_dynamic-update-slice_fusion.1.dy_ref), kind=kOutput, calls=%fused_computation.24 | convolution fusion | flops 35433480192 | bytes 58720256 | tf_op jit(solution)/shard_map/dot_general | solution.py:31
  1008.1 109.8 %up_back.1 = bf16[6144,5632]{1,0:T(8,128)(2,1)} custom-call(bf16[6144,2048]{1,0:T(8,128)(2,1)} %constant_dynamic-update-slice_fusion.1.dy_ref, bf16[2816,2048]{1,0:T(8,128)(2,1)} %constant_dynamic-update-slice_fusion.wd_ref, bf16[6144,2816]{1,0:T(8,128)(2,1)} %get-tuple-element.107.g_ref, bf16[6144,2816]{1,0:T(8,128)(2,1)} %get-tuple-element.108.l_ref), custom_call_target="tpu_custom_call" | custom-call | flops 70866960384 | bytes 175112192 | tf_op jit(solution)/shard_map/up_back/pallas_call | solution.py:216
  1117.9 44.9 %fusion = f32[1536,2048]{1,0:T(8,128)} fusion(bf16[2048,5632]{1,0:T(8,128)(2,1)} %constant_dynamic-update-slice_fusion.3.w_ref, bf16[6144,5632]{1,0:T(8,128)(2,1)} %up_back.1), kind=kOutput, calls=%fused_computation.4 | convolution fusion | flops 35433480192 | bytes 52953088 | tf_op jit(solution)/shard_map/dot_general | solution.py:31
  1163.0 44.7 %fusion.6 = f32[1536,2048]{1,0:T(8,128)} fusion(bf16[2048,5632]{1,0:T(8,128)(2,1)} %constant_dynamic-update-slice_fusion.3.w_ref, bf16[6144,5632]{1,0:T(8,128)(2,1)} %up_back.1), kind=kOutput, calls=%fused_computation.10 | convolution fusion | flops 35433480192 | bytes 52953088 | tf_op jit(solution)/shard_map/dot_general | solution.py:31
  1208.0 47.4 %fusion.43 = f32[1536,2048]{1,0:T(8,128)} fusion(f32[1536,2048]{1,0:T(8,128)} %collective-permute-done.18, bf16[2048,5632]{1,0:T(8,128)(2,1)} %constant_dynamic-update-slice_fusion.3.w_ref, bf16[6144,5632]{1,0:T(8,128)(2,1)} %up_back.1), kind=kOutput, calls=%fused_computation.57 | convolution fusion | flops 35436625920 | bytes 65536000 | tf_op jit(solution)/shard_map/dot_general | solution.py:31
  1255.4 47.3 %fusion.52 = f32[512,5632]{1,0:T(8,128)} fusion(bf16[6144,5632]{1,0:T(8,128)(2,1)} %up_back.1, bf16[6144,2048]{1,0:T(8,128)(2,1)} %constant_dynamic-update-slice_fusion.7.m_ref, s32[]{:T(128)S(6)} %select_n.128), kind=kOutput, calls=%fused_computation.65 | convolution fusion | flops 35433480192 | bytes 87031808 | tf_op jit(solution)/shard_map/dot_general | solution.py:31
  1302.7 47.1 %fusion.50 = f32[512,5632]{1,0:T(8,128)} fusion(bf16[6144,5632]{1,0:T(8,128)(2,1)} %up_back.1, bf16[6144,2048]{1,0:T(8,128)(2,1)} %constant_dynamic-update-slice_fusion.7.m_ref, s32[]{:T(128)S(6)} %select_n.129), kind=kOutput, calls=%fused_computation.63 | convolution fusion | flops 35433480192 | bytes 87031808 | tf_op jit(solution)/shard_map/dot_general | solution.py:31
  1349.8 24.9 fusion.38
  1376.3 44.6 %fusion.2 = f32[1536,2048]{1,0:T(8,128)} fusion(bf16[2048,5632]{1,0:T(8,128)(2,1)} %constant_dynamic-update-slice_fusion.3.w_ref, bf16[6144,5632]{1,0:T(8,128)(2,1)} %up_back.1), kind=kOutput, calls=%fused_computation.6 | convolution fusion | flops 35433480192 | bytes 52953088 | tf_op jit(solution)/shard_map/dot_general | solution.py:31
  1420.9 24.8 fusion.36
  1445.7 46.9 %fusion.46 = f32[512,5632]{1,0:T(8,128)} fusion(bf16[6144,5632]{1,0:T(8,128)(2,1)} %up_back.1, bf16[6144,2048]{1,0:T(8,128)(2,1)} %constant_dynamic-update-slice_fusion.7.m_ref, s32[]{:T(128)S(6)} %select_n.131), kind=kOutput, calls=%fused_computation.59 | convolution fusion | flops 35433480192 | bytes 87031808 | tf_op jit(solution)/shard_map/dot_general | solution.py:31
  1492.6 154.9 %collective-permute-done.22 = f32[1536,2048]{1,0:T(8,128)} collective-permute-done((f32[1536,2048]{1,0:T(8,128)}, f32[1536,2048]{1,0:T(8,128)}, u32[]{:S(2)}, u32[]{:S(2)}) %collective-permute-start.22) | collective-permute-done | bytes 12582944 | tf_op jit(solution)/shard_map/ppermute | solution.py:327
  1647.5 21.3 fusion.18
  1668.8 14.4 fusion.14
  1683.2 20.0 fusion.54
  1703.3 20.8 convolution_convert_fusion.dctx_ref
  1724.1 108.7 %attend_back.1 = (bf16[1536,2560]{1,0:T(8,128)(2,1)}, f32[1,2560]{1,0:T(1,128)S(1)}) custom-call(bf16[1536,2560]{1,0:T(8,128)(2,1)} %get-tuple-element.124.qkv_ref, bf16[1536,2048]{1,0:T(8,128)(2,1)} %convolution_convert_fusion.dctx_ref, f32[1536,128]{1,0:T(8,128)S(1)} %get-tuple-element.163.cos_ref, f32[1536,128]{1,0:T(8,128)S(1)} %get-tuple-element.162.sin_ref), custom_call_target="tpu_custom_call" | custom-call | flops 48318382080 | bytes 31457280 | tf_op jit(solution)/shard_map/attend_back/pallas_call | solution.py:159
  1832.8 22.1 fusion.68
  1869.7 441.2 %collective-permute-done.28 = f32[1376,1024]{1,0:T(8,128)} collective-permute-done((f32[1376,1024]{1,0:T(8,128)S(1)}, f32[1376,1024]{1,0:T(8,128)}, u32[]{:S(2)}, u32[]{:S(2)}) %collective-permute-start.28) | collective-permute-done | bytes 5636128 | tf_op jit(solution)/shard_map/ppermute | solution.py:327
  2319.7 112.1 %collective-permute-done.29 = f32[1376,1024]{1,0:T(8,128)} collective-permute-done((f32[1376,1024]{1,0:T(8,128)}, f32[1376,1024]{1,0:T(8,128)}, u32[]{:S(2)}, u32[]{:S(2)}) %collective-permute-start.29) | collective-permute-done | bytes 5636128 | tf_op jit(solution)/shard_map/ppermute | solution.py:327
  2431.8 8.7 dynamic-slice_add_fusion.4
  2440.4 10.5 pad_maximum_fusion
  2450.9 13.0 dynamic-slice_add_fusion
  2465.2 22.9 fusion.69
  2488.2 47.1 %fusion.48 = f32[512,5632]{1,0:T(8,128)} fusion(bf16[6144,5632]{1,0:T(8,128)(2,1)} %up_back.1, bf16[6144,2048]{1,0:T(8,128)(2,1)} %constant_dynamic-update-slice_fusion.7.m_ref, s32[]{:T(128)S(6)} %select_n.130), kind=kOutput, calls=%fused_computation.61 | convolution fusion | flops 35433480192 | bytes 87031808 | tf_op jit(solution)/shard_map/dot_general | solution.py:31
  2535.3 141.8 %collective-permute-done.23 = f32[512,5632]{1,0:T(8,128)} collective-permute-done((f32[512,5632]{1,0:T(8,128)}, f32[512,5632]{1,0:T(8,128)}, u32[]{:S(2)}, u32[]{:S(2)}) %collective-permute-start.23) | collective-permute-done | bytes 11534368 | tf_op jit(solution)/shard_map/ppermute | solution.py:327
  2677.1 12.8 dynamic-slice_add_fusion.2
  2696.6 31.7 %all-reduce.2 = f32[8,832]{1,0:T(8,128)S(1)} all-reduce(f32[8,832]{1,0:T(8,128)S(1)} %pad_maximum_fusion.1), channel_id=2, replica_groups=mesh['fsdp'=8] {'fsdp'}, use_global_device_ids=true, to_apply=%region_6.7.clone | all-reduce | flops 6656 | bytes 53248
  2729.6 14.2 fusion.30
  2743.9 18.3 add_convert_fusion
  2762.1 21.0 join_up.1
  (148 shorter events, 160.2 us)
Async XLA Ops:
  7.2 63.2 %all-gather.3.cloned.1.call-start = ((), (), s32[]{:S(2)}) async-start(), calls=%async_computation.2 | async-start | bytes 11796480 | tf_op jit(solution)/shard_map/all_gather | solution.py:330
  7.9 172.3 %all-gather.5.cloned.1.call-start = ((), (), s32[]{:S(2)}) async-start(), calls=%async_computation.3 | async-start | bytes 9437184 | tf_op jit(solution)/shard_map/all_gather | solution.py:330
  8.7 2774.5 %reduce-scatter.5.cloned.1.call-start = ((), (), s32[]{:S(2)}) async-start(), calls=%async_computation.5 | async-start | bytes 18874368 | tf_op jit(solution)/shard_map/reduce_scatter | solution.py:333
  9.5 8.8 collective-permute-start
  18.3 4.6 collective-permute-start.1
  21.1 71.6 %copy-start.4 = (f32[1536]{0:T(1024)}, f32[1536]{0:T(1024)S(1)}, u32[]{:S(2)}) copy-start(f32[1536]{0:T(1024)S(1)} %rsqrt.20) | copy-start | bytes 18436
  22.9 15.8 collective-permute-start.2
  38.8 54.0 %copy-start.6 = (f32[1,2,8,128]{3,1,2,0:T(2,128)}, f32[1,2,8,128]{3,1,2,0:T(2,128)S(1)}, u32[]{:S(2)}) copy-start(f32[1,2,8,128]{3,1,2,0:T(2,128)S(1)} %copy.19) | copy-start | bytes 24580
  38.9 160.3 %copy-start.8 = (f32[1,2,8,128]{3,1,2,0:T(2,128)}, f32[1,2,8,128]{3,1,2,0:T(2,128)S(1)}, u32[]{:S(2)}) copy-start(f32[1,2,8,128]{3,1,2,0:T(2,128)S(1)} %copy.20) | copy-start | bytes 24580
  199.1 8.4 copy-start.13
  206.5 261.1 %collective-permute-start.9 = (bf16[1536,2048]{1,0:T(8,128)(2,1)}, bf16[1536,2048]{1,0:T(8,128)(2,1)}, u32[]{:S(2)}, u32[]{:S(2)}) collective-permute-start(bf16[1536,2048]{1,0:T(8,128)(2,1)} %fusion.10), channel_id=1, source_target_pairs={{0,2},{1,3},{2,0},{3,1},{4,6},{5,7},{6,4},{7,5}} | collective-permute-start | bytes 18874376 | tf_op jit(solution)/shard_map/ppermute | solution.py:327
  207.5 5.4 collective-permute-start.5
  207.5 264.2 %collective-permute-start.4 = (bf16[1536,2048]{1,0:T(8,128)(2,1)}, bf16[1536,2048]{1,0:T(8,128)(2,1)}, u32[]{:S(2)}, u32[]{:S(2)}) collective-permute-start(bf16[1536,2048]{1,0:T(8,128)(2,1)} %bitcast.2), channel_id=1, source_target_pairs={{0,1},{1,0},{2,3},{3,2},{4,5},{5,4},{6,7},{7,6}} | collective-permute-start | bytes 18874376 | tf_op jit(solution)/shard_map/ppermute | solution.py:327
  208.0 288.1 %collective-permute-start.3 = (bf16[1536,2048]{1,0:T(8,128)(2,1)}, bf16[1536,2048]{1,0:T(8,128)(2,1)}, u32[]{:S(2)}, u32[]{:S(2)}) collective-permute-start(bf16[1536,2048]{1,0:T(8,128)(2,1)} %fusion.10), channel_id=1, source_target_pairs={{0,1},{1,0},{2,3},{3,2},{4,5},{5,4},{6,7},{7,6}} | collective-permute-start | bytes 18874376 | tf_op jit(solution)/shard_map/ppermute | solution.py:327
  208.0 198.9 %collective-permute-start.6 = (bf16[256,5632]{1,0:T(8,128)(2,1)}, bf16[256,5632]{1,0:T(8,128)(2,1)}, u32[]{:S(2)}, u32[]{:S(2)}) collective-permute-start(bf16[256,5632]{1,0:T(8,128)(2,1)} %get-tuple-element.88), channel_id=1, source_target_pairs={{0,2},{1,3},{2,0},{3,1},{4,6},{5,7},{6,4},{7,5}} | collective-permute-start | bytes 8650760 | tf_op jit(solution)/shard_map/ppermute | solution.py:327
  212.9 254.1 %collective-permute-start.7 = (bf16[256,5632]{1,0:T(8,128)(2,1)}, bf16[256,5632]{1,0:T(8,128)(2,1)}, u32[]{:S(2)}, u32[]{:S(2)}) collective-permute-start(bf16[256,5632]{1,0:T(8,128)(2,1)} %get-tuple-element.89), channel_id=1, source_target_pairs={{0,3},{1,2},{2,1},{3,0},{4,7},{5,6},{6,5},{7,4}} | collective-permute-start | bytes 8650760 | tf_op jit(solution)/shard_map/ppermute | solution.py:327
  237.6 8.1 copy-start.3
  407.0 96.9 %collective-permute-start.8 = (bf16[256,5632]{1,0:T(8,128)(2,1)}, bf16[256,5632]{1,0:T(8,128)(2,1)S(1)}, u32[]{:S(2)}, u32[]{:S(2)}) collective-permute-start(bf16[256,5632]{1,0:T(8,128)(2,1)} %collective-permute-done.6), channel_id=1, source_target_pairs={{0,4},{1,5},{2,6},{3,7},{4,0},{5,1},{6,2},{7,3}} | collective-permute-start | bytes 8650760 | tf_op jit(solution)/shard_map/ppermute | solution.py:327
  467.0 65.4 %collective-permute-start.11 = (bf16[256,5632]{1,0:T(8,128)(2,1)S(1)}, bf16[256,5632]{1,0:T(8,128)(2,1)S(1)}, u32[]{:S(2)}, u32[]{:S(2)}) collective-permute-start(bf16[256,5632]{1,0:T(8,128)(2,1)S(1)} %copy-done.3), channel_id=1, source_target_pairs={{0,4},{1,5},{2,6},{3,7},{4,0},{5,1},{6,2},{7,3}} | collective-permute-start | bytes 8650760 | tf_op jit(solution)/shard_map/ppermute | solution.py:327
  467.5 192.0 %collective-permute-start.10 = (bf16[1536,2048]{1,0:T(8,128)(2,1)}, bf16[1536,2048]{1,0:T(8,128)(2,1)S(1)}, u32[]{:S(2)}, u32[]{:S(2)}) collective-permute-start(bf16[1536,2048]{1,0:T(8,128)(2,1)} %collective-permute-done.9), channel_id=1, source_target_pairs={{0,1},{1,0},{2,3},{3,2},{4,5},{5,4},{6,7},{7,6}} | collective-permute-start | bytes 18874376 | tf_op jit(solution)/shard_map/ppermute | solution.py:327
  471.7 122.4 %collective-permute-start.12 = (bf16[256,5632]{1,0:T(8,128)(2,1)}, bf16[256,5632]{1,0:T(8,128)(2,1)S(1)}, u32[]{:S(2)}, u32[]{:S(2)}) collective-permute-start(bf16[256,5632]{1,0:T(8,128)(2,1)} %collective-permute-done.5), channel_id=1, source_target_pairs={{0,4},{1,5},{2,6},{3,7},{4,0},{5,1},{6,2},{7,3}} | collective-permute-start | bytes 8650760 | tf_op jit(solution)/shard_map/ppermute | solution.py:327
  496.1 334.5 %collective-permute-start.14 = (bf16[1536,2048]{1,0:T(8,128)(2,1)}, bf16[1536,2048]{1,0:T(8,128)(2,1)}, u32[]{:S(2)}, u32[]{:S(2)}) collective-permute-start(bf16[1536,2048]{1,0:T(8,128)(2,1)} %bitcast.2), channel_id=1, source_target_pairs={{0,2},{1,3},{2,0},{3,1},{4,6},{5,7},{6,4},{7,5}} | collective-permute-start | bytes 18874376 | tf_op jit(solution)/shard_map/ppermute | solution.py:327
  503.9 152.2 %collective-permute-start.13 = (bf16[256,5632]{1,0:T(8,128)(2,1)}, bf16[256,5632]{1,0:T(8,128)(2,1)}, u32[]{:S(2)}, u32[]{:S(2)}) collective-permute-start(bf16[256,5632]{1,0:T(8,128)(2,1)} %collective-permute-done.7), channel_id=1, source_target_pairs={{0,4},{1,5},{2,6},{3,7},{4,0},{5,1},{6,2},{7,3}} | collective-permute-start | bytes 8650760 | tf_op jit(solution)/shard_map/ppermute | solution.py:327
  532.4 298.3 %collective-permute-start.15 = (bf16[1376,2048]{1,0:T(8,128)(2,1)}, bf16[1376,2048]{1,0:T(8,128)(2,1)}, u32[]{:S(2)}, u32[]{:S(2)}) collective-permute-start(bf16[1376,2048]{1,0:T(8,128)(2,1)} %param.19), channel_id=1, source_target_pairs={{0,4},{1,5},{2,6},{3,7},{4,0},{5,1},{6,2},{7,3}} | collective-permute-start | bytes 16908296 | tf_op jit(solution)/shard_map/ppermute | solution.py:327
  861.3 76.4 %collective-permute-start.17 = (f32[1536,2048]{1,0:T(8,128)}, f32[1536,2048]{1,0:T(8,128)}, u32[]{:S(2)}, u32[]{:S(2)}) collective-permute-start(f32[1536,2048]{1,0:T(8,128)} %fusion.41), channel_id=1, source_target_pairs={{0,1},{1,0},{2,3},{3,2},{4,5},{5,4},{6,7},{7,6}} | collective-permute-start | bytes 37748744 | tf_op jit(solution)/shard_map/ppermute | solution.py:327
  861.3 28.4 %collective-permute-start.16 = (bf16[1536,2048]{1,0:T(8,128)(2,1)}, bf16[1536,2048]{1,0:T(8,128)(2,1)S(1)}, u32[]{:S(2)}, u32[]{:S(2)}) collective-permute-start(bf16[1536,2048]{1,0:T(8,128)(2,1)} %collective-permute-done.14), channel_id=1, source_target_pairs={{0,1},{1,0},{2,3},{3,2},{4,5},{5,4},{6,7},{7,6}} | collective-permute-start | bytes 18874376 | tf_op jit(solution)/shard_map/ppermute | solution.py:327
  1162.8 45.2 %collective-permute-start.18 = (f32[1536,2048]{1,0:T(8,128)}, f32[1536,2048]{1,0:T(8,128)}, u32[]{:S(2)}, u32[]{:S(2)}) collective-permute-start(f32[1536,2048]{1,0:T(8,128)} %fusion), channel_id=1, source_target_pairs={{0,1},{1,0},{2,3},{3,2},{4,5},{5,4},{6,7},{7,6}} | collective-permute-start | bytes 37748744 | tf_op jit(solution)/shard_map/ppermute | solution.py:327
  1207.7 439.8 %collective-permute-start.21 = (f32[1536,2048]{1,0:T(8,128)}, f32[1536,2048]{1,0:T(8,128)}, u32[]{:S(2)}, u32[]{:S(2)}) collective-permute-start(f32[1536,2048]{1,0:T(8,128)} %fusion.6), channel_id=1, source_target_pairs={{0,1},{1,0},{2,3},{3,2},{4,5},{5,4},{6,7},{7,6}} | collective-permute-start | bytes 37748744 | tf_op jit(solution)/shard_map/ppermute | solution.py:327
  1374.7 272.8 %collective-permute-start.22 = (f32[1536,2048]{1,0:T(8,128)}, f32[1536,2048]{1,0:T(8,128)}, u32[]{:S(2)}, u32[]{:S(2)}) collective-permute-start(f32[1536,2048]{1,0:T(8,128)} %fusion.43), channel_id=1, source_target_pairs={{0,2},{1,3},{2,0},{3,1},{4,6},{5,7},{6,4},{7,5}} | collective-permute-start | bytes 37748744 | tf_op jit(solution)/shard_map/ppermute | solution.py:327
  1445.7 201.8 %copy-start.9 = (f32[1,2,8,128]{3,1,2,0:T(2,128)S(1)}, f32[1,2,8,128]{3,1,2,0:T(2,128)}, u32[]{:S(2)}) copy-start(f32[1,2,8,128]{3,1,2,0:T(2,128)} %copy-done.8) | copy-start | bytes 24580
  1445.7 201.8 %copy-start.11 = (f32[1536]{0:T(1024)S(1)}, f32[1536]{0:T(1024)}, u32[]{:S(2)}) copy-start(f32[1536]{0:T(1024)} %copy-done.10) | copy-start | bytes 18436
  1492.6 176.2 %copy-start.1 = (bf16[1536,2048]{1,0:T(8,128)(2,1)S(1)}, bf16[1536,2048]{1,0:T(8,128)(2,1)}, u32[]{:S(2)}) copy-start(bf16[1536,2048]{1,0:T(8,128)(2,1)} %copy-done) | copy-start | bytes 18874372
  1668.8 14.4 copy-start.14
  1703.2 1079.9 %reduce-scatter.3.cloned.1.call-start = ((), (), s32[]{:S(2)}) async-start(), calls=%async_computation.4 | async-start | bytes 23592960 | tf_op jit(solution)/shard_map/reduce_scatter | solution.py:333
  1703.2 129.5 %slice-start = ((s8[6291456]{0:T(1024)(128)(4,1)}), s8[2097152]{0:T(1024)(128)(4,1)S(1)}, s32[]{:S(2)}) async-start(s8[6291456]{0:T(1024)(128)(4,1)} %bitcast.68), calls=%async_computation.6 | async-start | bytes 4194304
  1724.1 108.7 %slice-start.1 = ((s8[6291456]{0:T(1024)(128)(4,1)}), s8[4194304]{0:T(1024)(128)(4,1)S(1)}, s32[]{:S(2)}) async-start(s8[6291456]{0:T(1024)(128)(4,1)} %bitcast.68), calls=%async_computation.7 | async-start | bytes 8388608
  1854.9 596.0 %collective-permute-start.25 = (f32[512,5632]{1,0:T(8,128)}, f32[512,5632]{1,0:T(8,128)}, u32[]{:S(2)}, u32[]{:S(2)}) collective-permute-start(f32[512,5632]{1,0:T(8,128)} %fusion.52), channel_id=1, source_target_pairs={{0,4},{1,5},{2,6},{3,7},{4,0},{5,1},{6,2},{7,3}} | collective-permute-start | bytes 34603016 | tf_op jit(solution)/shard_map/ppermute | solution.py:327
  1858.1 452.9 %collective-permute-start.28 = (f32[1376,1024]{1,0:T(8,128)S(1)}, f32[1376,1024]{1,0:T(8,128)}, u32[]{:S(2)}, u32[]{:S(2)}) collective-permute-start(f32[1376,1024]{1,0:T(8,128)S(1)} %constant_dynamic-slice_fusion.1), channel_id=1, source_target_pairs={{0,4},{1,5},{2,6},{3,7},{4,0},{5,1},{6,2},{7,3}} | collective-permute-start | bytes 16908296 | tf_op jit(solution)/shard_map/ppermute | solution.py:327
  1868.4 563.4 %collective-permute-start.29 = (f32[1376,1024]{1,0:T(8,128)}, f32[1376,1024]{1,0:T(8,128)}, u32[]{:S(2)}, u32[]{:S(2)}) collective-permute-start(f32[1376,1024]{1,0:T(8,128)} %constant_dynamic-slice_fusion), channel_id=1, source_target_pairs={{0,4},{1,5},{2,6},{3,7},{4,0},{5,1},{6,2},{7,3}} | collective-permute-start | bytes 16908296 | tf_op jit(solution)/shard_map/ppermute | solution.py:327
  1868.4 821.6 %collective-permute-start.20 = (f32[1536,2048]{1,0:T(8,128)}, f32[1536,2048]{1,0:T(8,128)}, u32[]{:S(2)}, u32[]{:S(2)}) collective-permute-start(f32[1536,2048]{1,0:T(8,128)} %convolution_add_fusion.1), channel_id=1, source_target_pairs={{0,2},{1,3},{2,0},{3,1},{4,6},{5,7},{6,4},{7,5}} | collective-permute-start | bytes 37748744 | tf_op jit(solution)/shard_map/ppermute | solution.py:327
  1869.7 820.2 %collective-permute-start.19 = (f32[1536,2048]{1,0:T(8,128)}, f32[1536,2048]{1,0:T(8,128)}, u32[]{:S(2)}, u32[]{:S(2)}) collective-permute-start(f32[1536,2048]{1,0:T(8,128)} %fusion.38), channel_id=1, source_target_pairs={{0,1},{1,0},{2,3},{3,2},{4,5},{5,4},{6,7},{7,6}} | collective-permute-start | bytes 37748744 | tf_op jit(solution)/shard_map/ppermute | solution.py:327
  2311.0 366.1 %collective-permute-start.23 = (f32[512,5632]{1,0:T(8,128)}, f32[512,5632]{1,0:T(8,128)}, u32[]{:S(2)}, u32[]{:S(2)}) collective-permute-start(f32[512,5632]{1,0:T(8,128)} %fusion.50), channel_id=1, source_target_pairs={{0,4},{1,5},{2,6},{3,7},{4,0},{5,1},{6,2},{7,3}} | collective-permute-start | bytes 34603016 | tf_op jit(solution)/shard_map/ppermute | solution.py:327
  2463.9 298.2 %collective-permute-start.26 = (f32[256,5632]{1,0:T(8,128)}, f32[256,5632]{1,0:T(8,128)}, u32[]{:S(2)}, u32[]{:S(2)}) collective-permute-start(f32[256,5632]{1,0:T(8,128)} %get-tuple-element.155), channel_id=1, source_target_pairs={{0,2},{1,3},{2,0},{3,1},{4,6},{5,7},{6,4},{7,5}} | collective-permute-start | bytes 17301512 | tf_op jit(solution)/shard_map/ppermute | solution.py:327
  2465.2 296.9 %collective-permute-start.27 = (f32[256,5632]{1,0:T(8,128)}, f32[256,5632]{1,0:T(8,128)}, u32[]{:S(2)}, u32[]{:S(2)}) collective-permute-start(f32[256,5632]{1,0:T(8,128)} %get-tuple-element.154), channel_id=1, source_target_pairs={{0,3},{1,2},{2,1},{3,0},{4,7},{5,6},{6,5},{7,4}} | collective-permute-start | bytes 17301512 | tf_op jit(solution)/shard_map/ppermute | solution.py:327
  2535.3 154.7 %copy-start.2 = (f32[1536,2048]{1,0:T(8,128)S(1)}, f32[1536,2048]{1,0:T(8,128)}, u32[]{:S(2)}) copy-start(f32[1536,2048]{1,0:T(8,128)} %fusion.69) | copy-start | bytes 37748740
  2535.3 154.7 %copy-start.5 = (f32[1536]{0:T(1024)S(1)}, f32[1536]{0:T(1024)}, u32[]{:S(2)}) copy-start(f32[1536]{0:T(1024)} %copy-done.4) | copy-start | bytes 18436
  2535.3 154.7 %copy-start.7 = (f32[1,2,8,128]{3,1,2,0:T(2,128)S(1)}, f32[1,2,8,128]{3,1,2,0:T(2,128)}, u32[]{:S(2)}) copy-start(f32[1,2,8,128]{3,1,2,0:T(2,128)} %copy-done.6) | copy-start | bytes 24580
  2690.0 72.2 %collective-permute-start.24 = (f32[256,5632]{1,0:T(8,128)}, f32[256,5632]{1,0:T(8,128)}, u32[]{:S(2)}, u32[]{:S(2)}) collective-permute-start(f32[256,5632]{1,0:T(8,128)} %get-tuple-element.156), channel_id=1, source_target_pairs={{0,1},{1,0},{2,3},{3,2},{4,5},{5,4},{6,7},{7,6}} | collective-permute-start | bytes 17301512 | tf_op jit(solution)/shard_map/ppermute | solution.py:327
  (3 other events, 17.0 us)
Sparse Core Ops, SparseCore 0:
  9.8 60.5 all-gather.2
  72.2 48.6 all-gather.4
  1703.3 108.0 reduce-scatter.4
  1855.0 214.4 reduce-scatter.2

commit v2 on v1

--- a/solution.py
+++ b/solution.py
@@ -21,7 +21,8 @@
 SCALE = HEAD_DIM ** -0.5
 MASKED = -1e30
 Q_BLOCK = 128
-T_BLOCK = 512
+S_BLOCK = 64
+T_BLOCK = 768
 F_BLOCK = 256
 LANES = 128
 LOG2_E = 1.4426950408889634
@@ -54,19 +55,7 @@
     return jnp.where(lane % 2 == 0, pltpu.roll(v, HEAD_DIM - 1, 1), pltpu.roll(v, 1, 1))
 
 
-def causal_probs(q, k):
-    n = q.shape[0]
-    full = k.shape[0] - n
-    s = mm(q, k, NT_DIMS)
-    row = lax.broadcasted_iota(jnp.int32, (n, n), 0)
-    col = lax.broadcasted_iota(jnp.int32, (n, n), 1)
-    own = jnp.where(row >= col, s[:, full:], MASKED)
-    s = own if full == 0 else jnp.concatenate([s[:, :full], own], axis=1)
-    e = jnp.exp2((s - jnp.max(s, axis=1, keepdims=True)) * (SCALE * LOG2_E))
-    return e * (1.0 / jnp.sum(e, axis=1, keepdims=True))
-
-
-def attend_kernel(heads, kv_heads, z_ref, cos_ref, sin_ref, qkv_ref, ctx_ref):
+def attend_kernel(heads, kv_heads, z_ref, cos_ref, sin_ref, qkv_ref, ctx_ref, s_ref, p_ref):
     seq_len = z_ref.shape[0]
     group = heads // kv_heads
     cos_t, sin_t = cos_ref[...], sin_ref[...]
@@ -74,28 +63,40 @@
     def cols(i):
         return pl.ds(pl.multiple_of(i * HEAD_DIM, HEAD_DIM), HEAD_DIM)
 
-    for g in range(kv_heads):
+    @pl.loop(0, heads + kv_heads)
+    def _(i):
+        zh = z_ref[:, cols(i)]
+        qkv_ref[:, cols(i)] = (zh * cos_t + swap_pairs(zh) * sin_t).astype(BF16)
+
+    qkv_ref[:, (heads + kv_heads) * HEAD_DIM:] = z_ref[:, (heads + kv_heads) * HEAD_DIM:].astype(BF16)
+
+    @pl.loop(0, kv_heads)
+    def _(g):
         kc, vc = cols(heads + g), cols(heads + kv_heads + g)
-        zk = z_ref[:, kc]
-        qkv_ref[:, kc] = (zk * cos_t + swap_pairs(zk) * sin_t).astype(BF16)
-        qkv_ref[:, vc] = z_ref[:, vc].astype(BF16)
-
-        @pl.loop(0, group)
-        def _(h):
-            hc = cols(g * group + h)
-            zq = z_ref[:, hc]
-            q = (zq * cos_t + swap_pairs(zq) * sin_t).astype(BF16)
-            qkv_ref[:, hc] = q
-            for r in range(0, seq_len, Q_BLOCK):
-                n = r + Q_BLOCK
-                p = causal_probs(q[r:n], qkv_ref[:n, kc]).astype(BF16)
-                ctx_ref[r:n, hc] = mm(p, qkv_ref[:n, vc], NN_DIMS).astype(BF16)
-
-
-def attend_back_kernel(heads, kv_heads, qkv_ref, dctx_ref, cos_ref, sin_ref, dz_ref, sum_ref, dk_ref, dv_ref):
+        for r in range(0, seq_len, Q_BLOCK):
+            n = r + Q_BLOCK
+            q = jnp.concatenate([qkv_ref[r:n, cols(g * group + h)] for h in range(group)], axis=0)
+            s_ref[:, :n] = mm(q, qkv_ref[:n, kc], NT_DIMS)
+
+            @pl.loop(0, group * Q_BLOCK // S_BLOCK, unroll=2)
+            def _(c):
+                rows = pl.ds(pl.multiple_of(c * S_BLOCK, S_BLOCK), S_BLOCK)
+                s = s_ref[rows, :n]
+                row = lax.broadcasted_iota(jnp.int32, (S_BLOCK, Q_BLOCK), 0) + lax.rem(c * S_BLOCK, Q_BLOCK)
+                col = lax.broadcasted_iota(jnp.int32, (S_BLOCK, Q_BLOCK), 1)
+                own = jnp.where(row >= col, s[:, r:], MASKED)
+                s = own if r == 0 else jnp.concatenate([s[:, :r], own], axis=1)
+                e = jnp.exp2((s - jnp.max(s, axis=1, keepdims=True)) * (SCALE * LOG2_E))
+                p_ref[rows, :n] = (e * (1.0 / jnp.sum(e, axis=1, keepdims=True))).astype(BF16)
+
+            ctx = mm(p_ref[:, :n], qkv_ref[:n, vc], NN_DIMS).astype(BF16)
+            for h in range(group):
+                ctx_ref[r:n, cols(g * group + h)] = ctx[h * Q_BLOCK:(h + 1) * Q_BLOCK]
+
+
+def attend_back_kernel(heads, kv_heads, qkv_ref, dctx_ref, cos_ref, sin_ref, dz_ref, sum_ref, dk_ref, dv_ref, s_ref, dp_ref, p_ref, ds_ref):
     seq_len = qkv_ref.shape[0]
     group = heads // kv_heads
-    cos_t, sin_t = cos_ref[...], sin_ref[...]
 
     def cols(i):
         return pl.ds(pl.multiple_of(i * HEAD_DIM, HEAD_DIM), HEAD_DIM)
@@ -104,34 +105,48 @@
     def _():
         sum_ref[...] = jnp.zeros_like(sum_ref)
 
-    def put(c, d):
-        dz_ref[:, c] = d.astype(BF16)
+    def put(rows, c, d):
+        dz_ref[rows, c] = d.astype(BF16)
         sum_ref[:, c] += jnp.sum(d, axis=0, keepdims=True)
 
-    for g in range(kv_heads):
+    def turned_back(rows, d):
+        return d * cos_ref[rows, :] - swap_pairs(d) * sin_ref[rows, :]
+
+    @pl.loop(0, kv_heads)
+    def _(g):
         kc, vc = cols(heads + g), cols(heads + kv_heads + g)
         dk_ref[...] = jnp.zeros_like(dk_ref)
         dv_ref[...] = jnp.zeros_like(dv_ref)
-
-        @pl.loop(0, group)
-        def _(h):
-            hc = cols(g * group + h)
-            dq = []
-            for r in range(0, seq_len, Q_BLOCK):
-                n = r + Q_BLOCK
-                q, k, v, d = qkv_ref[r:n, hc], qkv_ref[:n, kc], qkv_ref[:n, vc], dctx_ref[r:n, hc]
-                p = causal_probs(q, k)
-                dp = mm(d, v, NT_DIMS)
-                dv_ref[:n] += mm(p.astype(BF16), d, TN_DIMS)
-                ds = (p * (dp - jnp.sum(p * dp, axis=1, keepdims=True)) * SCALE).astype(BF16)
-                dq.append(mm(ds, k, NN_DIMS))
-                dk_ref[:n] += mm(ds, q, TN_DIMS)
-            dq = jnp.concatenate(dq, axis=0)
-            put(hc, dq * cos_t - swap_pairs(dq) * sin_t)
-
-        dk = dk_ref[...]
-        put(kc, dk * cos_t - swap_pairs(dk) * sin_t)
-        put(vc, dv_ref[...])
+        for r in range(0, seq_len, Q_BLOCK):
+            n = r + Q_BLOCK
+            q = jnp.concatenate([qkv_ref[r:n, cols(g * group + h)] for h in range(group)], axis=0)
+            d = jnp.concatenate([dctx_ref[r:n, cols(g * group + h)] for h in range(group)], axis=0)
+            s_ref[:n] = mm(qkv_ref[:n, kc], q, NT_DIMS)
+            dp_ref[:n] = mm(qkv_ref[:n, vc], d, NT_DIMS)
+
+            @pl.loop(0, group)
+            def _(h):
+                c = cols(h)
+                s, dp = s_ref[:n, c], dp_ref[:n, c]
+                row = lax.broadcasted_iota(jnp.int32, (Q_BLOCK, Q_BLOCK), 0)
+                col = lax.broadcasted_iota(jnp.int32, (Q_BLOCK, Q_BLOCK), 1)
+                own = jnp.where(row <= col, s[r:], MASKED)
+                s = own if r == 0 else jnp.concatenate([s[:r], own], axis=0)
+                e = jnp.exp2((s - jnp.max(s, axis=0, keepdims=True)) * (SCALE * LOG2_E))
+                p = e * (1.0 / jnp.sum(e, axis=0, keepdims=True))
+                p_ref[:n, c] = p.astype(BF16)
+                ds_ref[:n, c] = (p * (dp - jnp.sum(p * dp, axis=0, keepdims=True)) * SCALE).astype(BF16)
+
+            dv_ref[:n] += mm(p_ref[:n], d, NN_DIMS)
+            dk_ref[:n] += mm(ds_ref[:n], q, NN_DIMS)
+            dq = mm(qkv_ref[:n, kc], ds_ref[:n], TN_DIMS)
+            for h in range(group):
+                rows = slice(r, n)
+                put(rows, cols(g * group + h), turned_back(rows, jnp.transpose(dq[:, h * Q_BLOCK:(h + 1) * Q_BLOCK])))
+
+        rows = slice(0, seq_len)
+        put(rows, kc, turned_back(rows, dk_ref[...]))
+        put(rows, vc, dv_ref[...])
 
 
 def attend(z, cos_t, sin_t, batch, heads, kv_heads):
@@ -145,6 +160,7 @@
         in_specs=[pl.BlockSpec((seq_len, width), row), pl.BlockSpec((seq_len, HEAD_DIM), row), pl.BlockSpec((seq_len, HEAD_DIM), row)],
         out_specs=[pl.BlockSpec((seq_len, width), row), pl.BlockSpec((seq_len, heads * HEAD_DIM), row)],
         out_shape=[jax.ShapeDtypeStruct((tokens, width), BF16), jax.ShapeDtypeStruct((tokens, heads * HEAD_DIM), BF16)],
+        scratch_shapes=[pltpu.VMEM((heads // kv_heads * Q_BLOCK, seq_len), F32), pltpu.VMEM((heads // kv_heads * Q_BLOCK, seq_len), BF16)],
         compiler_params=pltpu.CompilerParams(dimension_semantics=("arbitrary",), vmem_limit_bytes=48 * 2 ** 20),
         cost_estimate=pl.CostEstimate(flops=3 * flops, bytes_accessed=tokens * width * 8, transcendentals=tokens * seq_len * heads),
         name="attend",
@@ -162,7 +178,7 @@
         in_specs=[pl.BlockSpec((seq_len, width), row), pl.BlockSpec((seq_len, heads * HEAD_DIM), row), pl.BlockSpec((seq_len, HEAD_DIM), row), pl.BlockSpec((seq_len, HEAD_DIM), row)],
         out_specs=[pl.BlockSpec((seq_len, width), row), pl.BlockSpec((1, width), lambda b: (0, 0))],
         out_shape=[jax.ShapeDtypeStruct((tokens, width), BF16), jax.ShapeDtypeStruct((1, width), F32)],
-        scratch_shapes=[pltpu.VMEM((seq_len, HEAD_DIM), F32), pltpu.VMEM((seq_len, HEAD_DIM), F32)],
+        scratch_shapes=[pltpu.VMEM((seq_len, HEAD_DIM), F32)] * 2 + [pltpu.VMEM((seq_len, heads // kv_heads * Q_BLOCK), F32)] * 2 + [pltpu.VMEM((seq_len, heads // kv_heads * Q_BLOCK), BF16)] * 2,
         compiler_params=pltpu.CompilerParams(dimension_semantics=("arbitrary",), vmem_limit_bytes=48 * 2 ** 20),
         cost_estimate=pl.CostEstimate(flops=3 * flops, bytes_accessed=tokens * width * 8, transcendentals=tokens * seq_len * heads),
         name="attend_back",
@@ -332,10 +348,6 @@
     def scatter_rows(full):
         return lax.psum_scatter(full, ax, scatter_dimension=0, tiled=True)
 
-    def spread(v):
-        v2 = hop(v, 2)
-        return [v, hop(v, 1), v2, hop(v2, 1)]
-
     def joined(parts):
         rows, cols = parts[0].shape
         out = jnp.zeros((group * rows, cols), parts[0].dtype)
@@ -370,6 +382,7 @@
         bias = small[:, h_loc:h_loc + q_loc].reshape(1, n_dev * q_loc).astype(F32)
         gain_two = small[:, h_loc + q_loc:].reshape(1, width).astype(F32)
 
+        wqkv, up_part[2], up_part[3] = after(wqkv, up_part[2], up_part[3])
         up_near = [up_part[0]] + [hop(up_part[k], k) for k in (1, 2, 3)]
         up_far = [hop(v, group) for v in up_near]
         down_far = hop(w_down, group)
@@ -390,19 +403,19 @@
         mid_wide = mid.astype(F32)
         inv_two = norm_scale(mid_wide)
         mlp_in = (mid_wide * inv_two * gain_two).astype(BF16)
-        m_parts = spread(mlp_in)
-
         w_all = jnp.zeros((width, 2 * f_pad), BF16)
         for k in range(group):
             w_all = lax.dynamic_update_slice(w_all, up_near[k], ((me ^ k) * h_loc, 0))
-        m_all = joined(m_parts[:2])
+        for k in (0, 1, 2):
+            w_all = lax.dynamic_update_slice(w_all, up_far[k], ((me ^ group ^ k) * h_loc, 0))
+        m_all = joined([mlp_in, hop(mlp_in, 1)])
         dy_all = joined(dy_parts[:2])
         wd_all = lax.dynamic_update_slice(jnp.zeros((f_pad, width), BF16), w_down, (side * f_loc, 0))
-        m_all, dy_all, w_all, wd_all, up_far[2] = after(m_all, dy_all, w_all, wd_all, up_far[2])
-        for k in range(group):
-            w_all = lax.dynamic_update_slice(w_all, up_far[k], ((me ^ group ^ k) * h_loc, 0))
-        for k in (2, 3):
-            m_all = lax.dynamic_update_slice(m_all, m_parts[k], (k * tokens, 0))
+        m_far = hop(mlp_in, 2)
+        m_all, dy_all, w_all, wd_all, m_far = after(m_all, dy_all, w_all, wd_all, m_far)
+        w_all = lax.dynamic_update_slice(w_all, up_far[3], ((me ^ group ^ 3) * h_loc, 0))
+        m_all = lax.dynamic_update_slice(m_all, m_far, (2 * tokens, 0))
+        m_all = lax.dynamic_update_slice(m_all, hop(m_far, 1), (3 * tokens, 0))
 
         gate_low, lin_low, act = up_act(m_all, w_all)
         act, dy_far, down_far, dy_all = after(act, dy_parts[2], down_far, dy_all)
@@ -443,11 +456,9 @@
         dm3 = block(d_up, 3, w_all, NT_DIMS)
         d_up, dm3 = after(d_up, dm3)
         dm3 = hop(dm3, 1)
-        dm1 = block(d_up, 1, w_all, NT_DIMS)
-        d_up, dm1 = after(d_up, dm1)
-        dm1 = hop(dm1, 1)
-        dm2 = block(d_up, 2, w_all, NT_DIMS) + dm3
+        dm2 = block(d_up, 2, w_all, NT_DIMS)
         d_up, dm2 = after(d_up, dm2)
+        d_up, dm2 = after(d_up, dm2 + dm3)
         dm2 = hop(dm2, 2)
 
         far_a = up_grad(m_all, d_up, chip ^ 3)
@@ -459,6 +470,9 @@
         y1 = block(act, 1, wd_all, NN_DIMS)
         act, d_up, y1 = after(act, d_up, y1)
         y1 = hop(y1, 1)
+        dm1 = block(d_up, 1, w_all, NT_DIMS)
+        d_up, dm1 = after(d_up, dm1)
+        dm1 = hop(dm1, 1)
         dm0 = block(d_up, 0, w_all, NT_DIMS)
         d_up, dm0, act = after(d_up, dm0, act)
         y0 = block(act, 0, wd_all, NN_DIMS)
@@ -489,15 +503,21 @@
         d_normed, d_up = after(d_normed, d_up)
         near_b = up_grad(m_all, d_up, chip)
         near_b, d_normed = after(near_b, d_normed)
+        grad_attn_gain = jnp.sum(d_normed * hid_wide * inv_one, axis=0)
+        small_grads = jnp.concatenate([grad_attn_gain.reshape(n_dev, h_loc), grad_b_qkv.reshape(n_dev, q_loc), grad_mlp_gain.reshape(n_dev, h_loc)], axis=1)
+        for k in (1, 2, group):
+            pair = small_grads.reshape(n_dev // 2, 2, -1) if k == 1 else small_grads.reshape(-1, 2, h_loc + q_loc + h_loc)
+            mine = lax.div(me, k) % 2
+            small_grads = lax.dynamic_index_in_dim(pair, mine, 1, keepdims=False) + hop(lax.dynamic_index_in_dim(pair, 1 - mine, 1, keepdims=False), k)
+        small_grads = small_grads.reshape(-1)
+        scaled_one = d_normed * gain_one
+        grad_hidden = (d_mid + inv_one * (scaled_one - hid_wide * inv_one * inv_one * jnp.mean(scaled_one * hid_wide, axis=-1, keepdims=True))).astype(BF16)
+        y0, y1, y2, mid_late, grad_hidden = after(y0, y1, y2, mid, grad_hidden)
+        output = (mid_late.astype(F32) + (y0 + y1 + y2)).astype(BF16)
+        far_b, output, grad_hidden, grad_w_down = after(far_b, output, grad_hidden, grad_w_down)
         piece0 = rows_of(core, near_b, far_b)
         piece1 = hop(rows_of(1 - core, near_b, far_b), 1)
         grad_w_up = join_up([piece0, piece1, piece2, piece3], rank, group, f_loc)
-        y0, y1, y2, mid_late, d_normed = after(y0, y1, y2, mid, d_normed)
-        output = (mid_late.astype(F32) + (y0 + y1 + y2)).astype(BF16)
-        grad_attn_gain = jnp.sum(d_normed * hid_wide * inv_one, axis=0)
-        scaled_one = d_normed * gain_one
-        grad_hidden = (d_mid + inv_one * (scaled_one - hid_wide * inv_one * inv_one * jnp.mean(scaled_one * hid_wide, axis=-1, keepdims=True))).astype(BF16)
-        small_grads = scatter_rows(jnp.concatenate([grad_attn_gain.reshape(n_dev, h_loc), grad_b_qkv.reshape(n_dev, q_loc), grad_mlp_gain.reshape(n_dev, h_loc)], axis=1)).reshape(-1)
         return (output.reshape(hidden.shape), grad_hidden.reshape(hidden.shape), small_grads[:h_loc], grad_w_qkv, small_grads[h_loc:h_loc + q_loc], grad_w_out, small_grads[h_loc + q_loc:], grad_w_up, grad_w_down)
 
     row_spec = P(ax)

time: 2790 us -> 2620 us (0.939)
  waiting for transfers between devices: 1260 us -> 1150 us
  Pallas kernels: 508 us -> 456 us
  blocking collectives: 31.7 us -> 0 us
    ppermute x30 -> x33, waiting for transfers between devices: 1230 us -> 1130 us  [hop(): return lax.ppermute(v, ax, [(i, i ^ k) for i in range(n_dev)])]
    pallas_call x1, Pallas kernels: 109 us -> 71.6 us  [attend_back(): pl.pallas_call(functools.partial(attend_back_kernel, heads, kv_heads), gr...]
    unnamed x1 -> x0, blocking collectives: 31.7 us -> none
  transfers between devices with their start and end apart: 34 -> 37, of which waited for: 13 -> 15; matrix products, arithmetic and copies ran while one was open for 26% -> 23% of each run, Pallas kernels for 14% -> 13%
where the time goes in v2:
time: 2620 us
  waiting for transfers between devices  1150 us (44%)
  matrix products  687 us (26%)
  Pallas kernels  456 us (17%)
  other arithmetic  157 us (6%)
  local copies, waits for them, and re-layouts  130 us (5%)
    ppermute x33, waiting for transfers between devices, hop(): return lax.ppermute(v, ax, [(i, i ^ k) for i in range(n_dev)])  1130 us
    dot_general x20, matrix products, mm(): return lax.dot_general(a, b, dims, preferred_element_type=F32)  687 us
    pallas_call x1, Pallas kernels, up_act(): pl.pallas_call(up_kernel, grid=(tokens // T_BLOCK,), in_specs=[pl.BlockSp...  169 us
    pallas_call x1, Pallas kernels, up_back(): pl.pallas_call(up_back_kernel, grid=(tokens // T_BLOCK,), in_specs=[pl.Bl...  112 us
    pallas_call x1, Pallas kernels, attend_back(): pl.pallas_call(functools.partial(attend_back_kernel, heads, kv_heads), gr...  71.6 us
    pallas_call x1, Pallas kernels, attend(): pl.pallas_call(functools.partial(attend_kernel, heads, kv_heads), grid=(b...  68.8 us
  transfers between devices with their start and end apart: 37, of which 15 were waited for; matrix products, arithmetic and copies ran while one was open for 23% of the time, Pallas kernels for 13%

profile of v2, /device:TPU:0, one launch (start us, length us, event | category | flops | bytes accessed | tf_op | source)
XLA Modules:
  0.0 2616.3 jit_solution(13194974121981916097)
XLA Ops:
  25.0 13.4 split_up.1
  39.1 14.8 dynamic_update_slice.56
  58.1 12.2 all-gather.3.cloned.1.call-done
  71.9 22.4 convolution_add_fusion.z_ref
  94.3 68.8 %attend.1 = (bf16[1536,2560]{1,0:T(8,128)(2,1)}, bf16[1536,2048]{1,0:T(8,128)(2,1)}) custom-call(f32[1536,2560]{1,0:T(8,128)} %convolution_add_fusion.z_ref, f32[1536,128]{1,0:T(8,128)S(1)} %get-tuple-element.183.cos_ref, f32[1536,128]{1,0:T(8,128)S(1)} %get-tuple-element.182.sin_ref), custom_call_target="tpu_custom_call" | custom-call | flops 19327352832 | bytes 31457280 | tf_op jit(solution)/shard_map/attend/pallas_call | solution.py:157
  163.1 19.1 fusion.15
  219.6 18.6 dynamic_update_slice.54
  245.8 27.3 %collective-permute-done.8 = bf16[256,5632]{1,0:T(8,128)(2,1)S(1)} collective-permute-done((bf16[256,5632]{1,0:T(8,128)(2,1)}, bf16[256,5632]{1,0:T(8,128)(2,1)S(1)}, u32[]{:S(2)}, u32[]{:S(2)}) %collective-permute-start.8) | collective-permute-done | bytes 2883616 | tf_op jit(solution)/shard_map/ppermute | solution.py:343
  274.8 60.1 %collective-permute-done.9 = bf16[256,5632]{1,0:T(8,128)(2,1)S(1)} collective-permute-done((bf16[256,5632]{1,0:T(8,128)(2,1)}, bf16[256,5632]{1,0:T(8,128)(2,1)S(1)}, u32[]{:S(2)}, u32[]{:S(2)}) %collective-permute-start.9) | collective-permute-done | bytes 2883616 | tf_op jit(solution)/shard_map/ppermute | solution.py:343
  336.6 59.3 %collective-permute-done.10 = bf16[256,5632]{1,0:T(8,128)(2,1)S(1)} collective-permute-done((bf16[256,5632]{1,0:T(8,128)(2,1)}, bf16[256,5632]{1,0:T(8,128)(2,1)S(1)}, u32[]{:S(2)}, u32[]{:S(2)}) %collective-permute-start.10) | collective-permute-done | bytes 2883616 | tf_op jit(solution)/shard_map/ppermute | solution.py:343
  413.3 56.5 %collective-permute-done.13 = bf16[256,5632]{1,0:T(8,128)(2,1)} collective-permute-done((bf16[256,5632]{1,0:T(8,128)(2,1)}, bf16[256,5632]{1,0:T(8,128)(2,1)}, u32[]{:S(2)}, u32[]{:S(2)}) %collective-permute-start.13) | collective-permute-done | bytes 2883616 | tf_op jit(solution)/shard_map/ppermute | solution.py:343
  479.9 169.0 %up_act.1 = (bf16[6144,2816]{1,0:T(8,128)(2,1)}, bf16[6144,2816]{1,0:T(8,128)(2,1)}, bf16[6144,2816]{1,0:T(8,128)(2,1)}) custom-call(bf16[6144,2048]{1,0:T(8,128)(2,1)} %constant_dynamic-update-slice_fusion.4.m_ref, bf16[2048,5632]{1,0:T(8,128)(2,1)} %constant_dynamic-update-slice_fusion.3.w_ref), custom_call_target="tpu_custom_call" | custom-call | flops 141733920768 | bytes 152043520 | tf_op jit(solution)/shard_map/up_act/pallas_call | solution.py:204
  654.9 24.9 fusion.41
  686.8 21.4 collective-permute-done.16
  711.5 44.8 %fusion.21 = f32[2816,1024]{1,0:T(8,128)} fusion(bf16[6144,2816]{1,0:T(8,128)(2,1)} %get-tuple-element.135, bf16[6144,2048]{1,0:T(8,128)(2,1)} %constant_dynamic-update-slice_fusion.1.dy_ref), kind=kOutput, calls=%fused_computation.26 | convolution fusion | flops 35433480192 | bytes 58720256 | tf_op jit(solution)/shard_map/dot_general | solution.py:32
  756.2 25.7 convolution_add_fusion.1
  781.9 45.0 %fusion.19 = f32[2816,1024]{1,0:T(8,128)} fusion(bf16[6144,2816]{1,0:T(8,128)(2,1)} %get-tuple-element.135, bf16[6144,2048]{1,0:T(8,128)(2,1)} %constant_dynamic-update-slice_fusion.1.dy_ref), kind=kOutput, calls=%fused_computation.24 | convolution fusion | flops 35433480192 | bytes 58720256 | tf_op jit(solution)/shard_map/dot_general | solution.py:32
  826.9 112.0 %up_back.1 = bf16[6144,5632]{1,0:T(8,128)(2,1)} custom-call(bf16[6144,2048]{1,0:T(8,128)(2,1)} %constant_dynamic-update-slice_fusion.1.dy_ref, bf16[2816,2048]{1,0:T(8,128)(2,1)} %constant_dynamic-update-slice_fusion.wd_ref, bf16[6144,2816]{1,0:T(8,128)(2,1)} %get-tuple-element.119.g_ref, bf16[6144,2816]{1,0:T(8,128)(2,1)} %get-tuple-element.120.l_ref), custom_call_target="tpu_custom_call" | custom-call | flops 70866960384 | bytes 175112192 | tf_op jit(solution)/shard_map/up_back/pallas_call | solution.py:232
  938.9 44.9 %fusion = f32[1536,2048]{1,0:T(8,128)} fusion(bf16[2048,5632]{1,0:T(8,128)(2,1)} %constant_dynamic-update-slice_fusion.3.w_ref, bf16[6144,5632]{1,0:T(8,128)(2,1)} %up_back.1), kind=kOutput, calls=%fused_computation.4 | convolution fusion | flops 35433480192 | bytes 52953088 | tf_op jit(solution)/shard_map/dot_general | solution.py:32
  984.0 44.8 %fusion.6 = f32[1536,2048]{1,0:T(8,128)} fusion(bf16[2048,5632]{1,0:T(8,128)(2,1)} %constant_dynamic-update-slice_fusion.3.w_ref, bf16[6144,5632]{1,0:T(8,128)(2,1)} %up_back.1), kind=kOutput, calls=%fused_computation.10 | convolution fusion | flops 35433480192 | bytes 52953088 | tf_op jit(solution)/shard_map/dot_general | solution.py:32
  1028.8 14.4 add.213
  1043.2 47.0 %fusion.49 = f32[512,5632]{1,0:T(8,128)} fusion(bf16[6144,5632]{1,0:T(8,128)(2,1)} %up_back.1, bf16[6144,2048]{1,0:T(8,128)(2,1)} %constant_dynamic-update-slice_fusion.4.m_ref, s32[]{:T(128)S(6)} %select_n.163), kind=kOutput, calls=%fused_computation.64 | convolution fusion | flops 35433480192 | bytes 87031808 | tf_op jit(solution)/shard_map/dot_general | solution.py:32
  1090.2 46.7 %fusion.47 = f32[512,5632]{1,0:T(8,128)} fusion(bf16[6144,5632]{1,0:T(8,128)(2,1)} %up_back.1, bf16[6144,2048]{1,0:T(8,128)(2,1)} %constant_dynamic-update-slice_fusion.4.m_ref, s32[]{:T(128)S(6)} %select_n.164), kind=kOutput, calls=%fused_computation.62 | convolution fusion | flops 35433480192 | bytes 87031808 | tf_op jit(solution)/shard_map/dot_general | solution.py:32
  1136.9 24.9 fusion.38
  1161.8 44.6 %fusion.4 = f32[1536,2048]{1,0:T(8,128)} fusion(bf16[2048,5632]{1,0:T(8,128)(2,1)} %constant_dynamic-update-slice_fusion.3.w_ref, bf16[6144,5632]{1,0:T(8,128)(2,1)} %up_back.1), kind=kOutput, calls=%fused_computation.8 | convolution fusion | flops 35433480192 | bytes 52953088 | tf_op jit(solution)/shard_map/dot_general | solution.py:32
  1207.3 45.1 %fusion.2 = f32[1536,2048]{1,0:T(8,128)} fusion(bf16[2048,5632]{1,0:T(8,128)(2,1)} %constant_dynamic-update-slice_fusion.3.w_ref, bf16[6144,5632]{1,0:T(8,128)(2,1)} %up_back.1), kind=kOutput, calls=%fused_computation.6 | convolution fusion | flops 35433480192 | bytes 52953088 | tf_op jit(solution)/shard_map/dot_general | solution.py:32
  1252.4 24.7 fusion.36
  1277.1 46.8 %fusion.45 = f32[512,5632]{1,0:T(8,128)} fusion(bf16[6144,5632]{1,0:T(8,128)(2,1)} %up_back.1, bf16[6144,2048]{1,0:T(8,128)(2,1)} %constant_dynamic-update-slice_fusion.4.m_ref, s32[]{:T(128)S(6)} %select_n.165), kind=kOutput, calls=%fused_computation.60 | convolution fusion | flops 35433480192 | bytes 87031808 | tf_op jit(solution)/shard_map/dot_general | solution.py:32
  1323.9 155.6 %collective-permute-done.23 = f32[1536,2048]{1,0:T(8,128)} collective-permute-done((f32[1536,2048]{1,0:T(8,128)}, f32[1536,2048]{1,0:T(8,128)}, u32[]{:S(2)}, u32[]{:S(2)}) %collective-permute-start.23) | collective-permute-done | bytes 12582944 | tf_op jit(solution)/shard_map/ppermute | solution.py:343
  1479.5 21.4 fusion.18
  1500.9 12.4 fusion.14
  1513.2 21.4 fusion.51
  1535.4 22.1 convolution_convert_fusion.dctx_ref
  1557.5 71.6 %attend_back.1 = (bf16[1536,2560]{1,0:T(8,128)(2,1)}, f32[1,2560]{1,0:T(1,128)S(1)}) custom-call(bf16[1536,2560]{1,0:T(8,128)(2,1)} %get-tuple-element.144.qkv_ref, bf16[1536,2048]{1,0:T(8,128)(2,1)} %convolution_convert_fusion.dctx_ref, f32[1536,128]{1,0:T(8,128)S(1)} %get-tuple-element.183.cos_ref, f32[1536,128]{1,0:T(8,128)S(1)} %get-tuple-element.182.sin_ref), custom_call_target="tpu_custom_call" | custom-call | flops 48318382080 | bytes 31457280 | tf_op jit(solution)/shard_map/attend_back/pallas_call | solution.py:175
  1629.1 22.3 fusion.66
  1665.6 392.7 %collective-permute-done.24 = f32[1376,1024]{1,0:T(8,128)} collective-permute-done((f32[1376,1024]{1,0:T(8,128)}, f32[1376,1024]{1,0:T(8,128)}, u32[]{:S(2)}, u32[]{:S(2)}) %collective-permute-start.24) | collective-permute-done | bytes 5636128 | tf_op jit(solution)/shard_map/ppermute | solution.py:343
  2067.4 109.9 %collective-permute-done.25 = f32[1376,1024]{1,0:T(8,128)} collective-permute-done((f32[1376,1024]{1,0:T(8,128)}, f32[1376,1024]{1,0:T(8,128)}, u32[]{:S(2)}, u32[]{:S(2)}) %collective-permute-start.25) | collective-permute-done | bytes 5636128 | tf_op jit(solution)/shard_map/ppermute | solution.py:343
  2186.0 10.5 pad_maximum_fusion
  2197.1 12.9 dynamic-slice_add_fusion
  2211.8 22.9 fusion.67
  2234.7 46.9 %fusion.43 = f32[512,5632]{1,0:T(8,128)} fusion(bf16[6144,5632]{1,0:T(8,128)(2,1)} %up_back.1, bf16[6144,2048]{1,0:T(8,128)(2,1)} %constant_dynamic-update-slice_fusion.4.m_ref, s32[]{:T(128)S(6)} %select_n.166), kind=kOutput, calls=%fused_computation.58 | convolution fusion | flops 35433480192 | bytes 87031808 | tf_op jit(solution)/shard_map/dot_general | solution.py:32
  2290.6 14.6 fusion.30
  2305.2 35.2 %collective-permute-done.21 = f32[1536,2048]{1,0:T(8,128)} collective-permute-done((f32[1536,2048]{1,0:T(8,128)}, f32[1536,2048]{1,0:T(8,128)}, u32[]{:S(2)}, u32[]{:S(2)}) %collective-permute-start.21) | collective-permute-done | bytes 12582944 | tf_op jit(solution)/shard_map/ppermute | solution.py:343
  2340.4 16.6 add_convert_fusion
  2357.0 90.1 %collective-permute-done.19 = f32[512,5632]{1,0:T(8,128)} collective-permute-done((f32[512,5632]{1,0:T(8,128)}, f32[512,5632]{1,0:T(8,128)}, u32[]{:S(2)}, u32[]{:S(2)}) %collective-permute-start.19) | collective-permute-done | bytes 11534368 | tf_op jit(solution)/shard_map/ppermute | solution.py:343
  2447.1 12.9 dynamic-slice_add_fusion.2
  2470.3 113.2 %collective-permute-done.27 = f32[2,832]{1,0:T(2,128)S(1)} collective-permute-done((f32[2,832]{1,0:T(2,128)S(1)}, f32[2,832]{1,0:T(2,128)S(1)}, u32[]{:S(2)}, u32[]{:S(2)}) %collective-permute-start.27) | collective-permute-done | bytes 6688 | tf_op jit(solution)/shard_map/ppermute | solution.py:343
  2588.3 21.0 join_up.1
  (169 shorter events, 176.8 us)
Async XLA Ops:
  7.2 63.2 %all-gather.3.cloned.1.call-start = ((), (), s32[]{:S(2)}) async-start(), calls=%async_computation.2 | async-start | bytes 11796480 | tf_op jit(solution)/shard_map/all_gather | solution.py:346
  7.9 155.2 %all-gather.5.cloned.1.call-start = ((), (), s32[]{:S(2)}) async-start(), calls=%async_computation.3 | async-start | bytes 9437184 | tf_op jit(solution)/shard_map/all_gather | solution.py:346
  8.7 2600.7 %reduce-scatter.5.cloned.1.call-start = ((), (), s32[]{:S(2)}) async-start(), calls=%async_computation.5 | async-start | bytes 18874368 | tf_op jit(solution)/shard_map/reduce_scatter | solution.py:349
  9.5 8.8 collective-permute-start
  18.3 4.6 collective-permute-start.1
  22.9 15.4 collective-permute-start.2
  38.5 143.8 %copy-start.8 = (f32[1,2,8,128]{3,1,2,0:T(2,128)}, f32[1,2,8,128]{3,1,2,0:T(2,128)S(1)}, u32[]{:S(2)}) copy-start(f32[1,2,8,128]{3,1,2,0:T(2,128)S(1)} %copy.24) | copy-start | bytes 24580
  38.6 155.6 %collective-permute-start.5 = (bf16[256,5632]{1,0:T(8,128)(2,1)}, bf16[256,5632]{1,0:T(8,128)(2,1)}, u32[]{:S(2)}, u32[]{:S(2)}) collective-permute-start(bf16[256,5632]{1,0:T(8,128)(2,1)} %get-tuple-element.99), channel_id=1, source_target_pairs={{0,1},{1,0},{2,3},{3,2},{4,5},{5,4},{6,7},{7,6}} | collective-permute-start | bytes 8650760 | tf_op jit(solution)/shard_map/ppermute | solution.py:343
  38.6 168.8 %collective-permute-start.4 = (bf16[1536,2048]{1,0:T(8,128)(2,1)}, bf16[1536,2048]{1,0:T(8,128)(2,1)}, u32[]{:S(2)}, u32[]{:S(2)}) collective-permute-start(bf16[1536,2048]{1,0:T(8,128)(2,1)} %bitcast.80), channel_id=1, source_target_pairs={{0,1},{1,0},{2,3},{3,2},{4,5},{5,4},{6,7},{7,6}} | collective-permute-start | bytes 18874376 | tf_op jit(solution)/shard_map/ppermute | solution.py:343
  70.3 141.1 %collective-permute-start.6 = (bf16[256,5632]{1,0:T(8,128)(2,1)}, bf16[256,5632]{1,0:T(8,128)(2,1)}, u32[]{:S(2)}, u32[]{:S(2)}) collective-permute-start(bf16[256,5632]{1,0:T(8,128)(2,1)} %get-tuple-element.100), channel_id=1, source_target_pairs={{0,2},{1,3},{2,0},{3,1},{4,6},{5,7},{6,4},{7,5}} | collective-permute-start | bytes 8650760 | tf_op jit(solution)/shard_map/ppermute | solution.py:343
  71.8 166.3 %collective-permute-start.7 = (bf16[256,5632]{1,0:T(8,128)(2,1)}, bf16[256,5632]{1,0:T(8,128)(2,1)}, u32[]{:S(2)}, u32[]{:S(2)}) collective-permute-start(bf16[256,5632]{1,0:T(8,128)(2,1)} %get-tuple-element.101), channel_id=1, source_target_pairs={{0,3},{1,2},{2,1},{3,0},{4,7},{5,6},{6,5},{7,4}} | collective-permute-start | bytes 8650760 | tf_op jit(solution)/shard_map/ppermute | solution.py:343
  183.8 213.7 %collective-permute-start.3 = (bf16[1536,2048]{1,0:T(8,128)(2,1)S(1)}, bf16[1536,2048]{1,0:T(8,128)(2,1)}, u32[]{:S(2)}, u32[]{:S(2)}) collective-permute-start(bf16[1536,2048]{1,0:T(8,128)(2,1)S(1)} %fusion.10), channel_id=1, source_target_pairs={{0,1},{1,0},{2,3},{3,2},{4,5},{5,4},{6,7},{7,6}} | collective-permute-start | bytes 18874376 | tf_op jit(solution)/shard_map/ppermute | solution.py:343
  194.1 210.0 %collective-permute-start.11 = (bf16[1536,2048]{1,0:T(8,128)(2,1)S(1)}, bf16[1536,2048]{1,0:T(8,128)(2,1)}, u32[]{:S(2)}, u32[]{:S(2)}) collective-permute-start(bf16[1536,2048]{1,0:T(8,128)(2,1)S(1)} %fusion.10), channel_id=1, source_target_pairs={{0,2},{1,3},{2,0},{3,1},{4,6},{5,7},{6,4},{7,5}} | collective-permute-start | bytes 18874376 | tf_op jit(solution)/shard_map/ppermute | solution.py:343
  207.5 65.6 %collective-permute-start.8 = (bf16[256,5632]{1,0:T(8,128)(2,1)}, bf16[256,5632]{1,0:T(8,128)(2,1)S(1)}, u32[]{:S(2)}, u32[]{:S(2)}) collective-permute-start(bf16[256,5632]{1,0:T(8,128)(2,1)} %get-tuple-element.98), channel_id=1, source_target_pairs={{0,4},{1,5},{2,6},{3,7},{4,0},{5,1},{6,2},{7,3}} | collective-permute-start | bytes 8650760 | tf_op jit(solution)/shard_map/ppermute | solution.py:343
  211.4 123.4 %collective-permute-start.9 = (bf16[256,5632]{1,0:T(8,128)(2,1)}, bf16[256,5632]{1,0:T(8,128)(2,1)S(1)}, u32[]{:S(2)}, u32[]{:S(2)}) collective-permute-start(bf16[256,5632]{1,0:T(8,128)(2,1)} %collective-permute-done.5), channel_id=1, source_target_pairs={{0,4},{1,5},{2,6},{3,7},{4,0},{5,1},{6,2},{7,3}} | collective-permute-start | bytes 8650760 | tf_op jit(solution)/shard_map/ppermute | solution.py:343
  238.1 157.7 %collective-permute-start.10 = (bf16[256,5632]{1,0:T(8,128)(2,1)}, bf16[256,5632]{1,0:T(8,128)(2,1)S(1)}, u32[]{:S(2)}, u32[]{:S(2)}) collective-permute-start(bf16[256,5632]{1,0:T(8,128)(2,1)} %collective-permute-done.6), channel_id=1, source_target_pairs={{0,4},{1,5},{2,6},{3,7},{4,0},{5,1},{6,2},{7,3}} | collective-permute-start | bytes 8650760 | tf_op jit(solution)/shard_map/ppermute | solution.py:343
  404.1 69.2 %collective-permute-start.12 = (bf16[1536,2048]{1,0:T(8,128)(2,1)}, bf16[1536,2048]{1,0:T(8,128)(2,1)}, u32[]{:S(2)}, u32[]{:S(2)}) collective-permute-start(bf16[1536,2048]{1,0:T(8,128)(2,1)} %collective-permute-done.11), channel_id=1, source_target_pairs={{0,1},{1,0},{2,3},{3,2},{4,5},{5,4},{6,7},{7,6}} | collective-permute-start | bytes 18874376 | tf_op jit(solution)/shard_map/ppermute | solution.py:343
  404.1 65.7 %collective-permute-start.13 = (bf16[256,5632]{1,0:T(8,128)(2,1)}, bf16[256,5632]{1,0:T(8,128)(2,1)}, u32[]{:S(2)}, u32[]{:S(2)}) collective-permute-start(bf16[256,5632]{1,0:T(8,128)(2,1)} %collective-permute-done.7), channel_id=1, source_target_pairs={{0,4},{1,5},{2,6},{3,7},{4,0},{5,1},{6,2},{7,3}} | collective-permute-start | bytes 8650760 | tf_op jit(solution)/shard_map/ppermute | solution.py:343
  404.7 244.3 %collective-permute-start.15 = (bf16[1376,2048]{1,0:T(8,128)(2,1)}, bf16[1376,2048]{1,0:T(8,128)(2,1)}, u32[]{:S(2)}, u32[]{:S(2)}) collective-permute-start(bf16[1376,2048]{1,0:T(8,128)(2,1)} %param.19), channel_id=1, source_target_pairs={{0,4},{1,5},{2,6},{3,7},{4,0},{5,1},{6,2},{7,3}} | collective-permute-start | bytes 16908296 | tf_op jit(solution)/shard_map/ppermute | solution.py:343
  406.2 242.8 %collective-permute-start.14 = (bf16[1536,2048]{1,0:T(8,128)(2,1)}, bf16[1536,2048]{1,0:T(8,128)(2,1)}, u32[]{:S(2)}, u32[]{:S(2)}) collective-permute-start(bf16[1536,2048]{1,0:T(8,128)(2,1)} %bitcast.82), channel_id=1, source_target_pairs={{0,2},{1,3},{2,0},{3,1},{4,6},{5,7},{6,4},{7,5}} | collective-permute-start | bytes 18874376 | tf_op jit(solution)/shard_map/ppermute | solution.py:343
  679.8 76.4 %collective-permute-start.17 = (f32[1536,2048]{1,0:T(8,128)}, f32[1536,2048]{1,0:T(8,128)}, u32[]{:S(2)}, u32[]{:S(2)}) collective-permute-start(f32[1536,2048]{1,0:T(8,128)} %fusion.41), channel_id=1, source_target_pairs={{0,1},{1,0},{2,3},{3,2},{4,5},{5,4},{6,7},{7,6}} | collective-permute-start | bytes 37748744 | tf_op jit(solution)/shard_map/ppermute | solution.py:343
  679.8 28.4 %collective-permute-start.16 = (bf16[1536,2048]{1,0:T(8,128)(2,1)}, bf16[1536,2048]{1,0:T(8,128)(2,1)S(1)}, u32[]{:S(2)}, u32[]{:S(2)}) collective-permute-start(bf16[1536,2048]{1,0:T(8,128)(2,1)} %collective-permute-done.14), channel_id=1, source_target_pairs={{0,1},{1,0},{2,3},{3,2},{4,5},{5,4},{6,7},{7,6}} | collective-permute-start | bytes 18874376 | tf_op jit(solution)/shard_map/ppermute | solution.py:343
  983.8 45.0 %collective-permute-start.18 = (f32[1536,2048]{1,0:T(8,128)}, f32[1536,2048]{1,0:T(8,128)}, u32[]{:S(2)}, u32[]{:S(2)}) collective-permute-start(f32[1536,2048]{1,0:T(8,128)} %fusion), channel_id=1, source_target_pairs={{0,1},{1,0},{2,3},{3,2},{4,5},{5,4},{6,7},{7,6}} | collective-permute-start | bytes 37748744 | tf_op jit(solution)/shard_map/ppermute | solution.py:343
  1206.4 273.1 %collective-permute-start.22 = (f32[1536,2048]{1,0:T(8,128)}, f32[1536,2048]{1,0:T(8,128)}, u32[]{:S(2)}, u32[]{:S(2)}) collective-permute-start(f32[1536,2048]{1,0:T(8,128)} %fusion.4), channel_id=1, source_target_pairs={{0,1},{1,0},{2,3},{3,2},{4,5},{5,4},{6,7},{7,6}} | collective-permute-start | bytes 37748744 | tf_op jit(solution)/shard_map/ppermute | solution.py:343
  1206.8 272.7 %collective-permute-start.23 = (f32[1536,2048]{1,0:T(8,128)}, f32[1536,2048]{1,0:T(8,128)}, u32[]{:S(2)}, u32[]{:S(2)}) collective-permute-start(f32[1536,2048]{1,0:T(8,128)} %add.213), channel_id=1, source_target_pairs={{0,2},{1,3},{2,0},{3,1},{4,6},{5,7},{6,4},{7,5}} | collective-permute-start | bytes 37748744 | tf_op jit(solution)/shard_map/ppermute | solution.py:343
  1277.1 202.4 %copy-start.9 = (f32[1,2,8,128]{3,1,2,0:T(2,128)S(1)}, f32[1,2,8,128]{3,1,2,0:T(2,128)}, u32[]{:S(2)}) copy-start(f32[1,2,8,128]{3,1,2,0:T(2,128)} %copy-done.8) | copy-start | bytes 24580
  1277.1 202.4 %copy-start.11 = (f32[1536]{0:T(1024)S(1)}, f32[1536]{0:T(1024)}, u32[]{:S(2)}) copy-start(f32[1536]{0:T(1024)} %copy-done.10) | copy-start | bytes 18436
  1323.9 177.0 %copy-start.1 = (bf16[1536,2048]{1,0:T(8,128)(2,1)S(1)}, bf16[1536,2048]{1,0:T(8,128)(2,1)}, u32[]{:S(2)}) copy-start(bf16[1536,2048]{1,0:T(8,128)(2,1)} %copy-done) | copy-start | bytes 18874372
  1323.9 177.0 %copy-start.2 = (bf16[3,512,2048]{2,1,0:T(8,128)(2,1)S(1)}, bf16[3,512,2048]{2,1,0:T(8,128)(2,1)}, u32[]{:S(2)}) copy-start(bf16[3,512,2048]{2,1,0:T(8,128)(2,1)} %param.12) | copy-start | bytes 18874372
  1534.6 1074.7 %reduce-scatter.3.cloned.1.call-start = ((), (), s32[]{:S(2)}) async-start(), calls=%async_computation.4 | async-start | bytes 23592960 | tf_op jit(solution)/shard_map/reduce_scatter | solution.py:349
  1534.7 662.4 %collective-permute-start.30 = (f32[512,5632]{1,0:T(8,128)}, f32[512,5632]{1,0:T(8,128)}, u32[]{:S(2)}, u32[]{:S(2)}) collective-permute-start(f32[512,5632]{1,0:T(8,128)} %fusion.49), channel_id=1, source_target_pairs={{0,4},{1,5},{2,6},{3,7},{4,0},{5,1},{6,2},{7,3}} | collective-permute-start | bytes 34603016 | tf_op jit(solution)/shard_map/ppermute | solution.py:343
  1535.4 93.7 %slice-start.4 = ((s8[6291456]{0:T(1024)(128)(4,1)}), s8[2097152]{0:T(1024)(128)(4,1)S(1)}, s32[]{:S(2)}) async-start(s8[6291456]{0:T(1024)(128)(4,1)} %bitcast.85), calls=%async_computation.10 | async-start | bytes 4194304
  1557.5 71.6 %slice-start.5 = ((s8[6291456]{0:T(1024)(128)(4,1)}), s8[4194304]{0:T(1024)(128)(4,1)S(1)}, s32[]{:S(2)}) async-start(s8[6291456]{0:T(1024)(128)(4,1)} %bitcast.85), calls=%async_computation.11 | async-start | bytes 8388608
  1657.5 400.7 %collective-permute-start.24 = (f32[1376,1024]{1,0:T(8,128)}, f32[1376,1024]{1,0:T(8,128)}, u32[]{:S(2)}, u32[]{:S(2)}) collective-permute-start(f32[1376,1024]{1,0:T(8,128)} %constant_dynamic-slice_fusion.7), channel_id=1, source_target_pairs={{0,4},{1,5},{2,6},{3,7},{4,0},{5,1},{6,2},{7,3}} | collective-permute-start | bytes 16908296 | tf_op jit(solution)/shard_map/ppermute | solution.py:343
  1664.7 512.6 %collective-permute-start.25 = (f32[1376,1024]{1,0:T(8,128)}, f32[1376,1024]{1,0:T(8,128)}, u32[]{:S(2)}, u32[]{:S(2)}) collective-permute-start(f32[1376,1024]{1,0:T(8,128)} %constant_dynamic-slice_fusion.6), channel_id=1, source_target_pairs={{0,4},{1,5},{2,6},{3,7},{4,0},{5,1},{6,2},{7,3}} | collective-permute-start | bytes 16908296 | tf_op jit(solution)/shard_map/ppermute | solution.py:343
  2066.9 273.5 %collective-permute-start.21 = (f32[1536,2048]{1,0:T(8,128)}, f32[1536,2048]{1,0:T(8,128)}, u32[]{:S(2)}, u32[]{:S(2)}) collective-permute-start(f32[1536,2048]{1,0:T(8,128)} %convolution_add_fusion.1), channel_id=1, source_target_pairs={{0,2},{1,3},{2,0},{3,1},{4,6},{5,7},{6,4},{7,5}} | collective-permute-start | bytes 37748744 | tf_op jit(solution)/shard_map/ppermute | solution.py:343
  2186.0 154.4 %collective-permute-start.20 = (f32[1536,2048]{1,0:T(8,128)}, f32[1536,2048]{1,0:T(8,128)}, u32[]{:S(2)}, u32[]{:S(2)}) collective-permute-start(f32[1536,2048]{1,0:T(8,128)} %fusion.38), channel_id=1, source_target_pairs={{0,1},{1,0},{2,3},{3,2},{4,5},{5,4},{6,7},{7,6}} | collective-permute-start | bytes 37748744 | tf_op jit(solution)/shard_map/ppermute | solution.py:343
  2196.5 250.6 %collective-permute-start.19 = (f32[512,5632]{1,0:T(8,128)}, f32[512,5632]{1,0:T(8,128)}, u32[]{:S(2)}, u32[]{:S(2)}) collective-permute-start(f32[512,5632]{1,0:T(8,128)} %fusion.47), channel_id=1, source_target_pairs={{0,4},{1,5},{2,6},{3,7},{4,0},{5,1},{6,2},{7,3}} | collective-permute-start | bytes 34603016 | tf_op jit(solution)/shard_map/ppermute | solution.py:343
  2210.0 378.4 %collective-permute-start.32 = (f32[256,5632]{1,0:T(8,128)}, f32[256,5632]{1,0:T(8,128)}, u32[]{:S(2)}, u32[]{:S(2)}) collective-permute-start(f32[256,5632]{1,0:T(8,128)} %get-tuple-element.172), channel_id=1, source_target_pairs={{0,3},{1,2},{2,1},{3,0},{4,7},{5,6},{6,5},{7,4}} | collective-permute-start | bytes 17301512 | tf_op jit(solution)/shard_map/ppermute | solution.py:343
  2210.8 377.6 %collective-permute-start.31 = (f32[256,5632]{1,0:T(8,128)}, f32[256,5632]{1,0:T(8,128)}, u32[]{:S(2)}, u32[]{:S(2)}) collective-permute-start(f32[256,5632]{1,0:T(8,128)} %get-tuple-element.173), channel_id=1, source_target_pairs={{0,2},{1,3},{2,0},{3,1},{4,6},{5,7},{6,4},{7,5}} | collective-permute-start | bytes 17301512 | tf_op jit(solution)/shard_map/ppermute | solution.py:343
  2234.7 46.9 %copy-start.7 = (f32[1,2,8,128]{3,1,2,0:T(2,128)S(1)}, f32[1,2,8,128]{3,1,2,0:T(2,128)}, u32[]{:S(2)}) copy-start(f32[1,2,8,128]{3,1,2,0:T(2,128)} %copy-done.6) | copy-start | bytes 24580
  2281.6 58.8 %slice-start = ((s8[6291456]{0:T(1024)(128)(4,1)}), s8[4194304]{0:T(1024)(128)(4,1)S(1)}, s32[]{:S(2)}) async-start(s8[6291456]{0:T(1024)(128)(4,1)} %bitcast.76), calls=%async_computation.6 | async-start | bytes 8388608
  2290.6 49.8 %slice-start.1 = ((s8[6291456]{0:T(1024)(128)(4,1)}), s8[2097152]{0:T(1024)(128)(4,1)S(1)}, s32[]{:S(2)}) async-start(s8[6291456]{0:T(1024)(128)(4,1)} %bitcast.76), calls=%async_computation.7 | async-start | bytes 4194304
  2357.0 103.0 %copy-start.12 = (f32[2048]{0:T(1024)S(1)}, f32[2048]{0:T(1024)}, u32[]{:S(2)}) copy-start(f32[2048]{0:T(1024)} %get-tuple-element.169) | copy-start | bytes 24580
  2460.0 128.4 %collective-permute-start.29 = (f32[256,5632]{1,0:T(8,128)}, f32[256,5632]{1,0:T(8,128)}, u32[]{:S(2)}, u32[]{:S(2)}) collective-permute-start(f32[256,5632]{1,0:T(8,128)} %get-tuple-element.174), channel_id=1, source_target_pairs={{0,1},{1,0},{2,3},{3,2},{4,5},{5,4},{6,7},{7,6}} | collective-permute-start | bytes 17301512 | tf_op jit(solution)/shard_map/ppermute | solution.py:343
  2460.2 9.5 collective-permute-start.26
  2469.8 113.7 %collective-permute-start.27 = (f32[2,832]{1,0:T(2,128)S(1)}, f32[2,832]{1,0:T(2,128)S(1)}, u32[]{:S(2)}, u32[]{:S(2)}) collective-permute-start(f32[2,832]{1,0:T(2,128)S(1)} %bitcast.94), channel_id=1, source_target_pairs={{0,2},{1,3},{2,0},{3,1},{4,6},{5,7},{6,4},{7,5}} | collective-permute-start | bytes 19976 | tf_op jit(solution)/shard_map/ppermute | solution.py:343
  2583.5 3.6 collective-permute-start.28
  (8 other events, 154.4 us)
Sparse Core Ops, SparseCore 0:
  9.8 60.5 all-gather.2
  72.2 82.1 all-gather.4
  1534.8 175.0 reduce-scatter.4
  1713.8 212.4 reduce-scatter.2

commit v3 on v2

--- a/solution.py
+++ b/solution.py
@@ -55,7 +55,8 @@
     return jnp.where(lane % 2 == 0, pltpu.roll(v, HEAD_DIM - 1, 1), pltpu.roll(v, 1, 1))
 
 
-def attend_kernel(heads, kv_heads, z_ref, cos_ref, sin_ref, qkv_ref, ctx_ref, s_ref, p_ref):
+def attend_kernel(heads, kv_heads, z_ref, cos_ref, sin_ref, qkv_ref, ctx_ref, *bufs):
+    s_refs, p_refs = bufs[:2], bufs[2:]
     seq_len = z_ref.shape[0]
     group = heads // kv_heads
     cos_t, sin_t = cos_ref[...], sin_ref[...]
@@ -63,7 +64,7 @@
     def cols(i):
         return pl.ds(pl.multiple_of(i * HEAD_DIM, HEAD_DIM), HEAD_DIM)
 
-    @pl.loop(0, heads + kv_heads)
+    @pl.loop(0, heads + kv_heads, unroll=3)
     def _(i):
         zh = z_ref[:, cols(i)]
         qkv_ref[:, cols(i)] = (zh * cos_t + swap_pairs(zh) * sin_t).astype(BF16)
@@ -76,9 +77,10 @@
         for r in range(0, seq_len, Q_BLOCK):
             n = r + Q_BLOCK
             q = jnp.concatenate([qkv_ref[r:n, cols(g * group + h)] for h in range(group)], axis=0)
+            s_ref, p_ref = s_refs[r // Q_BLOCK % 2], p_refs[r // Q_BLOCK % 2]
             s_ref[:, :n] = mm(q, qkv_ref[:n, kc], NT_DIMS)
 
-            @pl.loop(0, group * Q_BLOCK // S_BLOCK, unroll=2)
+            @pl.loop(0, group * Q_BLOCK // S_BLOCK, unroll=True)
             def _(c):
                 rows = pl.ds(pl.multiple_of(c * S_BLOCK, S_BLOCK), S_BLOCK)
                 s = s_ref[rows, :n]
@@ -124,7 +126,7 @@
             s_ref[:n] = mm(qkv_ref[:n, kc], q, NT_DIMS)
             dp_ref[:n] = mm(qkv_ref[:n, vc], d, NT_DIMS)
 
-            @pl.loop(0, group)
+            @pl.loop(0, group, unroll=True)
             def _(h):
                 c = cols(h)
                 s, dp = s_ref[:n, c], dp_ref[:n, c]
@@ -160,7 +162,7 @@
         in_specs=[pl.BlockSpec((seq_len, width), row), pl.BlockSpec((seq_len, HEAD_DIM), row), pl.BlockSpec((seq_len, HEAD_DIM), row)],
         out_specs=[pl.BlockSpec((seq_len, width), row), pl.BlockSpec((seq_len, heads * HEAD_DIM), row)],
         out_shape=[jax.ShapeDtypeStruct((tokens, width), BF16), jax.ShapeDtypeStruct((tokens, heads * HEAD_DIM), BF16)],
-        scratch_shapes=[pltpu.VMEM((heads // kv_heads * Q_BLOCK, seq_len), F32), pltpu.VMEM((heads // kv_heads * Q_BLOCK, seq_len), BF16)],
+        scratch_shapes=[pltpu.VMEM((heads // kv_heads * Q_BLOCK, seq_len), t) for t in (F32, F32, BF16, BF16)],
         compiler_params=pltpu.CompilerParams(dimension_semantics=("arbitrary",), vmem_limit_bytes=48 * 2 ** 20),
         cost_estimate=pl.CostEstimate(flops=3 * flops, bytes_accessed=tokens * width * 8, transcendentals=tokens * seq_len * heads),
         name="attend",
@@ -275,7 +277,7 @@
         def _():
             for q in range(group):
                 for h in range(2):
-                    segments = [(s * f_loc, f_loc, load, ((2 * h + s) * group + q) * f_loc, cols // LANES) for s in range(2)]
+                    segments = [(s * f_pad // 2, f_loc, load, ((2 * h + s) * group + q) * f_loc, cols // LANES) for s in range(2)]
                     for lo in range(0, f_pad, LANES):
                         out_refs[r ^ q][:, h * f_pad + lo:h * f_pad + lo + LANES] = gathered_tile(lo, segments, (rows, LANES)).astype(BF16)
 
@@ -310,7 +312,7 @@
                 return lambda t: ref[:, t * LANES:(t + 1) * LANES]
 
             for h in range(2):
-                segments = [(b * f_loc, f_loc, loader(parts[r ^ (b % group)]), h * f_pad + b // group * f_loc, 2 * f_pad // LANES) for b in range(2 * group)]
+                segments = [(b * f_loc, f_loc, loader(parts[r ^ (b % group)]), h * f_pad + b // group * f_pad // 2, 2 * f_pad // LANES) for b in range(2 * group)]
                 for lo in range(0, half, LANES):
                     out_ref[:, h * half + lo:h * half + lo + LANES] = gathered_tile(lo, segments, (rows, LANES))
 
@@ -361,8 +363,8 @@
         h_loc = w_up.shape[0]
         h_chip = 2 * h_loc
         f_loc = w_down.shape[0]
-        pad = -(2 * f_loc) % 256
-        f_pad = 2 * f_loc + pad
+        f_blk = f_loc + -f_loc % LANES
+        f_pad = 2 * f_blk
         q_loc = b_qkv.shape[0]
         me = lax.axis_index(ax)
         rank = lax.rem(me, group)
@@ -382,7 +384,6 @@
         bias = small[:, h_loc:h_loc + q_loc].reshape(1, n_dev * q_loc).astype(F32)
         gain_two = small[:, h_loc + q_loc:].reshape(1, width).astype(F32)
 
-        wqkv, up_part[2], up_part[3] = after(wqkv, up_part[2], up_part[3])
         up_near = [up_part[0]] + [hop(up_part[k], k) for k in (1, 2, 3)]
         up_far = [hop(v, group) for v in up_near]
         down_far = hop(w_down, group)
@@ -410,7 +411,7 @@
             w_all = lax.dynamic_update_slice(w_all, up_far[k], ((me ^ group ^ k) * h_loc, 0))
         m_all = joined([mlp_in, hop(mlp_in, 1)])
         dy_all = joined(dy_parts[:2])
-        wd_all = lax.dynamic_update_slice(jnp.zeros((f_pad, width), BF16), w_down, (side * f_loc, 0))
+        wd_all = lax.dynamic_update_slice(jnp.zeros((f_pad, width), BF16), w_down, (side * f_blk, 0))
         m_far = hop(mlp_in, 2)
         m_all, dy_all, w_all, wd_all, m_far = after(m_all, dy_all, w_all, wd_all, m_far)
         w_all = lax.dynamic_update_slice(w_all, up_far[3], ((me ^ group ^ 3) * h_loc, 0))
@@ -422,18 +423,13 @@
         dy_parts[2:] = [dy_far, hop(dy_far, 1)]
         for k in (2, 3):
             dy_all = lax.dynamic_update_slice(dy_all, dy_parts[k], (k * tokens, 0))
-        wd_all = lax.dynamic_update_slice(wd_all, down_far, ((1 - side) * f_loc, 0))
+        wd_all = lax.dynamic_update_slice(wd_all, down_far, ((1 - side) * f_blk, 0))
 
         def block(rows, k, w, dims):
             return mm(rows[k * tokens:(k + 1) * tokens], w, dims)
 
-        half = width // 2
-
-        def down_grad(a, j):
-            return mm(a, dy_all[:, j * half:(j + 1) * half], TN_DIMS)
-
-        def send_down(g_full):
-            return hop(lax.dynamic_slice(g_full, ((1 - side) * f_loc, 0), (f_loc, half)), group)
+        def down_grad(a, blk):
+            return mm(lax.dynamic_slice(a, (0, blk * f_blk), (group * tokens, f_blk)), dy_all, TN_DIMS)
 
         def up_grad(m, d_up, chip_id):
             cols = lax.dynamic_slice(m, (0, chip_id * h_chip), (group * tokens, h_chip))
@@ -442,17 +438,18 @@
         y3 = block(act, 3, wd_all, NN_DIMS)
         act, y3 = after(act, y3)
         y3 = hop(y3, 1)
-        dwd0 = down_grad(act, 0)
-        act, dwd0 = after(act, dwd0)
-        dwd0_far = send_down(dwd0)
-        y2 = block(act, 2, wd_all, NN_DIMS) + y3
+        y2 = block(act, 2, wd_all, NN_DIMS)
         act, y2 = after(act, y2)
+        act, dy_all, y2 = after(act, dy_all, y2 + y3)
         y2 = hop(y2, 2)
-        dwd1 = down_grad(act, 1)
-        dwd1, act, gate_low, lin_low = after(dwd1, act, gate_low, lin_low)
-        dwd1_far = send_down(dwd1)
-
+        down_sum = down_grad(act, 1 - side)
+        down_sum, act, gate_low, lin_low = after(down_sum, act, gate_low, lin_low)
+        down_sum = hop(down_sum, group)
         d_up = up_back(dy_all, wd_all, gate_low, lin_low)
+
+        far_a = up_grad(m_all, d_up, chip ^ 3)
+        d_up, far_a = after(d_up, far_a)
+        far_a = hop(far_a, group)
         dm3 = block(d_up, 3, w_all, NT_DIMS)
         d_up, dm3 = after(d_up, dm3)
         dm3 = hop(dm3, 1)
@@ -460,27 +457,21 @@
         d_up, dm2 = after(d_up, dm2)
         d_up, dm2 = after(d_up, dm2 + dm3)
         dm2 = hop(dm2, 2)
-
-        far_a = up_grad(m_all, d_up, chip ^ 3)
-        d_up, far_a = after(d_up, far_a)
-        far_a = hop(far_a, group)
         far_b = up_grad(m_all, d_up, chip ^ 2)
-        d_up, act, far_b = after(d_up, act, far_b)
+        d_up, far_b = after(d_up, far_b)
         far_b = hop(far_b, group)
+        near_a = up_grad(m_all, d_up, chip ^ 1)
+        d_up, near_a = after(d_up, near_a)
+        dm1 = block(d_up, 1, w_all, NT_DIMS)
+        d_up, dm1, near_a = after(d_up, dm1, near_a)
+        dm1 = hop(dm1, 1)
+        dm0 = block(d_up, 0, w_all, NT_DIMS)
+        d_up, dm0, act = after(d_up, dm0, act)
         y1 = block(act, 1, wd_all, NN_DIMS)
         act, d_up, y1 = after(act, d_up, y1)
         y1 = hop(y1, 1)
-        dm1 = block(d_up, 1, w_all, NT_DIMS)
-        d_up, dm1 = after(d_up, dm1)
-        dm1 = hop(dm1, 1)
-        dm0 = block(d_up, 0, w_all, NT_DIMS)
-        d_up, dm0, act = after(d_up, dm0, act)
         y0 = block(act, 0, wd_all, NN_DIMS)
-        d_up, y0 = after(d_up, y0)
-        near_a = up_grad(m_all, d_up, chip ^ 1)
-        d_up, near_a, dm2 = after(d_up, near_a, dm2)
-
-        grad_w_down = jnp.concatenate([lax.dynamic_slice(g, (side * f_loc, 0), (f_loc, half)) + far for g, far in ((dwd0, dwd0_far), (dwd1, dwd1_far))], axis=1)
+        d_up, y0, dm2 = after(d_up, y0, dm2)
 
         def rows_of(c, *parts):
             return sum(lax.dynamic_slice(v, (c * h_loc, 0), (h_loc, 2 * f_pad)) for v in parts)
@@ -502,19 +493,23 @@
         d_normed = mm(d_proj, wqkv, NT_DIMS)
         d_normed, d_up = after(d_normed, d_up)
         near_b = up_grad(m_all, d_up, chip)
-        near_b, d_normed = after(near_b, d_normed)
+        near_b, d_normed, act, down_sum = after(near_b, d_normed, act, down_sum)
+        grad_w_down = mm(lax.dynamic_slice(act, (0, side * f_blk), (group * tokens, f_blk)), dy_all, TN_DIMS)[:f_loc] + down_sum[:f_loc]
         grad_attn_gain = jnp.sum(d_normed * hid_wide * inv_one, axis=0)
         small_grads = jnp.concatenate([grad_attn_gain.reshape(n_dev, h_loc), grad_b_qkv.reshape(n_dev, q_loc), grad_mlp_gain.reshape(n_dev, h_loc)], axis=1)
-        for k in (1, 2, group):
-            pair = small_grads.reshape(n_dev // 2, 2, -1) if k == 1 else small_grads.reshape(-1, 2, h_loc + q_loc + h_loc)
+
+        def halved(sums, k):
+            pair = sums.reshape(-1, 2, h_loc + q_loc + h_loc)
             mine = lax.div(me, k) % 2
-            small_grads = lax.dynamic_index_in_dim(pair, mine, 1, keepdims=False) + hop(lax.dynamic_index_in_dim(pair, 1 - mine, 1, keepdims=False), k)
-        small_grads = small_grads.reshape(-1)
+            return lax.dynamic_index_in_dim(pair, mine, 1, keepdims=False) + hop(lax.dynamic_index_in_dim(pair, 1 - mine, 1, keepdims=False), k)
+
+        small_grads = halved(halved(small_grads, 1), 2)
         scaled_one = d_normed * gain_one
         grad_hidden = (d_mid + inv_one * (scaled_one - hid_wide * inv_one * inv_one * jnp.mean(scaled_one * hid_wide, axis=-1, keepdims=True))).astype(BF16)
         y0, y1, y2, mid_late, grad_hidden = after(y0, y1, y2, mid, grad_hidden)
         output = (mid_late.astype(F32) + (y0 + y1 + y2)).astype(BF16)
-        far_b, output, grad_hidden, grad_w_down = after(far_b, output, grad_hidden, grad_w_down)
+        far_b, output, grad_hidden, grad_w_down, small_grads = after(far_b, output, grad_hidden, grad_w_down, small_grads)
+        small_grads = halved(small_grads, group).reshape(-1)
         piece0 = rows_of(core, near_b, far_b)
         piece1 = hop(rows_of(1 - core, near_b, far_b), 1)
         grad_w_up = join_up([piece0, piece1, piece2, piece3], rank, group, f_loc)

time: 2620 us -> 2430 us (0.927)
  waiting for transfers between devices: 1150 us -> 1040 us
  Pallas kernels: 456 us -> 395 us
    ppermute x33 -> x32, waiting for transfers between devices: 1130 us -> 969 us  [hop(): return lax.ppermute(v, ax, [(i, i ^ k) for i in range(n_dev)])]
    all_gather x2, waiting for transfers between devices: 12.2 us -> 67.5 us  [gather_rows(): return lax.all_gather(shard, ax, axis=0, tiled=True)]
    pallas_call x1, Pallas kernels: 68.8 us -> 33.2 us  [attend(): pl.pallas_call(functools.partial(attend_kernel, heads, kv_heads), grid=(b...]
  transfers between devices with their start and end apart: 37 -> 36, of which waited for: 15 -> 14; matrix products, arithmetic and copies ran while one was open for 23% -> 23% of each run, Pallas kernels for 13% -> 12%
where the time goes in v3:
time: 2430 us; the launch traced here: 2420 us
  waiting for transfers between devices  1040 us (43%)
  matrix products  696 us (29%)
  Pallas kernels  395 us (16%)
  other arithmetic  134 us (6%)
  local copies, waits for them, and re-layouts  123 us (5%)
    ppermute x32, waiting for transfers between devices, hop(): return lax.ppermute(v, ax, [(i, i ^ k) for i in range(n_dev)])  969 us
    dot_general x20, matrix products, mm(): return lax.dot_general(a, b, dims, preferred_element_type=F32)  696 us
    pallas_call x1, Pallas kernels, up_act(): pl.pallas_call(up_kernel, grid=(tokens // T_BLOCK,), in_specs=[pl.BlockSp...  169 us
    pallas_call x1, Pallas kernels, up_back(): pl.pallas_call(up_back_kernel, grid=(tokens // T_BLOCK,), in_specs=[pl.Bl...  112 us
    all_gather x2, waiting for transfers between devices, gather_rows(): return lax.all_gather(shard, ax, axis=0, tiled=True)  67.5 us
  transfers between devices with their start and end apart: 36, of which 14 were waited for; matrix products, arithmetic and copies ran while one was open for 23% of the time, Pallas kernels for 12%

profile of v3, /device:TPU:0, one launch (start us, length us, event | category | flops | bytes accessed | tf_op | source)
XLA Modules:
  0.0 2424.2 jit_solution(9401330670741796085)
XLA Ops:
  25.0 13.2 split_up.1
  40.6 14.3 dynamic_update_slice.56
  59.2 37.6 %all-gather.3.cloned.1.call-done = bf16[2048,2560]{1,0:T(8,128)(2,1)} async-done(((bf16[256,2560]{1,0:T(8,128)(2,1)}), bf16[2048,2560]{1,0:T(8,128)(2,1)}) %all-gather.3.cloned.1.call-update) | async-done | bytes 10485776 | tf_op jit(solution)/shard_map/all_gather | solution.py:348
  96.8 22.4 convolution_add_fusion.z_ref
  119.2 33.2 %attend.1 = (bf16[1536,2560]{1,0:T(8,128)(2,1)}, bf16[1536,2048]{1,0:T(8,128)(2,1)}) custom-call(f32[1536,2560]{1,0:T(8,128)} %convolution_add_fusion.z_ref, f32[1536,128]{1,0:T(8,128)S(1)} %get-tuple-element.185.cos_ref, f32[1536,128]{1,0:T(8,128)S(1)} %get-tuple-element.184.sin_ref), custom_call_target="tpu_custom_call" | custom-call | flops 19327352832 | bytes 31457280 | tf_op jit(solution)/shard_map/attend/pallas_call | solution.py:159
  152.3 29.9 %all-gather.5.cloned.1.call-done = bf16[2048,2048]{1,0:T(8,128)(2,1)} async-done(((bf16[256,2048]{1,0:T(8,128)(2,1)}), bf16[2048,2048]{1,0:T(8,128)(2,1)}) %all-gather.5.cloned.1.call-update) | async-done | bytes 8388624 | tf_op jit(solution)/shard_map/all_gather | solution.py:348
  182.2 18.9 fusion.19
  203.0 8.0 broadcast_in_dim.37
  241.9 49.2 %collective-permute-done.9 = bf16[256,5632]{1,0:T(8,128)(2,1)S(1)} collective-permute-done((bf16[256,5632]{1,0:T(8,128)(2,1)}, bf16[256,5632]{1,0:T(8,128)(2,1)S(1)}, u32[]{:S(2)}, u32[]{:S(2)}) %collective-permute-start.9) | collective-permute-done | bytes 2883616 | tf_op jit(solution)/shard_map/ppermute | solution.py:345
  292.7 59.3 %collective-permute-done.10 = bf16[256,5632]{1,0:T(8,128)(2,1)S(1)} collective-permute-done((bf16[256,5632]{1,0:T(8,128)(2,1)}, bf16[256,5632]{1,0:T(8,128)(2,1)S(1)}, u32[]{:S(2)}, u32[]{:S(2)}) %collective-permute-start.10) | collective-permute-done | bytes 2883616 | tf_op jit(solution)/shard_map/ppermute | solution.py:345
  360.3 18.5 dynamic_update_slice.54
  394.9 56.1 %collective-permute-done.13 = bf16[256,5632]{1,0:T(8,128)(2,1)} collective-permute-done((bf16[256,5632]{1,0:T(8,128)(2,1)}, bf16[256,5632]{1,0:T(8,128)(2,1)}, u32[]{:S(2)}, u32[]{:S(2)}) %collective-permute-start.13) | collective-permute-done | bytes 2883616 | tf_op jit(solution)/shard_map/ppermute | solution.py:345
  461.2 169.2 %up_act.1 = (bf16[6144,2816]{1,0:T(8,128)(2,1)}, bf16[6144,2816]{1,0:T(8,128)(2,1)}, bf16[6144,2816]{1,0:T(8,128)(2,1)}) custom-call(bf16[6144,2048]{1,0:T(8,128)(2,1)} %constant_dynamic-update-slice_fusion.4.m_ref, bf16[2048,5632]{1,0:T(8,128)(2,1)} %constant_dynamic-update-slice_fusion.3.w_ref), custom_call_target="tpu_custom_call" | custom-call | flops 141733920768 | bytes 152043520 | tf_op jit(solution)/shard_map/up_act/pallas_call | solution.py:206
  636.4 24.9 %fusion.42 = f32[1536,2048]{1,0:T(8,128)} fusion(bf16[2816,2048]{1,0:T(8,128)(2,1)} %constant_dynamic-update-slice_fusion.2.wd_ref, bf16[6144,2816]{1,0:T(8,128)(2,1)} %get-tuple-element.157), kind=kOutput, calls=%fused_computation.55 | convolution fusion | flops 17716740096 | bytes 32768000 | tf_op jit(solution)/shard_map/dot_general | solution.py:32
  661.8 22.5 fusion.40
  697.4 10.9 add.207
  708.3 46.2 %fusion.10 = f32[1408,2048]{1,0:T(8,128)} fusion(bf16[6144,2048]{1,0:T(8,128)(2,1)} %constant_dynamic-update-slice_fusion.dy_ref, bf16[6144,2816]{1,0:T(8,128)(2,1)} %get-tuple-element.157, s32[]{:T(128)S(6)} %select_n.160), kind=kOutput, calls=%fused_computation.14 | convolution fusion | flops 35433480192 | bytes 54001668 | tf_op jit(solution)/shard_map/dot_general | solution.py:32
  754.6 112.1 %up_back.1 = bf16[6144,5632]{1,0:T(8,128)(2,1)} custom-call(bf16[6144,2048]{1,0:T(8,128)(2,1)} %constant_dynamic-update-slice_fusion.dy_ref, bf16[2816,2048]{1,0:T(8,128)(2,1)} %constant_dynamic-update-slice_fusion.2.wd_ref, bf16[6144,2816]{1,0:T(8,128)(2,1)} %get-tuple-element.119.g_ref, bf16[6144,2816]{1,0:T(8,128)(2,1)} %get-tuple-element.120.l_ref), custom_call_target="tpu_custom_call" | custom-call | flops 70866960384 | bytes 175112192 | tf_op jit(solution)/shard_map/up_back/pallas_call | solution.py:234
  866.7 47.0 %fusion.52 = f32[512,5632]{1,0:T(8,128)} fusion(bf16[6144,5632]{1,0:T(8,128)(2,1)} %up_back.1, bf16[6144,2048]{1,0:T(8,128)(2,1)} %constant_dynamic-update-slice_fusion.4.m_ref, s32[]{:T(128)S(6)} %select_n.161), kind=kOutput, calls=%fused_computation.64 | convolution fusion | flops 35433480192 | bytes 87031808 | tf_op jit(solution)/shard_map/dot_general | solution.py:32
  913.7 44.7 %fusion.8 = f32[1536,2048]{1,0:T(8,128)} fusion(bf16[2048,5632]{1,0:T(8,128)(2,1)} %constant_dynamic-update-slice_fusion.3.w_ref, bf16[6144,5632]{1,0:T(8,128)(2,1)} %up_back.1), kind=kOutput, calls=%fused_computation.12 | convolution fusion | flops 35433480192 | bytes 52953088 | tf_op jit(solution)/shard_map/dot_general | solution.py:32
  958.5 44.8 %fusion.6 = f32[1536,2048]{1,0:T(8,128)} fusion(bf16[2048,5632]{1,0:T(8,128)(2,1)} %constant_dynamic-update-slice_fusion.3.w_ref, bf16[6144,5632]{1,0:T(8,128)(2,1)} %up_back.1), kind=kOutput, calls=%fused_computation.10 | convolution fusion | flops 35433480192 | bytes 52953088 | tf_op jit(solution)/shard_map/dot_general | solution.py:32
  1003.3 14.3 add.209
  1017.6 47.0 %fusion.50 = f32[512,5632]{1,0:T(8,128)} fusion(bf16[6144,5632]{1,0:T(8,128)(2,1)} %up_back.1, bf16[6144,2048]{1,0:T(8,128)(2,1)} %constant_dynamic-update-slice_fusion.4.m_ref, s32[]{:T(128)S(6)} %select_n.162), kind=kOutput, calls=%fused_computation.62 | convolution fusion | flops 35433480192 | bytes 87031808 | tf_op jit(solution)/shard_map/dot_general | solution.py:32
  1064.6 47.0 %fusion.48 = f32[512,5632]{1,0:T(8,128)} fusion(bf16[6144,5632]{1,0:T(8,128)(2,1)} %up_back.1, bf16[6144,2048]{1,0:T(8,128)(2,1)} %constant_dynamic-update-slice_fusion.4.m_ref, s32[]{:T(128)S(6)} %select_n.163), kind=kOutput, calls=%fused_computation.60 | convolution fusion | flops 35433480192 | bytes 87031808 | tf_op jit(solution)/shard_map/dot_general | solution.py:32
  1111.6 45.0 %fusion.4 = f32[1536,2048]{1,0:T(8,128)} fusion(bf16[2048,5632]{1,0:T(8,128)(2,1)} %constant_dynamic-update-slice_fusion.3.w_ref, bf16[6144,5632]{1,0:T(8,128)(2,1)} %up_back.1), kind=kOutput, calls=%fused_computation.8 | convolution fusion | flops 35433480192 | bytes 52953088 | tf_op jit(solution)/shard_map/dot_general | solution.py:32
  1157.7 44.8 %fusion.2 = f32[1536,2048]{1,0:T(8,128)} fusion(bf16[2048,5632]{1,0:T(8,128)(2,1)} %constant_dynamic-update-slice_fusion.3.w_ref, bf16[6144,5632]{1,0:T(8,128)(2,1)} %up_back.1), kind=kOutput, calls=%fused_computation.6 | convolution fusion | flops 35433480192 | bytes 52953088 | tf_op jit(solution)/shard_map/dot_general | solution.py:32
  1202.5 24.8 %fusion.38 = f32[1536,2048]{1,0:T(8,128)} fusion(bf16[2816,2048]{1,0:T(8,128)(2,1)} %constant_dynamic-update-slice_fusion.2.wd_ref, bf16[6144,2816]{1,0:T(8,128)(2,1)} %get-tuple-element.157), kind=kOutput, calls=%fused_computation.51 | convolution fusion | flops 17716740096 | bytes 32768000 | tf_op jit(solution)/shard_map/dot_general | solution.py:32
  1227.4 25.3 %fusion.36 = f32[1536,2048]{1,0:T(8,128)} fusion(bf16[2816,2048]{1,0:T(8,128)(2,1)} %constant_dynamic-update-slice_fusion.2.wd_ref, bf16[6144,2816]{1,0:T(8,128)(2,1)} %get-tuple-element.157), kind=kOutput, calls=%fused_computation.49 | convolution fusion | flops 17716740096 | bytes 32768000 | tf_op jit(solution)/shard_map/dot_general | solution.py:32
  1252.7 177.1 %collective-permute-done.20 = f32[1536,2048]{1,0:T(8,128)} collective-permute-done((f32[1536,2048]{1,0:T(8,128)}, f32[1536,2048]{1,0:T(8,128)}, u32[]{:S(2)}, u32[]{:S(2)}) %collective-permute-start.20) | collective-permute-done | bytes 12582944 | tf_op jit(solution)/shard_map/ppermute | solution.py:345
  1429.8 19.6 fusion.22
  1449.3 12.1 fusion.18
  1461.5 21.5 fusion.54
  1484.3 21.6 convolution_convert_fusion.dctx_ref
  1505.9 46.3 %attend_back.1 = (bf16[1536,2560]{1,0:T(8,128)(2,1)}, f32[1,2560]{1,0:T(1,128)S(1)}) custom-call(bf16[1536,2560]{1,0:T(8,128)(2,1)} %get-tuple-element.144.qkv_ref, bf16[1536,2048]{1,0:T(8,128)(2,1)} %convolution_convert_fusion.dctx_ref, f32[1536,128]{1,0:T(8,128)S(1)} %get-tuple-element.185.cos_ref, f32[1536,128]{1,0:T(8,128)S(1)} %get-tuple-element.184.sin_ref), custom_call_target="tpu_custom_call" | custom-call | flops 48318382080 | bytes 31457280 | tf_op jit(solution)/shard_map/attend_back/pallas_call | solution.py:177
  1552.2 22.1 fusion.71
  1575.5 310.3 %collective-permute-done.29 = f32[512,5632]{1,0:T(8,128)} collective-permute-done((f32[512,5632]{1,0:T(8,128)}, f32[512,5632]{1,0:T(8,128)}, u32[]{:S(2)}, u32[]{:S(2)}) %collective-permute-start.29) | collective-permute-done | bytes 11534368 | tf_op jit(solution)/shard_map/ppermute | solution.py:345
  1885.8 12.9 dynamic-slice_add_fusion
  1901.0 22.9 fusion.72
  1923.9 46.8 %fusion.46 = f32[512,5632]{1,0:T(8,128)} fusion(bf16[6144,5632]{1,0:T(8,128)(2,1)} %up_back.1, bf16[6144,2048]{1,0:T(8,128)(2,1)} %constant_dynamic-update-slice_fusion.4.m_ref, s32[]{:T(128)S(6)} %select_n.164), kind=kOutput, calls=%fused_computation.58 | convolution fusion | flops 35433480192 | bytes 87031808 | tf_op jit(solution)/shard_map/dot_general | solution.py:32
  1970.7 162.2 %collective-permute-done.24 = f32[1408,2048]{1,0:T(8,128)} collective-permute-done((f32[1408,2048]{1,0:T(8,128)}, f32[1408,2048]{1,0:T(8,128)}, u32[]{:S(2)}, u32[]{:S(2)}) %collective-permute-start.24) | collective-permute-done | bytes 11534368 | tf_op jit(solution)/shard_map/ppermute | solution.py:345
  2133.0 8.6 fusion.35
  2141.9 55.6 %slice_add_fusion = f32[1376,2048]{1,0:T(8,128)} fusion(f32[1408,2048]{1,0:T(8,128)} %collective-permute-done.24, bf16[6144,2048]{1,0:T(8,128)(2,1)} %constant_dynamic-update-slice_fusion.dy_ref, bf16[6144,2816]{1,0:T(8,128)(2,1)} %get-tuple-element.157, s32[]{:T(128)S(6)} %select_n.158), kind=kOutput, calls=%fused_computation.48 | convolution fusion | flops 34630991872 | bytes 65011716 | tf_op jit(solution)/shard_map/dot_general | solution.py:32
  2197.5 14.4 fusion.30
  2214.2 18.9 add_convert_fusion
  2233.1 105.8 %collective-permute-done.26 = f32[2,832]{1,0:T(2,128)S(1)} collective-permute-done((f32[2,832]{1,0:T(2,128)S(1)}, f32[2,832]{1,0:T(2,128)S(1)}, u32[]{:S(2)}, u32[]{:S(2)}) %collective-permute-start.26) | collective-permute-done | bytes 6688 | tf_op jit(solution)/shard_map/ppermute | solution.py:345
  2338.9 39.9 %collective-permute-done.19 = f32[512,5632]{1,0:T(8,128)} collective-permute-done((f32[512,5632]{1,0:T(8,128)}, f32[512,5632]{1,0:T(8,128)}, u32[]{:S(2)}, u32[]{:S(2)}) %collective-permute-start.19) | collective-permute-done | bytes 11534368 | tf_op jit(solution)/shard_map/ppermute | solution.py:345
  2378.8 7.8 dynamic-slice_add_fusion.2
  2396.4 21.0 join_up.1
  (171 shorter events, 131.0 us)
Async XLA Ops:
  7.2 89.6 %all-gather.3.cloned.1.call-start = ((), (), s32[]{:S(2)}) async-start(), calls=%async_computation.2 | async-start | bytes 11796480 | tf_op jit(solution)/shard_map/all_gather | solution.py:348
  7.9 174.3 %all-gather.5.cloned.1.call-start = ((), (), s32[]{:S(2)}) async-start(), calls=%async_computation.3 | async-start | bytes 9437184 | tf_op jit(solution)/shard_map/all_gather | solution.py:348
  8.7 2408.8 %reduce-scatter.5.cloned.1.call-start = ((), (), s32[]{:S(2)}) async-start(), calls=%async_computation.5 | async-start | bytes 18874368 | tf_op jit(solution)/shard_map/reduce_scatter | solution.py:351
  9.5 8.8 collective-permute-start
  18.3 4.6 collective-permute-start.1
  22.9 15.3 collective-permute-start.2
  38.2 164.5 %collective-permute-start.5 = (bf16[256,5632]{1,0:T(8,128)(2,1)}, bf16[256,5632]{1,0:T(8,128)(2,1)}, u32[]{:S(2)}, u32[]{:S(2)}) collective-permute-start(bf16[256,5632]{1,0:T(8,128)(2,1)} %get-tuple-element.97), channel_id=1, source_target_pairs={{0,1},{1,0},{2,3},{3,2},{4,5},{5,4},{6,7},{7,6}} | collective-permute-start | bytes 8650760 | tf_op jit(solution)/shard_map/ppermute | solution.py:345
  38.2 174.8 %collective-permute-start.6 = (bf16[256,5632]{1,0:T(8,128)(2,1)}, bf16[256,5632]{1,0:T(8,128)(2,1)}, u32[]{:S(2)}, u32[]{:S(2)}) collective-permute-start(bf16[256,5632]{1,0:T(8,128)(2,1)} %get-tuple-element.98), channel_id=1, source_target_pairs={{0,2},{1,3},{2,0},{3,1},{4,6},{5,7},{6,4},{7,5}} | collective-permute-start | bytes 8650760 | tf_op jit(solution)/shard_map/ppermute | solution.py:345
  39.7 185.8 %collective-permute-start.7 = (bf16[256,5632]{1,0:T(8,128)(2,1)}, bf16[256,5632]{1,0:T(8,128)(2,1)}, u32[]{:S(2)}, u32[]{:S(2)}) collective-permute-start(bf16[256,5632]{1,0:T(8,128)(2,1)} %get-tuple-element.99), channel_id=1, source_target_pairs={{0,3},{1,2},{2,1},{3,0},{4,7},{5,6},{6,5},{7,4}} | collective-permute-start | bytes 8650760 | tf_op jit(solution)/shard_map/ppermute | solution.py:345
  40.1 190.5 %collective-permute-start.8 = (bf16[256,5632]{1,0:T(8,128)(2,1)}, bf16[256,5632]{1,0:T(8,128)(2,1)}, u32[]{:S(2)}, u32[]{:S(2)}) collective-permute-start(bf16[256,5632]{1,0:T(8,128)(2,1)} %get-tuple-element.96), channel_id=1, source_target_pairs={{0,4},{1,5},{2,6},{3,7},{4,0},{5,1},{6,2},{7,3}} | collective-permute-start | bytes 8650760 | tf_op jit(solution)/shard_map/ppermute | solution.py:345
  40.5 313.3 %collective-permute-start.4 = (bf16[1536,2048]{1,0:T(8,128)(2,1)}, bf16[1536,2048]{1,0:T(8,128)(2,1)}, u32[]{:S(2)}, u32[]{:S(2)}) collective-permute-start(bf16[1536,2048]{1,0:T(8,128)(2,1)} %bitcast.80), channel_id=1, source_target_pairs={{0,1},{1,0},{2,3},{3,2},{4,5},{5,4},{6,7},{7,6}} | collective-permute-start | bytes 18874376 | tf_op jit(solution)/shard_map/ppermute | solution.py:345
  202.7 176.2 %collective-permute-start.3 = (bf16[1536,2048]{1,0:T(8,128)(2,1)S(1)}, bf16[1536,2048]{1,0:T(8,128)(2,1)}, u32[]{:S(2)}, u32[]{:S(2)}) collective-permute-start(bf16[1536,2048]{1,0:T(8,128)(2,1)S(1)} %fusion.14), channel_id=1, source_target_pairs={{0,1},{1,0},{2,3},{3,2},{4,5},{5,4},{6,7},{7,6}} | collective-permute-start | bytes 18874376 | tf_op jit(solution)/shard_map/ppermute | solution.py:345
  213.0 172.4 %collective-permute-start.11 = (bf16[1536,2048]{1,0:T(8,128)(2,1)S(1)}, bf16[1536,2048]{1,0:T(8,128)(2,1)}, u32[]{:S(2)}, u32[]{:S(2)}) collective-permute-start(bf16[1536,2048]{1,0:T(8,128)(2,1)S(1)} %fusion.14), channel_id=1, source_target_pairs={{0,2},{1,3},{2,0},{3,1},{4,6},{5,7},{6,4},{7,5}} | collective-permute-start | bytes 18874376 | tf_op jit(solution)/shard_map/ppermute | solution.py:345
  225.5 65.6 %collective-permute-start.9 = (bf16[256,5632]{1,0:T(8,128)(2,1)}, bf16[256,5632]{1,0:T(8,128)(2,1)S(1)}, u32[]{:S(2)}, u32[]{:S(2)}) collective-permute-start(bf16[256,5632]{1,0:T(8,128)(2,1)} %collective-permute-done.5), channel_id=1, source_target_pairs={{0,4},{1,5},{2,6},{3,7},{4,0},{5,1},{6,2},{7,3}} | collective-permute-start | bytes 8650760 | tf_op jit(solution)/shard_map/ppermute | solution.py:345
  230.6 121.5 %collective-permute-start.10 = (bf16[256,5632]{1,0:T(8,128)(2,1)}, bf16[256,5632]{1,0:T(8,128)(2,1)S(1)}, u32[]{:S(2)}, u32[]{:S(2)}) collective-permute-start(bf16[256,5632]{1,0:T(8,128)(2,1)} %collective-permute-done.6), channel_id=1, source_target_pairs={{0,4},{1,5},{2,6},{3,7},{4,0},{5,1},{6,2},{7,3}} | collective-permute-start | bytes 8650760 | tf_op jit(solution)/shard_map/ppermute | solution.py:345
  385.4 69.2 %collective-permute-start.12 = (bf16[1536,2048]{1,0:T(8,128)(2,1)}, bf16[1536,2048]{1,0:T(8,128)(2,1)}, u32[]{:S(2)}, u32[]{:S(2)}) collective-permute-start(bf16[1536,2048]{1,0:T(8,128)(2,1)} %collective-permute-done.11), channel_id=1, source_target_pairs={{0,1},{1,0},{2,3},{3,2},{4,5},{5,4},{6,7},{7,6}} | collective-permute-start | bytes 18874376 | tf_op jit(solution)/shard_map/ppermute | solution.py:345
  385.4 65.7 %collective-permute-start.13 = (bf16[256,5632]{1,0:T(8,128)(2,1)}, bf16[256,5632]{1,0:T(8,128)(2,1)}, u32[]{:S(2)}, u32[]{:S(2)}) collective-permute-start(bf16[256,5632]{1,0:T(8,128)(2,1)} %collective-permute-done.7), channel_id=1, source_target_pairs={{0,4},{1,5},{2,6},{3,7},{4,0},{5,1},{6,2},{7,3}} | collective-permute-start | bytes 8650760 | tf_op jit(solution)/shard_map/ppermute | solution.py:345
  387.0 243.4 %collective-permute-start.14 = (bf16[1536,2048]{1,0:T(8,128)(2,1)}, bf16[1536,2048]{1,0:T(8,128)(2,1)}, u32[]{:S(2)}, u32[]{:S(2)}) collective-permute-start(bf16[1536,2048]{1,0:T(8,128)(2,1)} %bitcast.82), channel_id=1, source_target_pairs={{0,2},{1,3},{2,0},{3,1},{4,6},{5,7},{6,4},{7,5}} | collective-permute-start | bytes 18874376 | tf_op jit(solution)/shard_map/ppermute | solution.py:345
  387.9 242.6 %collective-permute-start.15 = (bf16[1376,2048]{1,0:T(8,128)(2,1)}, bf16[1376,2048]{1,0:T(8,128)(2,1)}, u32[]{:S(2)}, u32[]{:S(2)}) collective-permute-start(bf16[1376,2048]{1,0:T(8,128)(2,1)} %param.19), channel_id=1, source_target_pairs={{0,4},{1,5},{2,6},{3,7},{4,0},{5,1},{6,2},{7,3}} | collective-permute-start | bytes 16908296 | tf_op jit(solution)/shard_map/ppermute | solution.py:345
  661.3 36.1 %collective-permute-start.17 = (f32[1536,2048]{1,0:T(8,128)}, f32[1536,2048]{1,0:T(8,128)}, u32[]{:S(2)}, u32[]{:S(2)}) collective-permute-start(f32[1536,2048]{1,0:T(8,128)} %fusion.42), channel_id=1, source_target_pairs={{0,1},{1,0},{2,3},{3,2},{4,5},{5,4},{6,7},{7,6}} | collective-permute-start | bytes 37748744 | tf_op jit(solution)/shard_map/ppermute | solution.py:345
  661.3 29.5 %collective-permute-start.16 = (bf16[1536,2048]{1,0:T(8,128)(2,1)}, bf16[1536,2048]{1,0:T(8,128)(2,1)}, u32[]{:S(2)}, u32[]{:S(2)}) collective-permute-start(bf16[1536,2048]{1,0:T(8,128)(2,1)} %collective-permute-done.14), channel_id=1, source_target_pairs={{0,1},{1,0},{2,3},{3,2},{4,5},{5,4},{6,7},{7,6}} | collective-permute-start | bytes 18874376 | tf_op jit(solution)/shard_map/ppermute | solution.py:345
  958.5 44.8 %collective-permute-start.18 = (f32[1536,2048]{1,0:T(8,128)}, f32[1536,2048]{1,0:T(8,128)}, u32[]{:S(2)}, u32[]{:S(2)}) collective-permute-start(f32[1536,2048]{1,0:T(8,128)} %fusion.8), channel_id=1, source_target_pairs={{0,1},{1,0},{2,3},{3,2},{4,5},{5,4},{6,7},{7,6}} | collective-permute-start | bytes 37748744 | tf_op jit(solution)/shard_map/ppermute | solution.py:345
  1156.7 273.0 %collective-permute-start.20 = (f32[1536,2048]{1,0:T(8,128)}, f32[1536,2048]{1,0:T(8,128)}, u32[]{:S(2)}, u32[]{:S(2)}) collective-permute-start(f32[1536,2048]{1,0:T(8,128)} %add.209), channel_id=1, source_target_pairs={{0,2},{1,3},{2,0},{3,1},{4,6},{5,7},{6,4},{7,5}} | collective-permute-start | bytes 37748744 | tf_op jit(solution)/shard_map/ppermute | solution.py:345
  1157.5 272.2 %collective-permute-start.23 = (f32[1536,2048]{1,0:T(8,128)}, f32[1536,2048]{1,0:T(8,128)}, u32[]{:S(2)}, u32[]{:S(2)}) collective-permute-start(f32[1536,2048]{1,0:T(8,128)} %fusion.4), channel_id=1, source_target_pairs={{0,1},{1,0},{2,3},{3,2},{4,5},{5,4},{6,7},{7,6}} | collective-permute-start | bytes 37748744 | tf_op jit(solution)/shard_map/ppermute | solution.py:345
  1202.5 227.2 %slice-start = ((s8[6291456]{0:T(1024)(128)(4,1)}), s8[4194304]{0:T(1024)(128)(4,1)S(1)}, s32[]{:S(2)}) async-start(s8[6291456]{0:T(1024)(128)(4,1)} %bitcast.76), calls=%async_computation.6 | async-start | bytes 8388608
  1202.5 246.8 %slice-start.4 = ((s8[6291456]{0:T(1024)(128)(4,1)}), s8[4194304]{0:T(1024)(128)(4,1)S(1)}, s32[]{:S(2)}) async-start(s8[6291456]{0:T(1024)(128)(4,1)} %bitcast.83), calls=%async_computation.10 | async-start | bytes 8388608
  1227.3 202.4 %slice-start.1 = ((s8[6291456]{0:T(1024)(128)(4,1)}), s8[2097152]{0:T(1024)(128)(4,1)S(1)}, s32[]{:S(2)}) async-start(s8[6291456]{0:T(1024)(128)(4,1)} %bitcast.76), calls=%async_computation.7 | async-start | bytes 4194304
  1227.3 202.4 %copy-start.7 = (f32[1,2,8,128]{3,1,2,0:T(2,128)S(1)}, f32[1,2,8,128]{3,1,2,0:T(2,128)}, u32[]{:S(2)}) copy-start(f32[1,2,8,128]{3,1,2,0:T(2,128)} %copy-done.6) | copy-start | bytes 24580
  1227.3 202.4 %copy-start.9 = (f32[1536]{0:T(1024)S(1)}, f32[1536]{0:T(1024)}, u32[]{:S(2)}) copy-start(f32[1536]{0:T(1024)} %copy-done.8) | copy-start | bytes 18436
  1227.3 222.0 %slice-start.5 = ((s8[6291456]{0:T(1024)(128)(4,1)}), s8[2097152]{0:T(1024)(128)(4,1)S(1)}, s32[]{:S(2)}) async-start(s8[6291456]{0:T(1024)(128)(4,1)} %bitcast.83), calls=%async_computation.11 | async-start | bytes 4194304
  1483.0 934.5 %reduce-scatter.3.cloned.1.call-start = ((), (), s32[]{:S(2)}) async-start(), calls=%async_computation.4 | async-start | bytes 23592960 | tf_op jit(solution)/shard_map/reduce_scatter | solution.py:351
  1483.0 402.8 %collective-permute-start.29 = (f32[512,5632]{1,0:T(8,128)}, f32[512,5632]{1,0:T(8,128)}, u32[]{:S(2)}, u32[]{:S(2)}) collective-permute-start(f32[512,5632]{1,0:T(8,128)} %fusion.52), channel_id=1, source_target_pairs={{0,4},{1,5},{2,6},{3,7},{4,0},{5,1},{6,2},{7,3}} | collective-permute-start | bytes 34603016 | tf_op jit(solution)/shard_map/ppermute | solution.py:345
  1574.3 558.6 %collective-permute-start.24 = (f32[1408,2048]{1,0:T(8,128)}, f32[1408,2048]{1,0:T(8,128)}, u32[]{:S(2)}, u32[]{:S(2)}) collective-permute-start(f32[1408,2048]{1,0:T(8,128)} %fusion.10), channel_id=1, source_target_pairs={{0,4},{1,5},{2,6},{3,7},{4,0},{5,1},{6,2},{7,3}} | collective-permute-start | bytes 34603016 | tf_op jit(solution)/shard_map/ppermute | solution.py:345
  1574.8 637.2 %collective-permute-start.22 = (f32[1536,2048]{1,0:T(8,128)}, f32[1536,2048]{1,0:T(8,128)}, u32[]{:S(2)}, u32[]{:S(2)}) collective-permute-start(f32[1536,2048]{1,0:T(8,128)} %add.207), channel_id=1, source_target_pairs={{0,2},{1,3},{2,0},{3,1},{4,6},{5,7},{6,4},{7,5}} | collective-permute-start | bytes 37748744 | tf_op jit(solution)/shard_map/ppermute | solution.py:345
  1898.7 492.9 %collective-permute-start.30 = (f32[256,5632]{1,0:T(8,128)}, f32[256,5632]{1,0:T(8,128)}, u32[]{:S(2)}, u32[]{:S(2)}) collective-permute-start(f32[256,5632]{1,0:T(8,128)} %get-tuple-element.175), channel_id=1, source_target_pairs={{0,2},{1,3},{2,0},{3,1},{4,6},{5,7},{6,4},{7,5}} | collective-permute-start | bytes 17301512 | tf_op jit(solution)/shard_map/ppermute | solution.py:345
  1899.5 313.4 %collective-permute-start.21 = (f32[1536,2048]{1,0:T(8,128)}, f32[1536,2048]{1,0:T(8,128)}, u32[]{:S(2)}, u32[]{:S(2)}) collective-permute-start(f32[1536,2048]{1,0:T(8,128)} %fusion.38), channel_id=1, source_target_pairs={{0,1},{1,0},{2,3},{3,2},{4,5},{5,4},{6,7},{7,6}} | collective-permute-start | bytes 37748744 | tf_op jit(solution)/shard_map/ppermute | solution.py:345
  1899.5 479.3 %collective-permute-start.19 = (f32[512,5632]{1,0:T(8,128)}, f32[512,5632]{1,0:T(8,128)}, u32[]{:S(2)}, u32[]{:S(2)}) collective-permute-start(f32[512,5632]{1,0:T(8,128)} %fusion.50), channel_id=1, source_target_pairs={{0,4},{1,5},{2,6},{3,7},{4,0},{5,1},{6,2},{7,3}} | collective-permute-start | bytes 34603016 | tf_op jit(solution)/shard_map/ppermute | solution.py:345
  1923.9 209.1 %copy-start.3 = (f32[1536]{0:T(1024)S(1)}, f32[1536]{0:T(1024)}, u32[]{:S(2)}) copy-start(f32[1536]{0:T(1024)} %copy-done.2) | copy-start | bytes 18436
  1923.9 209.1 %copy-start.5 = (f32[1,2,8,128]{3,1,2,0:T(2,128)S(1)}, f32[1,2,8,128]{3,1,2,0:T(2,128)}, u32[]{:S(2)}) copy-start(f32[1,2,8,128]{3,1,2,0:T(2,128)} %copy-done.4) | copy-start | bytes 24580
  1970.7 171.0 %copy-start.10 = (f32[2048]{0:T(1024)S(1)}, f32[2048]{0:T(1024)}, u32[]{:S(2)}) copy-start(f32[2048]{0:T(1024)} %get-tuple-element.171) | copy-start | bytes 24580
  2141.9 71.0 %collective-permute-start.25 = (f32[4,832]{1,0:T(4,128)S(1)}, f32[4,832]{1,0:T(4,128)S(1)}, u32[]{:S(2)}, u32[]{:S(2)}) collective-permute-start(f32[4,832]{1,0:T(4,128)S(1)} %bitcast.97), channel_id=1, source_target_pairs={{0,1},{1,0},{2,3},{3,2},{4,5},{5,4},{6,7},{7,6}} | collective-permute-start | bytes 39944 | tf_op jit(solution)/shard_map/ppermute | solution.py:345
  2212.0 179.5 %collective-permute-start.31 = (f32[256,5632]{1,0:T(8,128)}, f32[256,5632]{1,0:T(8,128)}, u32[]{:S(2)}, u32[]{:S(2)}) collective-permute-start(f32[256,5632]{1,0:T(8,128)} %get-tuple-element.174), channel_id=1, source_target_pairs={{0,3},{1,2},{2,1},{3,0},{4,7},{5,6},{6,5},{7,4}} | collective-permute-start | bytes 17301512 | tf_op jit(solution)/shard_map/ppermute | solution.py:345
  2213.0 165.8 %slice-start.6 = ((s8[11534336]{0:T(1024)(128)(4,1)}), s8[4194304]{0:T(1024)(128)(4,1)S(1)}, s32[]{:S(2)}) async-start(s8[11534336]{0:T(1024)(128)(4,1)} %bitcast.85), calls=%async_computation.12 | async-start | bytes 8388608
  2213.0 165.8 %slice-start.7 = ((s8[11534336]{0:T(1024)(128)(4,1)}), s8[4194304]{0:T(1024)(128)(4,1)S(1)}, s32[]{:S(2)}) async-start(s8[11534336]{0:T(1024)(128)(4,1)} %bitcast.85), calls=%async_computation.13 | async-start | bytes 8388608
  2213.0 165.8 %slice-start.8 = ((s8[11534336]{0:T(1024)(128)(4,1)}), s8[3145728]{0:T(1024)(128)(4,1)S(1)}, s32[]{:S(2)}) async-start(s8[11534336]{0:T(1024)(128)(4,1)} %bitcast.85), calls=%async_computation.14 | async-start | bytes 6291456
  2213.0 125.9 %collective-permute-start.26 = (f32[2,832]{1,0:T(2,128)S(1)}, f32[2,832]{1,0:T(2,128)S(1)}, u32[]{:S(2)}, u32[]{:S(2)}) collective-permute-start(f32[2,832]{1,0:T(2,128)S(1)} %bitcast.98), channel_id=1, source_target_pairs={{0,2},{1,3},{2,0},{3,1},{4,6},{5,7},{6,4},{7,5}} | collective-permute-start | bytes 19976 | tf_op jit(solution)/shard_map/ppermute | solution.py:345
  2386.6 9.8 collective-permute-start.28
  2386.7 3.6 collective-permute-start.27
  (10 other events, 380.9 us)
Sparse Core Ops, SparseCore 0:
  9.8 86.9 all-gather.2
  98.6 83.5 all-gather.4
  1483.1 175.7 reduce-scatter.4
  1662.9 212.4 reduce-scatter.2

commit v4 on v3

--- a/solution.py
+++ b/solution.py
@@ -431,8 +431,8 @@
         def down_grad(a, blk):
             return mm(lax.dynamic_slice(a, (0, blk * f_blk), (group * tokens, f_blk)), dy_all, TN_DIMS)
 
-        def up_grad(m, d_up, chip_id):
-            cols = lax.dynamic_slice(m, (0, chip_id * h_chip), (group * tokens, h_chip))
+        def up_grad(m, d_up, block_id, chips):
+            cols = lax.dynamic_slice(m, (0, block_id * chips * h_chip), (group * tokens, chips * h_chip))
             return mm(cols, d_up, TN_DIMS)
 
         y3 = block(act, 3, wd_all, NN_DIMS)
@@ -447,9 +447,6 @@
         down_sum = hop(down_sum, group)
         d_up = up_back(dy_all, wd_all, gate_low, lin_low)
 
-        far_a = up_grad(m_all, d_up, chip ^ 3)
-        d_up, far_a = after(d_up, far_a)
-        far_a = hop(far_a, group)
         dm3 = block(d_up, 3, w_all, NT_DIMS)
         d_up, dm3 = after(d_up, dm3)
         dm3 = hop(dm3, 1)
@@ -457,27 +454,29 @@
         d_up, dm2 = after(d_up, dm2)
         d_up, dm2 = after(d_up, dm2 + dm3)
         dm2 = hop(dm2, 2)
-        far_b = up_grad(m_all, d_up, chip ^ 2)
+
+        far_a = up_grad(m_all, d_up, chip ^ 3, 1)
+        d_up, far_a = after(d_up, far_a)
+        far_a = hop(far_a, group)
+        far_b = up_grad(m_all, d_up, chip ^ 2, 1)
         d_up, far_b = after(d_up, far_b)
         far_b = hop(far_b, group)
-        near_a = up_grad(m_all, d_up, chip ^ 1)
-        d_up, near_a = after(d_up, near_a)
+        near = up_grad(m_all, d_up, side, 2)
+        d_up, near = after(d_up, near)
         dm1 = block(d_up, 1, w_all, NT_DIMS)
-        d_up, dm1, near_a = after(d_up, dm1, near_a)
+        d_up, dm1 = after(d_up, dm1)
         dm1 = hop(dm1, 1)
         dm0 = block(d_up, 0, w_all, NT_DIMS)
-        d_up, dm0, act = after(d_up, dm0, act)
-        y1 = block(act, 1, wd_all, NN_DIMS)
-        act, d_up, y1 = after(act, d_up, y1)
-        y1 = hop(y1, 1)
-        y0 = block(act, 0, wd_all, NN_DIMS)
-        d_up, y0, dm2 = after(d_up, y0, dm2)
-
-        def rows_of(c, *parts):
-            return sum(lax.dynamic_slice(v, (c * h_loc, 0), (h_loc, 2 * f_pad)) for v in parts)
-
-        piece2 = hop(rows_of(core, near_a, far_a), 2)
-        piece3 = hop(rows_of(1 - core, near_a, far_a), 3)
+        d_up, dm0, act, dm2, near = after(d_up, dm0, act, dm2, near)
+
+        x_id = lax.rem(chip, 2)
+
+        def rows_of(near, x, c, far):
+            own = lax.dynamic_slice(near, (x * h_chip + c * h_loc, 0), (h_loc, 2 * f_pad))
+            return own + lax.dynamic_slice(far, (c * h_loc, 0), (h_loc, 2 * f_pad))
+
+        piece2 = hop(rows_of(near, 1 - x_id, core, far_a), 2)
+        piece3 = hop(rows_of(near, 1 - x_id, 1 - core, far_a), 3)
 
         d_m = dm0 + dm1 + dm2
         grad_mlp_gain = jnp.sum(d_m * mid_wide * inv_two, axis=0)
@@ -491,10 +490,11 @@
         grad_w_qkv, d_proj = after(grad_w_qkv, d_proj)
         grad_w_qkv = scatter_rows(grad_w_qkv)
         d_normed = mm(d_proj, wqkv, NT_DIMS)
-        d_normed, d_up = after(d_normed, d_up)
-        near_b = up_grad(m_all, d_up, chip)
-        near_b, d_normed, act, down_sum = after(near_b, d_normed, act, down_sum)
+        d_normed, act = after(d_normed, act)
+        y1 = hop(block(act, 1, wd_all, NN_DIMS), 1)
+        act, d_normed, y1, down_sum = after(act, d_normed, y1, down_sum)
         grad_w_down = mm(lax.dynamic_slice(act, (0, side * f_blk), (group * tokens, f_blk)), dy_all, TN_DIMS)[:f_loc] + down_sum[:f_loc]
+        grad_w_down, act, near = after(grad_w_down, act, near)
         grad_attn_gain = jnp.sum(d_normed * hid_wide * inv_one, axis=0)
         small_grads = jnp.concatenate([grad_attn_gain.reshape(n_dev, h_loc), grad_b_qkv.reshape(n_dev, q_loc), grad_mlp_gain.reshape(n_dev, h_loc)], axis=1)
 
@@ -506,12 +506,12 @@
         small_grads = halved(halved(small_grads, 1), 2)
         scaled_one = d_normed * gain_one
         grad_hidden = (d_mid + inv_one * (scaled_one - hid_wide * inv_one * inv_one * jnp.mean(scaled_one * hid_wide, axis=-1, keepdims=True))).astype(BF16)
-        y0, y1, y2, mid_late, grad_hidden = after(y0, y1, y2, mid, grad_hidden)
-        output = (mid_late.astype(F32) + (y0 + y1 + y2)).astype(BF16)
+        act, y1, y2, mid, grad_hidden = after(act, y1, y2, mid, grad_hidden)
+        output = (mid.astype(F32) + (block(act, 0, wd_all, NN_DIMS) + y1 + y2)).astype(BF16)
         far_b, output, grad_hidden, grad_w_down, small_grads = after(far_b, output, grad_hidden, grad_w_down, small_grads)
         small_grads = halved(small_grads, group).reshape(-1)
-        piece0 = rows_of(core, near_b, far_b)
-        piece1 = hop(rows_of(1 - core, near_b, far_b), 1)
+        piece0 = rows_of(near, x_id, core, far_b)
+        piece1 = hop(rows_of(near, x_id, 1 - core, far_b), 1)
         grad_w_up = join_up([piece0, piece1, piece2, piece3], rank, group, f_loc)
         return (output.reshape(hidden.shape), grad_hidden.reshape(hidden.shape), small_grads[:h_loc], grad_w_qkv, small_grads[h_loc:h_loc + q_loc], grad_w_out, small_grads[h_loc + q_loc:], grad_w_up, grad_w_down)
 

time: 2430 us -> 2500 us (1.029)
  waiting for transfers between devices: 1040 us -> 1110 us
    ppermute x32, waiting for transfers between devices: 969 us -> 1040 us  [hop(): return lax.ppermute(v, ax, [(i, i ^ k) for i in range(n_dev)])]
    dot_general x20 -> x19, matrix products: 696 us -> 685 us  [mm(): return lax.dot_general(a, b, dims, preferred_element_type=F32)]
  transfers between devices with their start and end apart: 36 -> 36, of which waited for: 14 -> 14; matrix products, arithmetic and copies ran while one was open for 23% -> 23% of each run, Pallas kernels for 12% -> 11%
where the time goes in v4:
time: 2500 us; the launch traced here: 2490 us
  waiting for transfers between devices  1110 us (44%)
  matrix products  685 us (27%)
  Pallas kernels  395 us (16%)
  other arithmetic  141 us (6%)
  local copies, waits for them, and re-layouts  123 us (5%)
    ppermute x32, waiting for transfers between devices, hop(): return lax.ppermute(v, ax, [(i, i ^ k) for i in range(n_dev)])  1040 us
    dot_general x19, matrix products, mm(): return lax.dot_general(a, b, dims, preferred_element_type=F32)  685 us
    pallas_call x1, Pallas kernels, up_act(): pl.pallas_call(up_kernel, grid=(tokens // T_BLOCK,), in_specs=[pl.BlockSp...  169 us
    pallas_call x1, Pallas kernels, up_back(): pl.pallas_call(up_back_kernel, grid=(tokens // T_BLOCK,), in_specs=[pl.Bl...  112 us
    all_gather x2, waiting for transfers between devices, gather_rows(): return lax.all_gather(shard, ax, axis=0, tiled=True)  67.1 us
  transfers between devices with their start and end apart: 36, of which 14 were waited for; matrix products, arithmetic and copies ran while one was open for 23% of the time, Pallas kernels for 11%

profile of v4, /device:TPU:0, one launch (start us, length us, event | category | flops | bytes accessed | tf_op | source)
XLA Modules:
  0.0 2494.7 jit_solution(10956401457957398440)
XLA Ops:
  25.0 13.5 split_up.1
  40.9 14.2 dynamic_update_slice.56
  59.4 37.0 %all-gather.3.cloned.1.call-done = bf16[2048,2560]{1,0:T(8,128)(2,1)} async-done(((bf16[256,2560]{1,0:T(8,128)(2,1)}), bf16[2048,2560]{1,0:T(8,128)(2,1)}) %all-gather.3.cloned.1.call-update) | async-done | bytes 10485776 | tf_op jit(solution)/shard_map/all_gather | solution.py:348
  96.4 22.4 convolution_add_fusion.z_ref
  118.8 33.2 %attend.1 = (bf16[1536,2560]{1,0:T(8,128)(2,1)}, bf16[1536,2048]{1,0:T(8,128)(2,1)}) custom-call(f32[1536,2560]{1,0:T(8,128)} %convolution_add_fusion.z_ref, f32[1536,128]{1,0:T(8,128)S(1)} %get-tuple-element.179.cos_ref, f32[1536,128]{1,0:T(8,128)S(1)} %get-tuple-element.178.sin_ref), custom_call_target="tpu_custom_call" | custom-call | flops 19327352832 | bytes 31457280 | tf_op jit(solution)/shard_map/attend/pallas_call | solution.py:159
  152.0 30.1 %all-gather.5.cloned.1.call-done = bf16[2048,2048]{1,0:T(8,128)(2,1)} async-done(((bf16[256,2048]{1,0:T(8,128)(2,1)}), bf16[2048,2048]{1,0:T(8,128)(2,1)}) %all-gather.5.cloned.1.call-update) | async-done | bytes 8388624 | tf_op jit(solution)/shard_map/all_gather | solution.py:348
  182.0 18.9 fusion.19
  202.7 8.0 broadcast_in_dim.37
  241.9 49.1 %collective-permute-done.9 = bf16[256,5632]{1,0:T(8,128)(2,1)S(1)} collective-permute-done((bf16[256,5632]{1,0:T(8,128)(2,1)}, bf16[256,5632]{1,0:T(8,128)(2,1)S(1)}, u32[]{:S(2)}, u32[]{:S(2)}) %collective-permute-start.9) | collective-permute-done | bytes 2883616 | tf_op jit(solution)/shard_map/ppermute | solution.py:345
  292.8 59.2 %collective-permute-done.10 = bf16[256,5632]{1,0:T(8,128)(2,1)S(1)} collective-permute-done((bf16[256,5632]{1,0:T(8,128)(2,1)}, bf16[256,5632]{1,0:T(8,128)(2,1)S(1)}, u32[]{:S(2)}, u32[]{:S(2)}) %collective-permute-start.10) | collective-permute-done | bytes 2883616 | tf_op jit(solution)/shard_map/ppermute | solution.py:345
  360.3 18.6 dynamic_update_slice.54
  394.7 56.4 %collective-permute-done.13 = bf16[256,5632]{1,0:T(8,128)(2,1)} collective-permute-done((bf16[256,5632]{1,0:T(8,128)(2,1)}, bf16[256,5632]{1,0:T(8,128)(2,1)}, u32[]{:S(2)}, u32[]{:S(2)}) %collective-permute-start.13) | collective-permute-done | bytes 2883616 | tf_op jit(solution)/shard_map/ppermute | solution.py:345
  454.7 6.6 constant_dynamic-update-slice_fusion.4.m_ref
  461.3 169.0 %up_act.1 = (bf16[6144,2816]{1,0:T(8,128)(2,1)}, bf16[6144,2816]{1,0:T(8,128)(2,1)}, bf16[6144,2816]{1,0:T(8,128)(2,1)}) custom-call(bf16[6144,2048]{1,0:T(8,128)(2,1)} %constant_dynamic-update-slice_fusion.4.m_ref, bf16[2048,5632]{1,0:T(8,128)(2,1)} %constant_dynamic-update-slice_fusion.3.w_ref), custom_call_target="tpu_custom_call" | custom-call | flops 141733920768 | bytes 152043520 | tf_op jit(solution)/shard_map/up_act/pallas_call | solution.py:206
  636.3 25.1 %fusion.44 = f32[1536,2048]{1,0:T(8,128)} fusion(bf16[2816,2048]{1,0:T(8,128)(2,1)} %constant_dynamic-update-slice_fusion.2.wd_ref, bf16[6144,2816]{1,0:T(8,128)(2,1)} %get-tuple-element.149), kind=kOutput, calls=%fused_computation.57 | convolution fusion | flops 17716740096 | bytes 32768000 | tf_op jit(solution)/shard_map/dot_general | solution.py:32
  661.9 24.7 fusion.42
  693.1 6.6 constant_dynamic-update-slice_fusion.dy_ref
  699.7 10.9 add.224
  710.6 46.2 %fusion.10 = f32[1408,2048]{1,0:T(8,128)} fusion(bf16[6144,2048]{1,0:T(8,128)(2,1)} %constant_dynamic-update-slice_fusion.dy_ref, bf16[6144,2816]{1,0:T(8,128)(2,1)} %get-tuple-element.149, s32[]{:T(128)S(6)} %select_n.165), kind=kOutput, calls=%fused_computation.14 | convolution fusion | flops 35433480192 | bytes 54001668 | tf_op jit(solution)/shard_map/dot_general | solution.py:32
  756.8 112.1 %up_back.1 = bf16[6144,5632]{1,0:T(8,128)(2,1)} custom-call(bf16[6144,2048]{1,0:T(8,128)(2,1)} %constant_dynamic-update-slice_fusion.dy_ref, bf16[2816,2048]{1,0:T(8,128)(2,1)} %constant_dynamic-update-slice_fusion.2.wd_ref, bf16[6144,2816]{1,0:T(8,128)(2,1)} %get-tuple-element.116.g_ref, bf16[6144,2816]{1,0:T(8,128)(2,1)} %get-tuple-element.117.l_ref), custom_call_target="tpu_custom_call" | custom-call | flops 70866960384 | bytes 175112192 | tf_op jit(solution)/shard_map/up_back/pallas_call | solution.py:234
  868.9 44.8 %fusion.2 = f32[1536,2048]{1,0:T(8,128)} fusion(bf16[2048,5632]{1,0:T(8,128)(2,1)} %constant_dynamic-update-slice_fusion.3.w_ref, bf16[6144,5632]{1,0:T(8,128)(2,1)} %up_back.1), kind=kOutput, calls=%fused_computation.6 | convolution fusion | flops 35433480192 | bytes 52953088 | tf_op jit(solution)/shard_map/dot_general | solution.py:32
  913.7 45.1 %fusion.8 = f32[1536,2048]{1,0:T(8,128)} fusion(bf16[2048,5632]{1,0:T(8,128)(2,1)} %constant_dynamic-update-slice_fusion.3.w_ref, bf16[6144,5632]{1,0:T(8,128)(2,1)} %up_back.1), kind=kOutput, calls=%fused_computation.12 | convolution fusion | flops 35433480192 | bytes 52953088 | tf_op jit(solution)/shard_map/dot_general | solution.py:32
  958.8 14.5 add.225
  973.3 46.9 %fusion.50 = f32[512,5632]{1,0:T(8,128)} fusion(bf16[6144,5632]{1,0:T(8,128)(2,1)} %up_back.1, bf16[6144,2048]{1,0:T(8,128)(2,1)} %constant_dynamic-update-slice_fusion.4.m_ref, s32[]{:T(128)S(6)} %select_n.166), kind=kOutput, calls=%fused_computation.62 | convolution fusion | flops 35433480192 | bytes 87031808 | tf_op jit(solution)/shard_map/dot_general | solution.py:32
  1020.2 46.8 %fusion.48 = f32[512,5632]{1,0:T(8,128)} fusion(bf16[6144,5632]{1,0:T(8,128)(2,1)} %up_back.1, bf16[6144,2048]{1,0:T(8,128)(2,1)} %constant_dynamic-update-slice_fusion.4.m_ref, s32[]{:T(128)S(6)} %select_n.167), kind=kOutput, calls=%fused_computation.60 | convolution fusion | flops 35433480192 | bytes 87031808 | tf_op jit(solution)/shard_map/dot_general | solution.py:32
  1067.0 81.8 %fusion.36 = f32[1024,5632]{1,0:T(8,128)} fusion(bf16[6144,5632]{1,0:T(8,128)(2,1)} %up_back.1, bf16[6144,2048]{1,0:T(8,128)(2,1)} %constant_dynamic-update-slice_fusion.4.m_ref, s32[]{:T(128)S(6)} %select_n.168), kind=kOutput, calls=%fused_computation.48 | convolution fusion | flops 70866960384 | bytes 104857600 | tf_op jit(solution)/shard_map/dot_general | solution.py:32
  1149.4 44.9 %fusion.6 = f32[1536,2048]{1,0:T(8,128)} fusion(bf16[2048,5632]{1,0:T(8,128)(2,1)} %constant_dynamic-update-slice_fusion.3.w_ref, bf16[6144,5632]{1,0:T(8,128)(2,1)} %up_back.1), kind=kOutput, calls=%fused_computation.10 | convolution fusion | flops 35433480192 | bytes 52953088 | tf_op jit(solution)/shard_map/dot_general | solution.py:32
  1194.6 44.6 %fusion.4 = f32[1536,2048]{1,0:T(8,128)} fusion(bf16[2048,5632]{1,0:T(8,128)(2,1)} %constant_dynamic-update-slice_fusion.3.w_ref, bf16[6144,5632]{1,0:T(8,128)(2,1)} %up_back.1), kind=kOutput, calls=%fused_computation.8 | convolution fusion | flops 35433480192 | bytes 52953088 | tf_op jit(solution)/shard_map/dot_general | solution.py:32
  1239.2 182.6 %collective-permute-done.20 = f32[1536,2048]{1,0:T(8,128)} collective-permute-done((f32[1536,2048]{1,0:T(8,128)}, f32[1536,2048]{1,0:T(8,128)}, u32[]{:S(2)}, u32[]{:S(2)}) %collective-permute-start.20) | collective-permute-done | bytes 12582944 | tf_op jit(solution)/shard_map/ppermute | solution.py:345
  1421.9 21.3 fusion.22
  1443.1 12.2 fusion.18
  1455.3 21.7 fusion.52
  1477.1 21.4 convolution_convert_fusion.dctx_ref
  1498.5 46.5 %attend_back.1 = (bf16[1536,2560]{1,0:T(8,128)(2,1)}, f32[1,2560]{1,0:T(1,128)S(1)}) custom-call(bf16[1536,2560]{1,0:T(8,128)(2,1)} %get-tuple-element.125.qkv_ref, bf16[1536,2048]{1,0:T(8,128)(2,1)} %convolution_convert_fusion.dctx_ref, f32[1536,128]{1,0:T(8,128)S(1)} %get-tuple-element.179.cos_ref, f32[1536,128]{1,0:T(8,128)S(1)} %get-tuple-element.178.sin_ref), custom_call_target="tpu_custom_call" | custom-call | flops 48318382080 | bytes 31457280 | tf_op jit(solution)/shard_map/attend_back/pallas_call | solution.py:177
  1545.1 22.1 fusion.68
  1567.2 23.2 fusion.69
  1590.4 24.7 fusion.40
  1618.9 331.5 %collective-permute-done.29 = f32[512,5632]{1,0:T(8,128)} collective-permute-done((f32[512,5632]{1,0:T(8,128)}, f32[512,5632]{1,0:T(8,128)}, u32[]{:S(2)}, u32[]{:S(2)}) %collective-permute-start.29) | collective-permute-done | bytes 11534368 | tf_op jit(solution)/shard_map/ppermute | solution.py:345
  1950.4 12.8 dynamic-slice_add_fusion
  1963.8 233.8 %collective-permute-done.23 = f32[1408,2048]{1,0:T(8,128)} collective-permute-done((f32[1408,2048]{1,0:T(8,128)}, f32[1408,2048]{1,0:T(8,128)}, u32[]{:S(2)}, u32[]{:S(2)}) %collective-permute-start.23) | collective-permute-done | bytes 11534368 | tf_op jit(solution)/shard_map/ppermute | solution.py:345
  2197.6 9.0 fusion.35
  2207.3 55.4 %slice_add_fusion = f32[1376,2048]{1,0:T(8,128)} fusion(f32[1408,2048]{1,0:T(8,128)} %collective-permute-done.23, bf16[6144,2048]{1,0:T(8,128)(2,1)} %constant_dynamic-update-slice_fusion.dy_ref, bf16[6144,2816]{1,0:T(8,128)(2,1)} %get-tuple-element.149, s32[]{:T(128)S(6)} %select_n.163), kind=kOutput, calls=%fused_computation.50 | convolution fusion | flops 34630991872 | bytes 65011716 | tf_op jit(solution)/shard_map/dot_general | solution.py:32
  2262.8 14.4 fusion.30
  2277.2 24.7 fusion.38
  2303.6 18.3 add_convert_fusion
  2323.3 121.0 %collective-permute-done.19 = f32[512,5632]{1,0:T(8,128)} collective-permute-done((f32[512,5632]{1,0:T(8,128)}, f32[512,5632]{1,0:T(8,128)}, u32[]{:S(2)}, u32[]{:S(2)}) %collective-permute-start.19) | collective-permute-done | bytes 11534368 | tf_op jit(solution)/shard_map/ppermute | solution.py:345
  2444.3 12.9 dynamic-slice_add_fusion.2
  2467.0 21.0 join_up.1
  (157 shorter events, 118.4 us)
Async XLA Ops:
  7.2 89.2 %all-gather.3.cloned.1.call-start = ((), (), s32[]{:S(2)}) async-start(), calls=%async_computation.2 | async-start | bytes 11796480 | tf_op jit(solution)/shard_map/all_gather | solution.py:348
  7.9 174.1 %all-gather.5.cloned.1.call-start = ((), (), s32[]{:S(2)}) async-start(), calls=%async_computation.3 | async-start | bytes 9437184 | tf_op jit(solution)/shard_map/all_gather | solution.py:348
  8.7 2479.4 %reduce-scatter.5.cloned.1.call-start = ((), (), s32[]{:S(2)}) async-start(), calls=%async_computation.5 | async-start | bytes 18874368 | tf_op jit(solution)/shard_map/reduce_scatter | solution.py:351
  9.5 8.8 collective-permute-start
  18.3 4.6 collective-permute-start.1
  21.1 34.0 %copy-start.4 = (f32[1536]{0:T(1024)}, f32[1536]{0:T(1024)S(1)}, u32[]{:S(2)}) copy-start(f32[1536]{0:T(1024)S(1)} %rsqrt.20) | copy-start | bytes 18436
  22.9 15.6 collective-permute-start.2
  38.5 164.0 %collective-permute-start.5 = (bf16[256,5632]{1,0:T(8,128)(2,1)}, bf16[256,5632]{1,0:T(8,128)(2,1)}, u32[]{:S(2)}, u32[]{:S(2)}) collective-permute-start(bf16[256,5632]{1,0:T(8,128)(2,1)} %get-tuple-element.94), channel_id=1, source_target_pairs={{0,1},{1,0},{2,3},{3,2},{4,5},{5,4},{6,7},{7,6}} | collective-permute-start | bytes 8650760 | tf_op jit(solution)/shard_map/ppermute | solution.py:345
  38.6 174.2 %collective-permute-start.6 = (bf16[256,5632]{1,0:T(8,128)(2,1)}, bf16[256,5632]{1,0:T(8,128)(2,1)}, u32[]{:S(2)}, u32[]{:S(2)}) collective-permute-start(bf16[256,5632]{1,0:T(8,128)(2,1)} %get-tuple-element.95), channel_id=1, source_target_pairs={{0,2},{1,3},{2,0},{3,1},{4,6},{5,7},{6,4},{7,5}} | collective-permute-start | bytes 8650760 | tf_op jit(solution)/shard_map/ppermute | solution.py:345
  40.0 185.5 %collective-permute-start.7 = (bf16[256,5632]{1,0:T(8,128)(2,1)}, bf16[256,5632]{1,0:T(8,128)(2,1)}, u32[]{:S(2)}, u32[]{:S(2)}) collective-permute-start(bf16[256,5632]{1,0:T(8,128)(2,1)} %get-tuple-element.96), channel_id=1, source_target_pairs={{0,3},{1,2},{2,1},{3,0},{4,7},{5,6},{6,5},{7,4}} | collective-permute-start | bytes 8650760 | tf_op jit(solution)/shard_map/ppermute | solution.py:345
  40.4 190.2 %collective-permute-start.8 = (bf16[256,5632]{1,0:T(8,128)(2,1)}, bf16[256,5632]{1,0:T(8,128)(2,1)}, u32[]{:S(2)}, u32[]{:S(2)}) collective-permute-start(bf16[256,5632]{1,0:T(8,128)(2,1)} %get-tuple-element.93), channel_id=1, source_target_pairs={{0,4},{1,5},{2,6},{3,7},{4,0},{5,1},{6,2},{7,3}} | collective-permute-start | bytes 8650760 | tf_op jit(solution)/shard_map/ppermute | solution.py:345
  40.7 14.5 copy-start.6
  40.7 160.2 %copy-start.8 = (f32[1,2,8,128]{3,1,2,0:T(2,128)}, f32[1,2,8,128]{3,1,2,0:T(2,128)S(1)}, u32[]{:S(2)}) copy-start(f32[1,2,8,128]{3,1,2,0:T(2,128)S(1)} %copy.24) | copy-start | bytes 24580
  40.8 313.0 %collective-permute-start.4 = (bf16[1536,2048]{1,0:T(8,128)(2,1)}, bf16[1536,2048]{1,0:T(8,128)(2,1)}, u32[]{:S(2)}, u32[]{:S(2)}) collective-permute-start(bf16[1536,2048]{1,0:T(8,128)(2,1)} %bitcast.78), channel_id=1, source_target_pairs={{0,1},{1,0},{2,3},{3,2},{4,5},{5,4},{6,7},{7,6}} | collective-permute-start | bytes 18874376 | tf_op jit(solution)/shard_map/ppermute | solution.py:345
  202.5 176.4 %collective-permute-start.3 = (bf16[1536,2048]{1,0:T(8,128)(2,1)S(1)}, bf16[1536,2048]{1,0:T(8,128)(2,1)}, u32[]{:S(2)}, u32[]{:S(2)}) collective-permute-start(bf16[1536,2048]{1,0:T(8,128)(2,1)S(1)} %fusion.14), channel_id=1, source_target_pairs={{0,1},{1,0},{2,3},{3,2},{4,5},{5,4},{6,7},{7,6}} | collective-permute-start | bytes 18874376 | tf_op jit(solution)/shard_map/ppermute | solution.py:345
  212.8 172.6 %collective-permute-start.11 = (bf16[1536,2048]{1,0:T(8,128)(2,1)S(1)}, bf16[1536,2048]{1,0:T(8,128)(2,1)}, u32[]{:S(2)}, u32[]{:S(2)}) collective-permute-start(bf16[1536,2048]{1,0:T(8,128)(2,1)S(1)} %fusion.14), channel_id=1, source_target_pairs={{0,2},{1,3},{2,0},{3,1},{4,6},{5,7},{6,4},{7,5}} | collective-permute-start | bytes 18874376 | tf_op jit(solution)/shard_map/ppermute | solution.py:345
  225.5 65.6 %collective-permute-start.9 = (bf16[256,5632]{1,0:T(8,128)(2,1)}, bf16[256,5632]{1,0:T(8,128)(2,1)S(1)}, u32[]{:S(2)}, u32[]{:S(2)}) collective-permute-start(bf16[256,5632]{1,0:T(8,128)(2,1)} %collective-permute-done.5), channel_id=1, source_target_pairs={{0,4},{1,5},{2,6},{3,7},{4,0},{5,1},{6,2},{7,3}} | collective-permute-start | bytes 8650760 | tf_op jit(solution)/shard_map/ppermute | solution.py:345
  230.6 121.4 %collective-permute-start.10 = (bf16[256,5632]{1,0:T(8,128)(2,1)}, bf16[256,5632]{1,0:T(8,128)(2,1)S(1)}, u32[]{:S(2)}, u32[]{:S(2)}) collective-permute-start(bf16[256,5632]{1,0:T(8,128)(2,1)} %collective-permute-done.6), channel_id=1, source_target_pairs={{0,4},{1,5},{2,6},{3,7},{4,0},{5,1},{6,2},{7,3}} | collective-permute-start | bytes 8650760 | tf_op jit(solution)/shard_map/ppermute | solution.py:345
  385.4 69.2 %collective-permute-start.12 = (bf16[1536,2048]{1,0:T(8,128)(2,1)}, bf16[1536,2048]{1,0:T(8,128)(2,1)}, u32[]{:S(2)}, u32[]{:S(2)}) collective-permute-start(bf16[1536,2048]{1,0:T(8,128)(2,1)} %collective-permute-done.11), channel_id=1, source_target_pairs={{0,1},{1,0},{2,3},{3,2},{4,5},{5,4},{6,7},{7,6}} | collective-permute-start | bytes 18874376 | tf_op jit(solution)/shard_map/ppermute | solution.py:345
  385.4 65.7 %collective-permute-start.13 = (bf16[256,5632]{1,0:T(8,128)(2,1)}, bf16[256,5632]{1,0:T(8,128)(2,1)}, u32[]{:S(2)}, u32[]{:S(2)}) collective-permute-start(bf16[256,5632]{1,0:T(8,128)(2,1)} %collective-permute-done.7), channel_id=1, source_target_pairs={{0,4},{1,5},{2,6},{3,7},{4,0},{5,1},{6,2},{7,3}} | collective-permute-start | bytes 8650760 | tf_op jit(solution)/shard_map/ppermute | solution.py:345
  387.1 243.2 %collective-permute-start.14 = (bf16[1536,2048]{1,0:T(8,128)(2,1)}, bf16[1536,2048]{1,0:T(8,128)(2,1)}, u32[]{:S(2)}, u32[]{:S(2)}) collective-permute-start(bf16[1536,2048]{1,0:T(8,128)(2,1)} %bitcast.80), channel_id=1, source_target_pairs={{0,2},{1,3},{2,0},{3,1},{4,6},{5,7},{6,4},{7,5}} | collective-permute-start | bytes 18874376 | tf_op jit(solution)/shard_map/ppermute | solution.py:345
  387.6 242.7 %collective-permute-start.15 = (bf16[1376,2048]{1,0:T(8,128)(2,1)}, bf16[1376,2048]{1,0:T(8,128)(2,1)}, u32[]{:S(2)}, u32[]{:S(2)}) collective-permute-start(bf16[1376,2048]{1,0:T(8,128)(2,1)} %param.19), channel_id=1, source_target_pairs={{0,4},{1,5},{2,6},{3,7},{4,0},{5,1},{6,2},{7,3}} | collective-permute-start | bytes 16908296 | tf_op jit(solution)/shard_map/ppermute | solution.py:345
  661.4 38.3 %collective-permute-start.17 = (f32[1536,2048]{1,0:T(8,128)}, f32[1536,2048]{1,0:T(8,128)S(1)}, u32[]{:S(2)}, u32[]{:S(2)}) collective-permute-start(f32[1536,2048]{1,0:T(8,128)} %fusion.44), channel_id=1, source_target_pairs={{0,1},{1,0},{2,3},{3,2},{4,5},{5,4},{6,7},{7,6}} | collective-permute-start | bytes 37748744 | tf_op jit(solution)/shard_map/ppermute | solution.py:345
  661.4 31.7 %collective-permute-start.16 = (bf16[1536,2048]{1,0:T(8,128)(2,1)}, bf16[1536,2048]{1,0:T(8,128)(2,1)}, u32[]{:S(2)}, u32[]{:S(2)}) collective-permute-start(bf16[1536,2048]{1,0:T(8,128)(2,1)} %collective-permute-done.14), channel_id=1, source_target_pairs={{0,1},{1,0},{2,3},{3,2},{4,5},{5,4},{6,7},{7,6}} | collective-permute-start | bytes 18874376 | tf_op jit(solution)/shard_map/ppermute | solution.py:345
  913.7 45.1 %collective-permute-start.18 = (f32[1536,2048]{1,0:T(8,128)}, f32[1536,2048]{1,0:T(8,128)}, u32[]{:S(2)}, u32[]{:S(2)}) collective-permute-start(f32[1536,2048]{1,0:T(8,128)} %fusion.2), channel_id=1, source_target_pairs={{0,1},{1,0},{2,3},{3,2},{4,5},{5,4},{6,7},{7,6}} | collective-permute-start | bytes 37748744 | tf_op jit(solution)/shard_map/ppermute | solution.py:345
  1148.8 273.0 %collective-permute-start.20 = (f32[1536,2048]{1,0:T(8,128)}, f32[1536,2048]{1,0:T(8,128)}, u32[]{:S(2)}, u32[]{:S(2)}) collective-permute-start(f32[1536,2048]{1,0:T(8,128)} %add.225), channel_id=1, source_target_pairs={{0,2},{1,3},{2,0},{3,1},{4,6},{5,7},{6,4},{7,5}} | collective-permute-start | bytes 37748744 | tf_op jit(solution)/shard_map/ppermute | solution.py:345
  1194.3 227.6 %copy-start.9 = (f32[1,2,8,128]{3,1,2,0:T(2,128)S(1)}, f32[1,2,8,128]{3,1,2,0:T(2,128)}, u32[]{:S(2)}) copy-start(f32[1,2,8,128]{3,1,2,0:T(2,128)} %copy-done.8) | copy-start | bytes 24580
  1194.3 227.5 %copy-start.11 = (f32[1536]{0:T(1024)S(1)}, f32[1536]{0:T(1024)}, u32[]{:S(2)}) copy-start(f32[1536]{0:T(1024)} %copy-done.10) | copy-start | bytes 18436
  1194.3 227.5 %collective-permute-start.21 = (f32[1536,2048]{1,0:T(8,128)}, f32[1536,2048]{1,0:T(8,128)}, u32[]{:S(2)}, u32[]{:S(2)}) collective-permute-start(f32[1536,2048]{1,0:T(8,128)} %fusion.6), channel_id=1, source_target_pairs={{0,1},{1,0},{2,3},{3,2},{4,5},{5,4},{6,7},{7,6}} | collective-permute-start | bytes 37748744 | tf_op jit(solution)/shard_map/ppermute | solution.py:345
  1239.2 203.9 %copy-start.1 = (bf16[1536,2048]{1,0:T(8,128)(2,1)S(1)}, bf16[1536,2048]{1,0:T(8,128)(2,1)}, u32[]{:S(2)}) copy-start(bf16[1536,2048]{1,0:T(8,128)(2,1)} %copy-done) | copy-start | bytes 18874372
  1239.2 203.9 %copy-start.2 = (bf16[3,512,2048]{2,1,0:T(8,128)(2,1)S(1)}, bf16[3,512,2048]{2,1,0:T(8,128)(2,1)}, u32[]{:S(2)}) copy-start(bf16[3,512,2048]{2,1,0:T(8,128)(2,1)} %param.12) | copy-start | bytes 18874372
  1477.0 1011.0 %reduce-scatter.3.cloned.1.call-start = ((), (), s32[]{:S(2)}) async-start(), calls=%async_computation.4 | async-start | bytes 23592960 | tf_op jit(solution)/shard_map/reduce_scatter | solution.py:351
  1477.1 68.0 %slice-start.2 = ((s8[6291456]{0:T(1024)(128)(4,1)}), s8[2097152]{0:T(1024)(128)(4,1)S(1)}, s32[]{:S(2)}) async-start(s8[6291456]{0:T(1024)(128)(4,1)} %bitcast.83), calls=%async_computation.8 | async-start | bytes 4194304
  1498.5 46.5 %slice-start.3 = ((s8[6291456]{0:T(1024)(128)(4,1)}), s8[4194304]{0:T(1024)(128)(4,1)S(1)}, s32[]{:S(2)}) async-start(s8[6291456]{0:T(1024)(128)(4,1)} %bitcast.83), calls=%async_computation.9 | async-start | bytes 8388608
  1615.1 582.5 %collective-permute-start.22 = (f32[1536,2048]{1,0:T(8,128)}, f32[1536,2048]{1,0:T(8,128)}, u32[]{:S(2)}, u32[]{:S(2)}) collective-permute-start(f32[1536,2048]{1,0:T(8,128)} %fusion.40), channel_id=1, source_target_pairs={{0,1},{1,0},{2,3},{3,2},{4,5},{5,4},{6,7},{7,6}} | collective-permute-start | bytes 37748744 | tf_op jit(solution)/shard_map/ppermute | solution.py:345
  1615.1 335.3 %collective-permute-start.29 = (f32[512,5632]{1,0:T(8,128)}, f32[512,5632]{1,0:T(8,128)}, u32[]{:S(2)}, u32[]{:S(2)}) collective-permute-start(f32[512,5632]{1,0:T(8,128)} %fusion.50), channel_id=1, source_target_pairs={{0,4},{1,5},{2,6},{3,7},{4,0},{5,1},{6,2},{7,3}} | collective-permute-start | bytes 34603016 | tf_op jit(solution)/shard_map/ppermute | solution.py:345
  1616.4 581.1 %collective-permute-start.23 = (f32[1408,2048]{1,0:T(8,128)}, f32[1408,2048]{1,0:T(8,128)}, u32[]{:S(2)}, u32[]{:S(2)}) collective-permute-start(f32[1408,2048]{1,0:T(8,128)} %fusion.10), channel_id=1, source_target_pairs={{0,4},{1,5},{2,6},{3,7},{4,0},{5,1},{6,2},{7,3}} | collective-permute-start | bytes 34603016 | tf_op jit(solution)/shard_map/ppermute | solution.py:345
  1617.1 660.0 %collective-permute-start.24 = (f32[1536,2048]{1,0:T(8,128)}, f32[1536,2048]{1,0:T(8,128)}, u32[]{:S(2)}, u32[]{:S(2)}) collective-permute-start(f32[1536,2048]{1,0:T(8,128)} %add.224), channel_id=1, source_target_pairs={{0,2},{1,3},{2,0},{3,1},{4,6},{5,7},{6,4},{7,5}} | collective-permute-start | bytes 37748744 | tf_op jit(solution)/shard_map/ppermute | solution.py:345
  1617.6 346.2 %copy-start.12 = (f32[2048]{0:T(1024)S(1)}, f32[2048]{0:T(1024)}, u32[]{:S(2)}) copy-start(f32[2048]{0:T(1024)} %get-tuple-element.165) | copy-start | bytes 24580
  1617.6 580.0 %copy-start.5 = (f32[1536]{0:T(1024)S(1)}, f32[1536]{0:T(1024)}, u32[]{:S(2)}) copy-start(f32[1536]{0:T(1024)} %copy-done.4) | copy-start | bytes 18436
  1617.6 580.0 %copy-start.7 = (f32[1,2,8,128]{3,1,2,0:T(2,128)S(1)}, f32[1,2,8,128]{3,1,2,0:T(2,128)}, u32[]{:S(2)}) copy-start(f32[1,2,8,128]{3,1,2,0:T(2,128)} %copy-done.6) | copy-start | bytes 24580
  1617.6 826.7 %collective-permute-start.19 = (f32[512,5632]{1,0:T(8,128)}, f32[512,5632]{1,0:T(8,128)}, u32[]{:S(2)}, u32[]{:S(2)}) collective-permute-start(f32[512,5632]{1,0:T(8,128)} %fusion.48), channel_id=1, source_target_pairs={{0,4},{1,5},{2,6},{3,7},{4,0},{5,1},{6,2},{7,3}} | collective-permute-start | bytes 34603016 | tf_op jit(solution)/shard_map/ppermute | solution.py:345
  1963.2 498.9 %collective-permute-start.30 = (f32[256,5632]{1,0:T(8,128)}, f32[256,5632]{1,0:T(8,128)}, u32[]{:S(2)}, u32[]{:S(2)}) collective-permute-start(f32[256,5632]{1,0:T(8,128)} %get-tuple-element.169), channel_id=1, source_target_pairs={{0,2},{1,3},{2,0},{3,1},{4,6},{5,7},{6,4},{7,5}} | collective-permute-start | bytes 17301512 | tf_op jit(solution)/shard_map/ppermute | solution.py:345
  2197.6 264.5 %collective-permute-start.31 = (f32[256,5632]{1,0:T(8,128)}, f32[256,5632]{1,0:T(8,128)}, u32[]{:S(2)}, u32[]{:S(2)}) collective-permute-start(f32[256,5632]{1,0:T(8,128)} %get-tuple-element.168), channel_id=1, source_target_pairs={{0,3},{1,2},{2,1},{3,0},{4,7},{5,6},{6,5},{7,4}} | collective-permute-start | bytes 17301512 | tf_op jit(solution)/shard_map/ppermute | solution.py:345
  2206.8 95.1 %collective-permute-start.25 = (f32[4,832]{1,0:T(4,128)S(1)}, f32[4,832]{1,0:T(4,128)S(1)}, u32[]{:S(2)}, u32[]{:S(2)}) collective-permute-start(f32[4,832]{1,0:T(4,128)S(1)} %bitcast.91), channel_id=1, source_target_pairs={{0,1},{1,0},{2,3},{3,2},{4,5},{5,4},{6,7},{7,6}} | collective-permute-start | bytes 39944 | tf_op jit(solution)/shard_map/ppermute | solution.py:345
  2302.0 21.3 collective-permute-start.26
  2457.2 9.8 collective-permute-start.28
  2457.2 3.6 collective-permute-start.27
  (5 other events, 57.5 us)
Sparse Core Ops, SparseCore 0:
  9.8 86.5 all-gather.2
  98.2 83.7 all-gather.4
  1477.1 107.8 reduce-scatter.4
  1617.3 216.7 reduce-scatter.2

commit v5 on v4

--- a/solution.py
+++ b/solution.py
@@ -187,7 +187,8 @@
     )(qkv, d_ctx, cos_t, sin_t)
 
 
-def up_kernel(m_ref, w_ref, g_ref, l_ref, a_ref):
+def up_kernel(m_ref, w_ref, *refs):
+    g_ref, l_ref, a_ref = refs[-3:]
     f_pad = g_ref.shape[1]
     for j in range(0, f_pad, F_BLOCK):
         c = slice(j, j + F_BLOCK)
@@ -199,20 +200,22 @@
         a_ref[:, c] = (gate * (1.0 / (1.0 + jnp.exp(-gate))) * lin_low.astype(F32)).astype(BF16)
 
 
-def up_act(m, w):
+def up_act(m, w, half, filled=()):
     tokens, width = m.shape
     f_pad = w.shape[1] // 2
-    row = lambda i: (i, 0)
+    steps = tokens // 2 // T_BLOCK
+    row = lambda i: (i + half * steps, 0)
     return pl.pallas_call(
         up_kernel,
-        grid=(tokens // T_BLOCK,),
-        in_specs=[pl.BlockSpec((T_BLOCK, width), row), pl.BlockSpec(w.shape, lambda i: (0, 0), pipeline_mode=pl.Buffered(1))],
+        grid=(steps,),
+        in_specs=[pl.BlockSpec((T_BLOCK, width), row), pl.BlockSpec(w.shape, lambda i: (0, 0), pipeline_mode=pl.Buffered(1))] + [pl.BlockSpec(memory_space=pl.ANY)] * len(filled),
         out_specs=[pl.BlockSpec((T_BLOCK, f_pad), row)] * 3,
         out_shape=[jax.ShapeDtypeStruct((tokens, f_pad), BF16)] * 3,
+        input_output_aliases={2 + i: i for i in range(len(filled))},
         compiler_params=pltpu.CompilerParams(dimension_semantics=("arbitrary",), vmem_limit_bytes=60 * 2 ** 20),
-        cost_estimate=pl.CostEstimate(flops=2 * tokens * width * 2 * f_pad, bytes_accessed=2 * (m.size + w.size + 3 * tokens * f_pad), transcendentals=2 * tokens * f_pad),
+        cost_estimate=pl.CostEstimate(flops=2 * tokens * width * f_pad, bytes_accessed=m.size + 2 * w.size + 3 * tokens * f_pad, transcendentals=tokens * f_pad),
         name="up_act",
-    )(m, w)
+    )(m, w, *filled)
 
 
 def up_back_kernel(dy_ref, wd_ref, g_ref, l_ref, out_ref):
@@ -409,16 +412,19 @@
             w_all = lax.dynamic_update_slice(w_all, up_near[k], ((me ^ k) * h_loc, 0))
         for k in (0, 1, 2):
             w_all = lax.dynamic_update_slice(w_all, up_far[k], ((me ^ group ^ k) * h_loc, 0))
-        m_all = joined([mlp_in, hop(mlp_in, 1)])
+        m_near = hop(mlp_in, 1)
+        m_all = joined([mlp_in, m_near])
         dy_all = joined(dy_parts[:2])
         wd_all = lax.dynamic_update_slice(jnp.zeros((f_pad, width), BF16), w_down, (side * f_blk, 0))
         m_far = hop(mlp_in, 2)
-        m_all, dy_all, w_all, wd_all, m_far = after(m_all, dy_all, w_all, wd_all, m_far)
         w_all = lax.dynamic_update_slice(w_all, up_far[3], ((me ^ group ^ 3) * h_loc, 0))
+        m_all, dy_all, w_all, wd_all = after(m_all, dy_all, w_all, wd_all)
+
+        made = up_act(m_all, w_all, 0)
+        *made, m_all, m_far = after(*made, m_all, m_far)
         m_all = lax.dynamic_update_slice(m_all, m_far, (2 * tokens, 0))
         m_all = lax.dynamic_update_slice(m_all, hop(m_far, 1), (3 * tokens, 0))
-
-        gate_low, lin_low, act = up_act(m_all, w_all)
+        gate_low, lin_low, act = up_act(m_all, w_all, 1, made)
         act, dy_far, down_far, dy_all = after(act, dy_parts[2], down_far, dy_all)
         dy_parts[2:] = [dy_far, hop(dy_far, 1)]
         for k in (2, 3):

time: 2500 us -> 2570 us (1.028)
  waiting for transfers between devices: 1110 us -> 1180 us
    ppermute x32, waiting for transfers between devices: 1040 us -> 1120 us  [hop(): return lax.ppermute(v, ax, [(i, i ^ k) for i in range(n_dev)])]
    pallas_call x1 -> x2, Pallas kernels: 169 us -> 183 us  [up_act(): pl.pallas_call(up_kernel, grid=(steps,), in_specs=[pl.BlockSpec((T_BLOCK,...]
  transfers between devices with their start and end apart: 36 -> 36, of which waited for: 14 -> 18; matrix products, arithmetic and copies ran while one was open for 23% -> 22% of each run, Pallas kernels for 11% -> 12%
where the time goes in v5:
time: 2570 us
  waiting for transfers between devices  1180 us (46%)
  matrix products  685 us (27%)
  Pallas kernels  409 us (16%)
  other arithmetic  147 us (6%)
  local copies, waits for them, and re-layouts  112 us (4%)
    ppermute x32, waiting for transfers between devices, hop(): return lax.ppermute(v, ax, [(i, i ^ k) for i in range(n_dev)])  1120 us
    dot_general x19, matrix products, mm(): return lax.dot_general(a, b, dims, preferred_element_type=F32)  685 us
    pallas_call x2, Pallas kernels, up_act(): pl.pallas_call(up_kernel, grid=(steps,), in_specs=[pl.BlockSpec((T_BLOCK,...  183 us
    pallas_call x1, Pallas kernels, up_back(): pl.pallas_call(up_back_kernel, grid=(tokens // T_BLOCK,), in_specs=[pl.Bl...  112 us
    all_gather x2, waiting for transfers between devices, gather_rows(): return lax.all_gather(shard, ax, axis=0, tiled=True)  56.5 us
  transfers between devices with their start and end apart: 36, of which 18 were waited for; matrix products, arithmetic and copies ran while one was open for 22% of the time, Pallas kernels for 12%

profile of v5, /device:TPU:0, one launch (start us, length us, event | category | flops | bytes accessed | tf_op | source)
XLA Modules:
  0.0 2568.3 jit_solution(2905625539653126803)
XLA Ops:
  25.0 13.5 split_up.1
  40.9 12.2 dynamic_update_slice.56
  70.0 26.4 %all-gather.3.cloned.1.call-done = bf16[2048,2560]{1,0:T(8,128)(2,1)} async-done(((bf16[256,2560]{1,0:T(8,128)(2,1)}), bf16[2048,2560]{1,0:T(8,128)(2,1)}) %all-gather.3.cloned.1.call-update) | async-done | bytes 10485776 | tf_op jit(solution)/shard_map/all_gather | solution.py:351
  96.5 22.4 convolution_add_fusion.z_ref
  118.8 33.2 %attend.1 = (bf16[1536,2560]{1,0:T(8,128)(2,1)}, bf16[1536,2048]{1,0:T(8,128)(2,1)}) custom-call(f32[1536,2560]{1,0:T(8,128)} %convolution_add_fusion.z_ref, f32[1536,128]{1,0:T(8,128)S(1)} %get-tuple-element.193.cos_ref, f32[1536,128]{1,0:T(8,128)S(1)} %get-tuple-element.192.sin_ref), custom_call_target="tpu_custom_call" | custom-call | flops 19327352832 | bytes 31457280 | tf_op jit(solution)/shard_map/attend/pallas_call | solution.py:159
  152.0 30.0 %all-gather.5.cloned.1.call-done = bf16[2048,2048]{1,0:T(8,128)(2,1)} async-done(((bf16[256,2048]{1,0:T(8,128)(2,1)}), bf16[2048,2048]{1,0:T(8,128)(2,1)}) %all-gather.5.cloned.1.call-update) | async-done | bytes 8388624 | tf_op jit(solution)/shard_map/all_gather | solution.py:351
  182.1 18.9 fusion.19
  238.3 46.8 %collective-permute-done.9 = bf16[256,5632]{1,0:T(8,128)(2,1)S(1)} collective-permute-done((bf16[256,5632]{1,0:T(8,128)(2,1)}, bf16[256,5632]{1,0:T(8,128)(2,1)S(1)}, u32[]{:S(2)}, u32[]{:S(2)}) %collective-permute-start.9) | collective-permute-done | bytes 2883616 | tf_op jit(solution)/shard_map/ppermute | solution.py:348
  286.9 60.1 %collective-permute-done.10 = bf16[256,5632]{1,0:T(8,128)(2,1)S(1)} collective-permute-done((bf16[256,5632]{1,0:T(8,128)(2,1)}, bf16[256,5632]{1,0:T(8,128)(2,1)S(1)}, u32[]{:S(2)}, u32[]{:S(2)}) %collective-permute-start.10) | collective-permute-done | bytes 2883616 | tf_op jit(solution)/shard_map/ppermute | solution.py:348
  348.7 59.3 %collective-permute-done.11 = bf16[256,5632]{1,0:T(8,128)(2,1)S(1)} collective-permute-done((bf16[256,5632]{1,0:T(8,128)(2,1)}, bf16[256,5632]{1,0:T(8,128)(2,1)S(1)}, u32[]{:S(2)}, u32[]{:S(2)}) %collective-permute-start.11) | collective-permute-done | bytes 2883616 | tf_op jit(solution)/shard_map/ppermute | solution.py:348
  416.3 12.4 dynamic_update_slice.54
  432.4 91.2 %up_act.2 = (bf16[6144,2816]{1,0:T(8,128)(2,1)}, bf16[6144,2816]{1,0:T(8,128)(2,1)}, bf16[6144,2816]{1,0:T(8,128)(2,1)}) custom-call(bf16[6144,2048]{1,0:T(8,128)(2,1)} %constant_dynamic-update-slice_fusion.15.m_ref, bf16[2048,5632]{1,0:T(8,128)(2,1)} %constant_dynamic-update-slice_fusion.6.w_ref), custom_call_target="tpu_custom_call" | custom-call | flops 70866960384 | bytes 87556096 | tf_op jit(solution)/shard_map/up_act/pallas_call | solution.py:208
  523.6 42.3 %collective-permute-done.12 = bf16[1536,2048]{1,0:T(8,128)(2,1)} collective-permute-done((bf16[1536,2048]{1,0:T(8,128)(2,1)}, bf16[1536,2048]{1,0:T(8,128)(2,1)}, u32[]{:S(2)}, u32[]{:S(2)}) %collective-permute-start.12) | collective-permute-done | bytes 6291488 | tf_op jit(solution)/shard_map/ppermute | solution.py:348
  583.0 91.4 %up_act.3 = (bf16[6144,2816]{1,0:T(8,128)(2,1)}, bf16[6144,2816]{1,0:T(8,128)(2,1)}, bf16[6144,2816]{1,0:T(8,128)(2,1)}) custom-call(bf16[6144,2048]{1,0:T(8,128)(2,1)} %constant_dynamic-update-slice_fusion.3.m_ref, bf16[2048,5632]{1,0:T(8,128)(2,1)} %constant_dynamic-update-slice_fusion.6.w_ref, ...), custom_call_target="tpu_custom_call", output_to_operand_aliasing={{0}: (2, {}), {1}: (3, {}), {2}: (4, {})} | custom-call | flops 70866960384 | bytes 87556096 | tf_op jit(solution)/shard_map/up_act/pallas_call | solution.py:208
  674.4 15.7 collective-permute-done.15
  690.1 14.0 collective-permute-done.14
  710.1 24.9 fusion.44
  735.5 24.7 fusion.42
  773.3 10.9 add.224
  784.2 46.3 %fusion.10 = f32[1408,2048]{1,0:T(8,128)} fusion(bf16[6144,2048]{1,0:T(8,128)(2,1)} %constant_dynamic-update-slice_fusion.dy_ref, bf16[6144,2816]{1,0:T(8,128)(2,1)} %get-tuple-element.163, s32[]{:T(128)S(6)} %select_n.165), kind=kOutput, calls=%fused_computation.14 | convolution fusion | flops 35433480192 | bytes 54001668 | tf_op jit(solution)/shard_map/dot_general | solution.py:32
  830.5 112.2 %up_back.1 = bf16[6144,5632]{1,0:T(8,128)(2,1)} custom-call(bf16[6144,2048]{1,0:T(8,128)(2,1)} %constant_dynamic-update-slice_fusion.dy_ref, bf16[2816,2048]{1,0:T(8,128)(2,1)} %constant_dynamic-update-slice_fusion.2.wd_ref, bf16[6144,2816]{1,0:T(8,128)(2,1)} %get-tuple-element.130.g_ref, bf16[6144,2816]{1,0:T(8,128)(2,1)} %get-tuple-element.131.l_ref), custom_call_target="tpu_custom_call" | custom-call | flops 70866960384 | bytes 175112192 | tf_op jit(solution)/shard_map/up_back/pallas_call | solution.py:237
  942.7 45.0 %fusion.2 = f32[1536,2048]{1,0:T(8,128)} fusion(bf16[2048,5632]{1,0:T(8,128)(2,1)} %constant_dynamic-update-slice_fusion.6.w_ref, bf16[6144,5632]{1,0:T(8,128)(2,1)} %up_back.1), kind=kOutput, calls=%fused_computation.6 | convolution fusion | flops 35433480192 | bytes 52953088 | tf_op jit(solution)/shard_map/dot_general | solution.py:32
  987.7 44.8 %fusion.8 = f32[1536,2048]{1,0:T(8,128)} fusion(bf16[2048,5632]{1,0:T(8,128)(2,1)} %constant_dynamic-update-slice_fusion.6.w_ref, bf16[6144,5632]{1,0:T(8,128)(2,1)} %up_back.1), kind=kOutput, calls=%fused_computation.12 | convolution fusion | flops 35433480192 | bytes 52953088 | tf_op jit(solution)/shard_map/dot_general | solution.py:32
  1032.6 14.4 add.225
  1046.9 46.9 %fusion.50 = f32[512,5632]{1,0:T(8,128)} fusion(bf16[6144,5632]{1,0:T(8,128)(2,1)} %up_back.1, bf16[6144,2048]{1,0:T(8,128)(2,1)} %constant_dynamic-update-slice_fusion.3.m_ref, s32[]{:T(128)S(6)} %select_n.166), kind=kOutput, calls=%fused_computation.62 | convolution fusion | flops 35433480192 | bytes 87031808 | tf_op jit(solution)/shard_map/dot_general | solution.py:32
  1093.8 46.9 %fusion.48 = f32[512,5632]{1,0:T(8,128)} fusion(bf16[6144,5632]{1,0:T(8,128)(2,1)} %up_back.1, bf16[6144,2048]{1,0:T(8,128)(2,1)} %constant_dynamic-update-slice_fusion.3.m_ref, s32[]{:T(128)S(6)} %select_n.167), kind=kOutput, calls=%fused_computation.60 | convolution fusion | flops 35433480192 | bytes 87031808 | tf_op jit(solution)/shard_map/dot_general | solution.py:32
  1140.7 81.6 %fusion.36 = f32[1024,5632]{1,0:T(8,128)} fusion(bf16[6144,5632]{1,0:T(8,128)(2,1)} %up_back.1, bf16[6144,2048]{1,0:T(8,128)(2,1)} %constant_dynamic-update-slice_fusion.3.m_ref, s32[]{:T(128)S(6)} %select_n.168), kind=kOutput, calls=%fused_computation.48 | convolution fusion | flops 70866960384 | bytes 104857600 | tf_op jit(solution)/shard_map/dot_general | solution.py:32
  1222.6 44.9 %fusion.6 = f32[1536,2048]{1,0:T(8,128)} fusion(bf16[2048,5632]{1,0:T(8,128)(2,1)} %constant_dynamic-update-slice_fusion.6.w_ref, bf16[6144,5632]{1,0:T(8,128)(2,1)} %up_back.1), kind=kOutput, calls=%fused_computation.10 | convolution fusion | flops 35433480192 | bytes 52953088 | tf_op jit(solution)/shard_map/dot_general | solution.py:32
  1267.8 44.6 %fusion.4 = f32[1536,2048]{1,0:T(8,128)} fusion(bf16[2048,5632]{1,0:T(8,128)(2,1)} %constant_dynamic-update-slice_fusion.6.w_ref, bf16[6144,5632]{1,0:T(8,128)(2,1)} %up_back.1), kind=kOutput, calls=%fused_computation.8 | convolution fusion | flops 35433480192 | bytes 52953088 | tf_op jit(solution)/shard_map/dot_general | solution.py:32
  1312.4 183.0 %collective-permute-done.20 = f32[1536,2048]{1,0:T(8,128)} collective-permute-done((f32[1536,2048]{1,0:T(8,128)}, f32[1536,2048]{1,0:T(8,128)}, u32[]{:S(2)}, u32[]{:S(2)}) %collective-permute-start.20) | collective-permute-done | bytes 12582944 | tf_op jit(solution)/shard_map/ppermute | solution.py:348
  1495.4 21.3 fusion.22
  1516.7 12.1 fusion.18
  1528.8 21.9 fusion.52
  1550.8 21.0 convolution_convert_fusion.dctx_ref
  1571.8 46.6 %attend_back.1 = (bf16[1536,2560]{1,0:T(8,128)(2,1)}, f32[1,2560]{1,0:T(1,128)S(1)}) custom-call(bf16[1536,2560]{1,0:T(8,128)(2,1)} %get-tuple-element.139.qkv_ref, bf16[1536,2048]{1,0:T(8,128)(2,1)} %convolution_convert_fusion.dctx_ref, f32[1536,128]{1,0:T(8,128)S(1)} %get-tuple-element.193.cos_ref, f32[1536,128]{1,0:T(8,128)S(1)} %get-tuple-element.192.sin_ref), custom_call_target="tpu_custom_call" | custom-call | flops 48318382080 | bytes 31457280 | tf_op jit(solution)/shard_map/attend_back/pallas_call | solution.py:177
  1618.4 22.3 fusion.68
  1640.6 23.2 fusion.69
  1663.8 24.7 fusion.40
  1692.2 331.7 %collective-permute-done.29 = f32[512,5632]{1,0:T(8,128)} collective-permute-done((f32[512,5632]{1,0:T(8,128)}, f32[512,5632]{1,0:T(8,128)}, u32[]{:S(2)}, u32[]{:S(2)}) %collective-permute-start.29) | collective-permute-done | bytes 11534368 | tf_op jit(solution)/shard_map/ppermute | solution.py:348
  2023.9 12.8 dynamic-slice_add_fusion
  2036.8 234.2 %collective-permute-done.23 = f32[1408,2048]{1,0:T(8,128)} collective-permute-done((f32[1408,2048]{1,0:T(8,128)}, f32[1408,2048]{1,0:T(8,128)}, u32[]{:S(2)}, u32[]{:S(2)}) %collective-permute-start.23) | collective-permute-done | bytes 11534368 | tf_op jit(solution)/shard_map/ppermute | solution.py:348
  2280.3 55.5 %slice_add_fusion = f32[1376,2048]{1,0:T(8,128)} fusion(f32[1408,2048]{1,0:T(8,128)} %collective-permute-done.23, bf16[6144,2048]{1,0:T(8,128)(2,1)} %constant_dynamic-update-slice_fusion.dy_ref, bf16[6144,2816]{1,0:T(8,128)(2,1)} %get-tuple-element.163, s32[]{:T(128)S(6)} %select_n.164), kind=kOutput, calls=%fused_computation.50 | convolution fusion | flops 34630991872 | bytes 65011716 | tf_op jit(solution)/shard_map/dot_general | solution.py:32
  2335.9 14.4 fusion.30
  2350.3 24.7 fusion.38
  2377.2 18.3 add_convert_fusion
  2396.7 121.0 %collective-permute-done.19 = f32[512,5632]{1,0:T(8,128)} collective-permute-done((f32[512,5632]{1,0:T(8,128)}, f32[512,5632]{1,0:T(8,128)}, u32[]{:S(2)}, u32[]{:S(2)}) %collective-permute-start.19) | collective-permute-done | bytes 11534368 | tf_op jit(solution)/shard_map/ppermute | solution.py:348
  2517.8 13.0 dynamic-slice_add_fusion.2
  2540.5 21.0 join_up.1
  (153 shorter events, 153.2 us)
Async XLA Ops:
  7.2 89.3 %all-gather.3.cloned.1.call-start = ((), (), s32[]{:S(2)}) async-start(), calls=%async_computation.2 | async-start | bytes 11796480 | tf_op jit(solution)/shard_map/all_gather | solution.py:351
  7.9 174.2 %all-gather.5.cloned.1.call-start = ((), (), s32[]{:S(2)}) async-start(), calls=%async_computation.3 | async-start | bytes 9437184 | tf_op jit(solution)/shard_map/all_gather | solution.py:351
  8.7 2552.9 %reduce-scatter.5.cloned.1.call-start = ((), (), s32[]{:S(2)}) async-start(), calls=%async_computation.5 | async-start | bytes 18874368 | tf_op jit(solution)/shard_map/reduce_scatter | solution.py:354
  9.5 8.8 collective-permute-start
  18.3 4.6 collective-permute-start.1
  21.1 41.9 %copy-start.4 = (f32[1536]{0:T(1024)}, f32[1536]{0:T(1024)S(1)}, u32[]{:S(2)}) copy-start(f32[1536]{0:T(1024)S(1)} %rsqrt.20) | copy-start | bytes 18436
  22.9 15.5 collective-permute-start.2
  38.5 169.3 %collective-permute-start.5 = (bf16[256,5632]{1,0:T(8,128)(2,1)}, bf16[256,5632]{1,0:T(8,128)(2,1)}, u32[]{:S(2)}, u32[]{:S(2)}) collective-permute-start(bf16[256,5632]{1,0:T(8,128)(2,1)} %get-tuple-element.101), channel_id=1, source_target_pairs={{0,1},{1,0},{2,3},{3,2},{4,5},{5,4},{6,7},{7,6}} | collective-permute-start | bytes 8650760 | tf_op jit(solution)/shard_map/ppermute | solution.py:348
  38.5 181.1 %collective-permute-start.6 = (bf16[256,5632]{1,0:T(8,128)(2,1)}, bf16[256,5632]{1,0:T(8,128)(2,1)}, u32[]{:S(2)}, u32[]{:S(2)}) collective-permute-start(bf16[256,5632]{1,0:T(8,128)(2,1)} %get-tuple-element.102), channel_id=1, source_target_pairs={{0,2},{1,3},{2,0},{3,1},{4,6},{5,7},{6,4},{7,5}} | collective-permute-start | bytes 8650760 | tf_op jit(solution)/shard_map/ppermute | solution.py:348
  40.0 185.5 %collective-permute-start.7 = (bf16[256,5632]{1,0:T(8,128)(2,1)}, bf16[256,5632]{1,0:T(8,128)(2,1)}, u32[]{:S(2)}, u32[]{:S(2)}) collective-permute-start(bf16[256,5632]{1,0:T(8,128)(2,1)} %get-tuple-element.103), channel_id=1, source_target_pairs={{0,3},{1,2},{2,1},{3,0},{4,7},{5,6},{6,5},{7,4}} | collective-permute-start | bytes 8650760 | tf_op jit(solution)/shard_map/ppermute | solution.py:348
  40.4 190.4 %collective-permute-start.8 = (bf16[256,5632]{1,0:T(8,128)(2,1)}, bf16[256,5632]{1,0:T(8,128)(2,1)}, u32[]{:S(2)}, u32[]{:S(2)}) collective-permute-start(bf16[256,5632]{1,0:T(8,128)(2,1)} %get-tuple-element.100), channel_id=1, source_target_pairs={{0,4},{1,5},{2,6},{3,7},{4,0},{5,1},{6,2},{7,3}} | collective-permute-start | bytes 8650760 | tf_op jit(solution)/shard_map/ppermute | solution.py:348
  40.6 22.4 copy-start.6
  40.7 160.3 %copy-start.8 = (f32[1,2,8,128]{3,1,2,0:T(2,128)}, f32[1,2,8,128]{3,1,2,0:T(2,128)S(1)}, u32[]{:S(2)}) copy-start(f32[1,2,8,128]{3,1,2,0:T(2,128)S(1)} %copy.27) | copy-start | bytes 24580
  40.7 369.1 %collective-permute-start.4 = (bf16[1536,2048]{1,0:T(8,128)(2,1)}, bf16[1536,2048]{1,0:T(8,128)(2,1)}, u32[]{:S(2)}, u32[]{:S(2)}) collective-permute-start(bf16[1536,2048]{1,0:T(8,128)(2,1)} %bitcast.76), channel_id=1, source_target_pairs={{0,1},{1,0},{2,3},{3,2},{4,5},{5,4},{6,7},{7,6}} | collective-permute-start | bytes 18874376 | tf_op jit(solution)/shard_map/ppermute | solution.py:348
  207.8 221.2 %collective-permute-start.3 = (bf16[1536,2048]{1,0:T(8,128)(2,1)}, bf16[1536,2048]{1,0:T(8,128)(2,1)S(1)}, u32[]{:S(2)}, u32[]{:S(2)}) collective-permute-start(bf16[1536,2048]{1,0:T(8,128)(2,1)} %fusion.14), channel_id=1, source_target_pairs={{0,1},{1,0},{2,3},{3,2},{4,5},{5,4},{6,7},{7,6}} | collective-permute-start | bytes 18874376 | tf_op jit(solution)/shard_map/ppermute | solution.py:348
  219.6 65.6 %collective-permute-start.9 = (bf16[256,5632]{1,0:T(8,128)(2,1)}, bf16[256,5632]{1,0:T(8,128)(2,1)S(1)}, u32[]{:S(2)}, u32[]{:S(2)}) collective-permute-start(bf16[256,5632]{1,0:T(8,128)(2,1)} %collective-permute-done.5), channel_id=1, source_target_pairs={{0,4},{1,5},{2,6},{3,7},{4,0},{5,1},{6,2},{7,3}} | collective-permute-start | bytes 8650760 | tf_op jit(solution)/shard_map/ppermute | solution.py:348
  225.5 121.4 %collective-permute-start.10 = (bf16[256,5632]{1,0:T(8,128)(2,1)}, bf16[256,5632]{1,0:T(8,128)(2,1)S(1)}, u32[]{:S(2)}, u32[]{:S(2)}) collective-permute-start(bf16[256,5632]{1,0:T(8,128)(2,1)} %collective-permute-done.6), channel_id=1, source_target_pairs={{0,4},{1,5},{2,6},{3,7},{4,0},{5,1},{6,2},{7,3}} | collective-permute-start | bytes 8650760 | tf_op jit(solution)/shard_map/ppermute | solution.py:348
  230.8 177.2 %collective-permute-start.11 = (bf16[256,5632]{1,0:T(8,128)(2,1)}, bf16[256,5632]{1,0:T(8,128)(2,1)S(1)}, u32[]{:S(2)}, u32[]{:S(2)}) collective-permute-start(bf16[256,5632]{1,0:T(8,128)(2,1)} %collective-permute-done.7), channel_id=1, source_target_pairs={{0,4},{1,5},{2,6},{3,7},{4,0},{5,1},{6,2},{7,3}} | collective-permute-start | bytes 8650760 | tf_op jit(solution)/shard_map/ppermute | solution.py:348
  428.7 137.2 %collective-permute-start.12 = (bf16[1536,2048]{1,0:T(8,128)(2,1)}, bf16[1536,2048]{1,0:T(8,128)(2,1)}, u32[]{:S(2)}, u32[]{:S(2)}) collective-permute-start(bf16[1536,2048]{1,0:T(8,128)(2,1)} %fusion.14), channel_id=1, source_target_pairs={{0,2},{1,3},{2,0},{3,1},{4,6},{5,7},{6,4},{7,5}} | collective-permute-start | bytes 18874376 | tf_op jit(solution)/shard_map/ppermute | solution.py:348
  565.9 10.5 collective-permute-start.13
  565.9 138.2 %collective-permute-start.14 = (bf16[1536,2048]{1,0:T(8,128)(2,1)}, bf16[1536,2048]{1,0:T(8,128)(2,1)}, u32[]{:S(2)}, u32[]{:S(2)}) collective-permute-start(bf16[1536,2048]{1,0:T(8,128)(2,1)} %bitcast.78), channel_id=1, source_target_pairs={{0,2},{1,3},{2,0},{3,1},{4,6},{5,7},{6,4},{7,5}} | collective-permute-start | bytes 18874376 | tf_op jit(solution)/shard_map/ppermute | solution.py:348
  566.2 123.9 %collective-permute-start.15 = (bf16[1376,2048]{1,0:T(8,128)(2,1)}, bf16[1376,2048]{1,0:T(8,128)(2,1)}, u32[]{:S(2)}, u32[]{:S(2)}) collective-permute-start(bf16[1376,2048]{1,0:T(8,128)(2,1)} %param.19), channel_id=1, source_target_pairs={{0,4},{1,5},{2,6},{3,7},{4,0},{5,1},{6,2},{7,3}} | collective-permute-start | bytes 16908296 | tf_op jit(solution)/shard_map/ppermute | solution.py:348
  735.0 38.3 %collective-permute-start.17 = (f32[1536,2048]{1,0:T(8,128)}, f32[1536,2048]{1,0:T(8,128)S(1)}, u32[]{:S(2)}, u32[]{:S(2)}) collective-permute-start(f32[1536,2048]{1,0:T(8,128)} %fusion.44), channel_id=1, source_target_pairs={{0,1},{1,0},{2,3},{3,2},{4,5},{5,4},{6,7},{7,6}} | collective-permute-start | bytes 37748744 | tf_op jit(solution)/shard_map/ppermute | solution.py:348
  735.0 31.7 %collective-permute-start.16 = (bf16[1536,2048]{1,0:T(8,128)(2,1)}, bf16[1536,2048]{1,0:T(8,128)(2,1)}, u32[]{:S(2)}, u32[]{:S(2)}) collective-permute-start(bf16[1536,2048]{1,0:T(8,128)(2,1)} %collective-permute-done.14), channel_id=1, source_target_pairs={{0,1},{1,0},{2,3},{3,2},{4,5},{5,4},{6,7},{7,6}} | collective-permute-start | bytes 18874376 | tf_op jit(solution)/shard_map/ppermute | solution.py:348
  987.7 44.8 %collective-permute-start.18 = (f32[1536,2048]{1,0:T(8,128)}, f32[1536,2048]{1,0:T(8,128)}, u32[]{:S(2)}, u32[]{:S(2)}) collective-permute-start(f32[1536,2048]{1,0:T(8,128)} %fusion.2), channel_id=1, source_target_pairs={{0,1},{1,0},{2,3},{3,2},{4,5},{5,4},{6,7},{7,6}} | collective-permute-start | bytes 37748744 | tf_op jit(solution)/shard_map/ppermute | solution.py:348
  1222.3 273.0 %collective-permute-start.20 = (f32[1536,2048]{1,0:T(8,128)}, f32[1536,2048]{1,0:T(8,128)}, u32[]{:S(2)}, u32[]{:S(2)}) collective-permute-start(f32[1536,2048]{1,0:T(8,128)} %add.225), channel_id=1, source_target_pairs={{0,2},{1,3},{2,0},{3,1},{4,6},{5,7},{6,4},{7,5}} | collective-permute-start | bytes 37748744 | tf_op jit(solution)/shard_map/ppermute | solution.py:348
  1267.5 227.8 %copy-start.9 = (f32[1,2,8,128]{3,1,2,0:T(2,128)S(1)}, f32[1,2,8,128]{3,1,2,0:T(2,128)}, u32[]{:S(2)}) copy-start(f32[1,2,8,128]{3,1,2,0:T(2,128)} %copy-done.8) | copy-start | bytes 24580
  1267.6 227.8 %copy-start.11 = (f32[1536]{0:T(1024)S(1)}, f32[1536]{0:T(1024)}, u32[]{:S(2)}) copy-start(f32[1536]{0:T(1024)} %copy-done.10) | copy-start | bytes 18436
  1267.6 227.8 %collective-permute-start.21 = (f32[1536,2048]{1,0:T(8,128)}, f32[1536,2048]{1,0:T(8,128)}, u32[]{:S(2)}, u32[]{:S(2)}) collective-permute-start(f32[1536,2048]{1,0:T(8,128)} %fusion.6), channel_id=1, source_target_pairs={{0,1},{1,0},{2,3},{3,2},{4,5},{5,4},{6,7},{7,6}} | collective-permute-start | bytes 37748744 | tf_op jit(solution)/shard_map/ppermute | solution.py:348
  1312.4 204.3 %copy-start.1 = (bf16[1536,2048]{1,0:T(8,128)(2,1)S(1)}, bf16[1536,2048]{1,0:T(8,128)(2,1)}, u32[]{:S(2)}) copy-start(bf16[1536,2048]{1,0:T(8,128)(2,1)} %copy-done) | copy-start | bytes 18874372
  1312.4 204.3 %copy-start.2 = (bf16[3,512,2048]{2,1,0:T(8,128)(2,1)S(1)}, bf16[3,512,2048]{2,1,0:T(8,128)(2,1)}, u32[]{:S(2)}) copy-start(bf16[3,512,2048]{2,1,0:T(8,128)(2,1)} %param.12) | copy-start | bytes 18874372
  1550.7 1010.9 %reduce-scatter.3.cloned.1.call-start = ((), (), s32[]{:S(2)}) async-start(), calls=%async_computation.4 | async-start | bytes 23592960 | tf_op jit(solution)/shard_map/reduce_scatter | solution.py:354
  1550.7 67.6 %slice-start = ((s8[6291456]{0:T(1024)(128)(4,1)}), s8[2097152]{0:T(1024)(128)(4,1)S(1)}, s32[]{:S(2)}) async-start(s8[6291456]{0:T(1024)(128)(4,1)} %bitcast.81), calls=%async_computation.6 | async-start | bytes 4194304
  1571.8 46.6 %slice-start.1 = ((s8[6291456]{0:T(1024)(128)(4,1)}), s8[4194304]{0:T(1024)(128)(4,1)S(1)}, s32[]{:S(2)}) async-start(s8[6291456]{0:T(1024)(128)(4,1)} %bitcast.81), calls=%async_computation.7 | async-start | bytes 8388608
  1688.5 582.5 %collective-permute-start.22 = (f32[1536,2048]{1,0:T(8,128)}, f32[1536,2048]{1,0:T(8,128)}, u32[]{:S(2)}, u32[]{:S(2)}) collective-permute-start(f32[1536,2048]{1,0:T(8,128)} %fusion.40), channel_id=1, source_target_pairs={{0,1},{1,0},{2,3},{3,2},{4,5},{5,4},{6,7},{7,6}} | collective-permute-start | bytes 37748744 | tf_op jit(solution)/shard_map/ppermute | solution.py:348
  1688.5 335.3 %collective-permute-start.29 = (f32[512,5632]{1,0:T(8,128)}, f32[512,5632]{1,0:T(8,128)}, u32[]{:S(2)}, u32[]{:S(2)}) collective-permute-start(f32[512,5632]{1,0:T(8,128)} %fusion.50), channel_id=1, source_target_pairs={{0,4},{1,5},{2,6},{3,7},{4,0},{5,1},{6,2},{7,3}} | collective-permute-start | bytes 34603016 | tf_op jit(solution)/shard_map/ppermute | solution.py:348
  1689.6 581.4 %collective-permute-start.23 = (f32[1408,2048]{1,0:T(8,128)}, f32[1408,2048]{1,0:T(8,128)}, u32[]{:S(2)}, u32[]{:S(2)}) collective-permute-start(f32[1408,2048]{1,0:T(8,128)} %fusion.10), channel_id=1, source_target_pairs={{0,4},{1,5},{2,6},{3,7},{4,0},{5,1},{6,2},{7,3}} | collective-permute-start | bytes 34603016 | tf_op jit(solution)/shard_map/ppermute | solution.py:348
  1690.6 659.7 %collective-permute-start.24 = (f32[1536,2048]{1,0:T(8,128)}, f32[1536,2048]{1,0:T(8,128)}, u32[]{:S(2)}, u32[]{:S(2)}) collective-permute-start(f32[1536,2048]{1,0:T(8,128)} %add.224), channel_id=1, source_target_pairs={{0,2},{1,3},{2,0},{3,1},{4,6},{5,7},{6,4},{7,5}} | collective-permute-start | bytes 37748744 | tf_op jit(solution)/shard_map/ppermute | solution.py:348
  1690.7 346.1 %copy-start.12 = (f32[2048]{0:T(1024)S(1)}, f32[2048]{0:T(1024)}, u32[]{:S(2)}) copy-start(f32[2048]{0:T(1024)} %get-tuple-element.179) | copy-start | bytes 24580
  1690.7 580.3 %copy-start.5 = (f32[1536]{0:T(1024)S(1)}, f32[1536]{0:T(1024)}, u32[]{:S(2)}) copy-start(f32[1536]{0:T(1024)} %copy-done.4) | copy-start | bytes 18436
  1690.7 580.3 %copy-start.7 = (f32[1,2,8,128]{3,1,2,0:T(2,128)S(1)}, f32[1,2,8,128]{3,1,2,0:T(2,128)}, u32[]{:S(2)}) copy-start(f32[1,2,8,128]{3,1,2,0:T(2,128)} %copy-done.6) | copy-start | bytes 24580
  1690.7 827.0 %collective-permute-start.19 = (f32[512,5632]{1,0:T(8,128)}, f32[512,5632]{1,0:T(8,128)}, u32[]{:S(2)}, u32[]{:S(2)}) collective-permute-start(f32[512,5632]{1,0:T(8,128)} %fusion.48), channel_id=1, source_target_pairs={{0,4},{1,5},{2,6},{3,7},{4,0},{5,1},{6,2},{7,3}} | collective-permute-start | bytes 34603016 | tf_op jit(solution)/shard_map/ppermute | solution.py:348
  2036.7 499.0 %collective-permute-start.30 = (f32[256,5632]{1,0:T(8,128)}, f32[256,5632]{1,0:T(8,128)}, u32[]{:S(2)}, u32[]{:S(2)}) collective-permute-start(f32[256,5632]{1,0:T(8,128)} %get-tuple-element.183), channel_id=1, source_target_pairs={{0,2},{1,3},{2,0},{3,1},{4,6},{5,7},{6,4},{7,5}} | collective-permute-start | bytes 17301512 | tf_op jit(solution)/shard_map/ppermute | solution.py:348
  2271.0 264.6 %collective-permute-start.31 = (f32[256,5632]{1,0:T(8,128)}, f32[256,5632]{1,0:T(8,128)}, u32[]{:S(2)}, u32[]{:S(2)}) collective-permute-start(f32[256,5632]{1,0:T(8,128)} %get-tuple-element.182), channel_id=1, source_target_pairs={{0,3},{1,2},{2,1},{3,0},{4,7},{5,6},{6,5},{7,4}} | collective-permute-start | bytes 17301512 | tf_op jit(solution)/shard_map/ppermute | solution.py:348
  2280.3 94.7 %collective-permute-start.25 = (f32[4,832]{1,0:T(4,128)S(1)}, f32[4,832]{1,0:T(4,128)S(1)}, u32[]{:S(2)}, u32[]{:S(2)}) collective-permute-start(f32[4,832]{1,0:T(4,128)S(1)} %bitcast.89), channel_id=1, source_target_pairs={{0,1},{1,0},{2,3},{3,2},{4,5},{5,4},{6,7},{7,6}} | collective-permute-start | bytes 39944 | tf_op jit(solution)/shard_map/ppermute | solution.py:348
  2375.1 21.6 collective-permute-start.26
  2530.8 9.8 collective-permute-start.28
  2530.8 3.6 collective-permute-start.27
  (3 other events, 17.5 us)
Sparse Core Ops, SparseCore 0:
  9.8 86.6 all-gather.2
  98.3 83.7 all-gather.4
  1550.8 107.7 reduce-scatter.4
  1690.7 216.4 reduce-scatter.2

commit v6 on v5

--- a/solution.py
+++ b/solution.py
@@ -425,11 +425,9 @@
         m_all = lax.dynamic_update_slice(m_all, m_far, (2 * tokens, 0))
         m_all = lax.dynamic_update_slice(m_all, hop(m_far, 1), (3 * tokens, 0))
         gate_low, lin_low, act = up_act(m_all, w_all, 1, made)
-        act, dy_far, down_far, dy_all = after(act, dy_parts[2], down_far, dy_all)
-        dy_parts[2:] = [dy_far, hop(dy_far, 1)]
-        for k in (2, 3):
-            dy_all = lax.dynamic_update_slice(dy_all, dy_parts[k], (k * tokens, 0))
+        act, dy_far, dy_all, down_far = after(act, dy_parts[2], dy_all, down_far)
         wd_all = lax.dynamic_update_slice(wd_all, down_far, ((1 - side) * f_blk, 0))
+        dy_rest = hop(dy_far, 1)
 
         def block(rows, k, w, dims):
             return mm(rows[k * tokens:(k + 1) * tokens], w, dims)
@@ -446,8 +444,10 @@
         y3 = hop(y3, 1)
         y2 = block(act, 2, wd_all, NN_DIMS)
         act, y2 = after(act, y2)
-        act, dy_all, y2 = after(act, dy_all, y2 + y3)
+        act, dy_all, dy_far, dy_rest, y2 = after(act, dy_all, dy_far, dy_rest, y2 + y3)
         y2 = hop(y2, 2)
+        dy_all = lax.dynamic_update_slice(dy_all, dy_far, (2 * tokens, 0))
+        dy_all = lax.dynamic_update_slice(dy_all, dy_rest, (3 * tokens, 0))
         down_sum = down_grad(act, 1 - side)
         down_sum, act, gate_low, lin_low = after(down_sum, act, gate_low, lin_low)
         down_sum = hop(down_sum, group)
@@ -456,14 +456,12 @@
         dm3 = block(d_up, 3, w_all, NT_DIMS)
         d_up, dm3 = after(d_up, dm3)
         dm3 = hop(dm3, 1)
-        dm2 = block(d_up, 2, w_all, NT_DIMS)
-        d_up, dm2 = after(d_up, dm2)
-        d_up, dm2 = after(d_up, dm2 + dm3)
-        dm2 = hop(dm2, 2)
-
         far_a = up_grad(m_all, d_up, chip ^ 3, 1)
         d_up, far_a = after(d_up, far_a)
         far_a = hop(far_a, group)
+        dm2 = block(d_up, 2, w_all, NT_DIMS) + dm3
+        d_up, dm2 = after(d_up, dm2)
+        dm2 = hop(dm2, 2)
         far_b = up_grad(m_all, d_up, chip ^ 2, 1)
         d_up, far_b = after(d_up, far_b)
         far_b = hop(far_b, group)
@@ -497,8 +495,9 @@
         grad_w_qkv = scatter_rows(grad_w_qkv)
         d_normed = mm(d_proj, wqkv, NT_DIMS)
         d_normed, act = after(d_normed, act)
-        y1 = hop(block(act, 1, wd_all, NN_DIMS), 1)
+        y1 = block(act, 1, wd_all, NN_DIMS)
         act, d_normed, y1, down_sum = after(act, d_normed, y1, down_sum)
+        y1 = hop(y1, 1)
         grad_w_down = mm(lax.dynamic_slice(act, (0, side * f_blk), (group * tokens, f_blk)), dy_all, TN_DIMS)[:f_loc] + down_sum[:f_loc]
         grad_w_down, act, near = after(grad_w_down, act, near)
         grad_attn_gain = jnp.sum(d_normed * hid_wide * inv_one, axis=0)

time: 2570 us -> 2490 us (0.969)
  waiting for transfers between devices: 1180 us -> 1110 us
    ppermute x32, waiting for transfers between devices: 1120 us -> 1060 us  [hop(): return lax.ppermute(v, ax, [(i, i ^ k) for i in range(n_dev)])]
  transfers between devices with their start and end apart: 36 -> 36, of which waited for: 18 -> 17; matrix products, arithmetic and copies ran while one was open for 22% -> 22% of each run, Pallas kernels for 12% -> 12%
where the time goes in v6:
time: 2490 us; the launch traced here: 2480 us
  waiting for transfers between devices  1110 us (45%)
  matrix products  683 us (27%)
  Pallas kernels  409 us (16%)
  other arithmetic  127 us (5%)
  local copies, waits for them, and re-layouts  112 us (4%)
    ppermute x32, waiting for transfers between devices, hop(): return lax.ppermute(v, ax, [(i, i ^ k) for i in range(n_dev)])  1060 us
    dot_general x19, matrix products, mm(): return lax.dot_general(a, b, dims, preferred_element_type=F32)  683 us
    pallas_call x2, Pallas kernels, up_act(): pl.pallas_call(up_kernel, grid=(steps,), in_specs=[pl.BlockSpec((T_BLOCK,...  183 us
    pallas_call x1, Pallas kernels, up_back(): pl.pallas_call(up_back_kernel, grid=(tokens // T_BLOCK,), in_specs=[pl.Bl...  112 us
    all_gather x2, waiting for transfers between devices, gather_rows(): return lax.all_gather(shard, ax, axis=0, tiled=True)  56.8 us
  transfers between devices with their start and end apart: 36, of which 17 were waited for; matrix products, arithmetic and copies ran while one was open for 22% of the time, Pallas kernels for 12%

profile of v6, /device:TPU:0, one launch (start us, length us, event | category | flops | bytes accessed | tf_op | source)
XLA Modules:
  0.0 2481.9 jit_solution(1419611492866423527)
XLA Ops:
  25.0 13.2 split_up.1
  40.6 12.3 dynamic_update_slice.56
  52.9 8.1 broadcast_in_dim.37
  69.8 26.9 %all-gather.3.cloned.1.call-done = bf16[2048,2560]{1,0:T(8,128)(2,1)} async-done(((bf16[256,2560]{1,0:T(8,128)(2,1)}), bf16[2048,2560]{1,0:T(8,128)(2,1)}) %all-gather.3.cloned.1.call-update) | async-done | bytes 10485776 | tf_op jit(solution)/shard_map/all_gather | solution.py:351
  96.8 22.4 convolution_add_fusion.z_ref
  119.1 33.2 %attend.1 = (bf16[1536,2560]{1,0:T(8,128)(2,1)}, bf16[1536,2048]{1,0:T(8,128)(2,1)}) custom-call(f32[1536,2560]{1,0:T(8,128)} %convolution_add_fusion.z_ref, f32[1536,128]{1,0:T(8,128)S(1)} %get-tuple-element.193.cos_ref, f32[1536,128]{1,0:T(8,128)S(1)} %get-tuple-element.192.sin_ref), custom_call_target="tpu_custom_call" | custom-call | flops 19327352832 | bytes 31457280 | tf_op jit(solution)/shard_map/attend/pallas_call | solution.py:159
  152.3 29.9 %all-gather.5.cloned.1.call-done = bf16[2048,2048]{1,0:T(8,128)(2,1)} async-done(((bf16[256,2048]{1,0:T(8,128)(2,1)}), bf16[2048,2048]{1,0:T(8,128)(2,1)}) %all-gather.5.cloned.1.call-update) | async-done | bytes 8388624 | tf_op jit(solution)/shard_map/all_gather | solution.py:351
  182.2 18.9 fusion.19
  238.2 47.1 %collective-permute-done.9 = bf16[256,5632]{1,0:T(8,128)(2,1)S(1)} collective-permute-done((bf16[256,5632]{1,0:T(8,128)(2,1)}, bf16[256,5632]{1,0:T(8,128)(2,1)S(1)}, u32[]{:S(2)}, u32[]{:S(2)}) %collective-permute-start.9) | collective-permute-done | bytes 2883616 | tf_op jit(solution)/shard_map/ppermute | solution.py:348
  287.0 60.1 %collective-permute-done.10 = bf16[256,5632]{1,0:T(8,128)(2,1)S(1)} collective-permute-done((bf16[256,5632]{1,0:T(8,128)(2,1)}, bf16[256,5632]{1,0:T(8,128)(2,1)S(1)}, u32[]{:S(2)}, u32[]{:S(2)}) %collective-permute-start.10) | collective-permute-done | bytes 2883616 | tf_op jit(solution)/shard_map/ppermute | solution.py:348
  348.8 59.4 %collective-permute-done.11 = bf16[256,5632]{1,0:T(8,128)(2,1)S(1)} collective-permute-done((bf16[256,5632]{1,0:T(8,128)(2,1)}, bf16[256,5632]{1,0:T(8,128)(2,1)S(1)}, u32[]{:S(2)}, u32[]{:S(2)}) %collective-permute-start.11) | collective-permute-done | bytes 2883616 | tf_op jit(solution)/shard_map/ppermute | solution.py:348
  416.5 12.4 dynamic_update_slice.54
  432.6 91.4 %up_act.2 = (bf16[6144,2816]{1,0:T(8,128)(2,1)}, bf16[6144,2816]{1,0:T(8,128)(2,1)}, bf16[6144,2816]{1,0:T(8,128)(2,1)}) custom-call(bf16[6144,2048]{1,0:T(8,128)(2,1)} %constant_dynamic-update-slice_fusion.15.m_ref, bf16[2048,5632]{1,0:T(8,128)(2,1)} %constant_dynamic-update-slice_fusion.6.w_ref), custom_call_target="tpu_custom_call" | custom-call | flops 70866960384 | bytes 87556096 | tf_op jit(solution)/shard_map/up_act/pallas_call | solution.py:208
  524.0 42.1 %collective-permute-done.12 = bf16[1536,2048]{1,0:T(8,128)(2,1)} collective-permute-done((bf16[1536,2048]{1,0:T(8,128)(2,1)}, bf16[1536,2048]{1,0:T(8,128)(2,1)}, u32[]{:S(2)}, u32[]{:S(2)}) %collective-permute-start.12) | collective-permute-done | bytes 6291488 | tf_op jit(solution)/shard_map/ppermute | solution.py:348
  583.1 91.2 %up_act.3 = (bf16[6144,2816]{1,0:T(8,128)(2,1)}, bf16[6144,2816]{1,0:T(8,128)(2,1)}, bf16[6144,2816]{1,0:T(8,128)(2,1)}) custom-call(bf16[6144,2048]{1,0:T(8,128)(2,1)} %constant_dynamic-update-slice_fusion.3.m_ref, bf16[2048,5632]{1,0:T(8,128)(2,1)} %constant_dynamic-update-slice_fusion.6.w_ref, ...), custom_call_target="tpu_custom_call", output_to_operand_aliasing={{0}: (2, {}), {1}: (3, {}), {2}: (4, {})} | custom-call | flops 70866960384 | bytes 87556096 | tf_op jit(solution)/shard_map/up_act/pallas_call | solution.py:208
  674.3 16.0 collective-permute-done.15
  690.3 14.0 collective-permute-done.14
  710.2 24.9 %fusion.44 = f32[1536,2048]{1,0:T(8,128)} fusion(bf16[2816,2048]{1,0:T(8,128)(2,1)} %constant_dynamic-update-slice_fusion.2.wd_ref, bf16[6144,2816]{1,0:T(8,128)(2,1)} %get-tuple-element.163), kind=kOutput, calls=%fused_computation.57 | convolution fusion | flops 17716740096 | bytes 32768000 | tf_op jit(solution)/shard_map/dot_general | solution.py:32
  735.6 22.5 fusion.42
  777.6 46.3 %fusion.10 = f32[1408,2048]{1,0:T(8,128)} fusion(bf16[6144,2048]{1,0:T(8,128)(2,1)} %constant_dynamic-update-slice_fusion.dy_ref, bf16[6144,2816]{1,0:T(8,128)(2,1)} %get-tuple-element.163, s32[]{:T(128)S(6)} %select_n.165), kind=kOutput, calls=%fused_computation.14 | convolution fusion | flops 35433480192 | bytes 54001668 | tf_op jit(solution)/shard_map/dot_general | solution.py:32
  823.9 112.3 %up_back.1 = bf16[6144,5632]{1,0:T(8,128)(2,1)} custom-call(bf16[6144,2048]{1,0:T(8,128)(2,1)} %constant_dynamic-update-slice_fusion.dy_ref, bf16[2816,2048]{1,0:T(8,128)(2,1)} %constant_dynamic-update-slice_fusion.2.wd_ref, bf16[6144,2816]{1,0:T(8,128)(2,1)} %get-tuple-element.132.g_ref, bf16[6144,2816]{1,0:T(8,128)(2,1)} %get-tuple-element.133.l_ref), custom_call_target="tpu_custom_call" | custom-call | flops 70866960384 | bytes 175112192 | tf_op jit(solution)/shard_map/up_back/pallas_call | solution.py:237
  936.2 44.7 %fusion.2 = f32[1536,2048]{1,0:T(8,128)} fusion(bf16[2048,5632]{1,0:T(8,128)(2,1)} %constant_dynamic-update-slice_fusion.6.w_ref, bf16[6144,5632]{1,0:T(8,128)(2,1)} %up_back.1), kind=kOutput, calls=%fused_computation.6 | convolution fusion | flops 35433480192 | bytes 52953088 | tf_op jit(solution)/shard_map/dot_general | solution.py:32
  980.9 46.8 %fusion.53 = f32[512,5632]{1,0:T(8,128)} fusion(bf16[6144,5632]{1,0:T(8,128)(2,1)} %up_back.1, bf16[6144,2048]{1,0:T(8,128)(2,1)} %constant_dynamic-update-slice_fusion.3.m_ref, s32[]{:T(128)S(6)} %select_n.166), kind=kOutput, calls=%fused_computation.63 | convolution fusion | flops 35433480192 | bytes 87031808 | tf_op jit(solution)/shard_map/dot_general | solution.py:32
  1027.7 47.9 %fusion.48 = f32[1536,2048]{1,0:T(8,128)} fusion(f32[1536,2048]{1,0:T(8,128)} %collective-permute-done.18, bf16[2048,5632]{1,0:T(8,128)(2,1)} %constant_dynamic-update-slice_fusion.6.w_ref, bf16[6144,5632]{1,0:T(8,128)(2,1)} %up_back.1), kind=kOutput, calls=%fused_computation.59 | convolution fusion | flops 35436625920 | bytes 65536000 | tf_op jit(solution)/shard_map/dot_general | solution.py:32
  1075.6 46.4 %fusion.51 = f32[512,5632]{1,0:T(8,128)} fusion(bf16[6144,5632]{1,0:T(8,128)(2,1)} %up_back.1, bf16[6144,2048]{1,0:T(8,128)(2,1)} %constant_dynamic-update-slice_fusion.3.m_ref, s32[]{:T(128)S(6)} %select_n.167), kind=kOutput, calls=%fused_computation.61 | convolution fusion | flops 35433480192 | bytes 87031808 | tf_op jit(solution)/shard_map/dot_general | solution.py:32
  1122.0 81.5 %fusion.36 = f32[1024,5632]{1,0:T(8,128)} fusion(bf16[6144,5632]{1,0:T(8,128)(2,1)} %up_back.1, bf16[6144,2048]{1,0:T(8,128)(2,1)} %constant_dynamic-update-slice_fusion.3.m_ref, s32[]{:T(128)S(6)} %select_n.168), kind=kOutput, calls=%fused_computation.48 | convolution fusion | flops 70866960384 | bytes 104857600 | tf_op jit(solution)/shard_map/dot_general | solution.py:32
  1203.8 44.7 %fusion.6 = f32[1536,2048]{1,0:T(8,128)} fusion(bf16[2048,5632]{1,0:T(8,128)(2,1)} %constant_dynamic-update-slice_fusion.6.w_ref, bf16[6144,5632]{1,0:T(8,128)(2,1)} %up_back.1), kind=kOutput, calls=%fused_computation.10 | convolution fusion | flops 35433480192 | bytes 52953088 | tf_op jit(solution)/shard_map/dot_general | solution.py:32
  1248.8 44.6 %fusion.4 = f32[1536,2048]{1,0:T(8,128)} fusion(bf16[2048,5632]{1,0:T(8,128)(2,1)} %constant_dynamic-update-slice_fusion.6.w_ref, bf16[6144,5632]{1,0:T(8,128)(2,1)} %up_back.1), kind=kOutput, calls=%fused_computation.8 | convolution fusion | flops 35433480192 | bytes 52953088 | tf_op jit(solution)/shard_map/dot_general | solution.py:32
  1293.5 183.2 %collective-permute-done.20 = f32[1536,2048]{1,0:T(8,128)} collective-permute-done((f32[1536,2048]{1,0:T(8,128)}, f32[1536,2048]{1,0:T(8,128)}, u32[]{:S(2)}, u32[]{:S(2)}) %collective-permute-start.20) | collective-permute-done | bytes 12582944 | tf_op jit(solution)/shard_map/ppermute | solution.py:348
  1476.6 21.3 fusion.22
  1497.9 12.1 fusion.18
  1510.0 21.8 fusion.55
  1534.4 21.7 convolution_convert_fusion.dctx_ref
  1556.1 46.0 %attend_back.1 = (bf16[1536,2560]{1,0:T(8,128)(2,1)}, f32[1,2560]{1,0:T(1,128)S(1)}) custom-call(bf16[1536,2560]{1,0:T(8,128)(2,1)} %get-tuple-element.139.qkv_ref, bf16[1536,2048]{1,0:T(8,128)(2,1)} %convolution_convert_fusion.dctx_ref, f32[1536,128]{1,0:T(8,128)S(1)} %get-tuple-element.193.cos_ref, f32[1536,128]{1,0:T(8,128)S(1)} %get-tuple-element.192.sin_ref), custom_call_target="tpu_custom_call" | custom-call | flops 48318382080 | bytes 31457280 | tf_op jit(solution)/shard_map/attend_back/pallas_call | solution.py:177
  1602.1 22.1 fusion.71
  1624.2 23.0 fusion.72
  1647.2 24.8 fusion.40
  1672.0 508.7 %collective-permute-done.22 = f32[1408,2048]{1,0:T(8,128)} collective-permute-done((f32[1408,2048]{1,0:T(8,128)}, f32[1408,2048]{1,0:T(8,128)}, u32[]{:S(2)}, u32[]{:S(2)}) %collective-permute-start.22) | collective-permute-done | bytes 11534368 | tf_op jit(solution)/shard_map/ppermute | solution.py:348
  2182.4 12.8 dynamic-slice_add_fusion
  2195.7 9.0 fusion.35
  2205.1 55.5 %slice_add_fusion = f32[1376,2048]{1,0:T(8,128)} fusion(f32[1408,2048]{1,0:T(8,128)} %collective-permute-done.22, bf16[6144,2048]{1,0:T(8,128)(2,1)} %constant_dynamic-update-slice_fusion.dy_ref, bf16[6144,2816]{1,0:T(8,128)(2,1)} %get-tuple-element.163, s32[]{:T(128)S(6)} %select_n.164), kind=kOutput, calls=%fused_computation.50 | convolution fusion | flops 34630991872 | bytes 65011716 | tf_op jit(solution)/shard_map/dot_general | solution.py:32
  2262.2 15.9 fusion.30
  2278.1 43.9 %collective-permute-done.26 = f32[2,832]{1,0:T(2,128)S(1)} collective-permute-done((f32[2,832]{1,0:T(2,128)S(1)}, f32[2,832]{1,0:T(2,128)S(1)}, u32[]{:S(2)}, u32[]{:S(2)}) %collective-permute-start.26) | collective-permute-done | bytes 6688 | tf_op jit(solution)/shard_map/ppermute | solution.py:348
  2322.1 22.8 fusion.38
  2344.9 16.5 add_convert_fusion
  2361.5 69.8 %collective-permute-done.19 = f32[512,5632]{1,0:T(8,128)} collective-permute-done((f32[512,5632]{1,0:T(8,128)}, f32[512,5632]{1,0:T(8,128)}, u32[]{:S(2)}, u32[]{:S(2)}) %collective-permute-start.19) | collective-permute-done | bytes 11534368 | tf_op jit(solution)/shard_map/ppermute | solution.py:348
  2431.3 12.9 dynamic-slice_add_fusion.2
  2453.9 21.2 join_up.1
  (164 shorter events, 141.4 us)
Async XLA Ops:
  7.2 89.6 %all-gather.3.cloned.1.call-start = ((), (), s32[]{:S(2)}) async-start(), calls=%async_computation.2 | async-start | bytes 11796480 | tf_op jit(solution)/shard_map/all_gather | solution.py:351
  7.9 174.3 %all-gather.5.cloned.1.call-start = ((), (), s32[]{:S(2)}) async-start(), calls=%async_computation.3 | async-start | bytes 9437184 | tf_op jit(solution)/shard_map/all_gather | solution.py:351
  8.7 2466.5 %reduce-scatter.5.cloned.1.call-start = ((), (), s32[]{:S(2)}) async-start(), calls=%async_computation.5 | async-start | bytes 18874368 | tf_op jit(solution)/shard_map/reduce_scatter | solution.py:354
  9.5 8.8 collective-permute-start
  18.3 4.6 collective-permute-start.1
  21.1 41.7 %copy-start.4 = (f32[1536]{0:T(1024)}, f32[1536]{0:T(1024)S(1)}, u32[]{:S(2)}) copy-start(f32[1536]{0:T(1024)S(1)} %rsqrt.20) | copy-start | bytes 18436
  22.9 15.3 collective-permute-start.2
  38.2 169.7 %collective-permute-start.5 = (bf16[256,5632]{1,0:T(8,128)(2,1)}, bf16[256,5632]{1,0:T(8,128)(2,1)}, u32[]{:S(2)}, u32[]{:S(2)}) collective-permute-start(bf16[256,5632]{1,0:T(8,128)(2,1)} %get-tuple-element.101), channel_id=1, source_target_pairs={{0,1},{1,0},{2,3},{3,2},{4,5},{5,4},{6,7},{7,6}} | collective-permute-start | bytes 8650760 | tf_op jit(solution)/shard_map/ppermute | solution.py:348
  38.3 181.5 %collective-permute-start.6 = (bf16[256,5632]{1,0:T(8,128)(2,1)}, bf16[256,5632]{1,0:T(8,128)(2,1)}, u32[]{:S(2)}, u32[]{:S(2)}) collective-permute-start(bf16[256,5632]{1,0:T(8,128)(2,1)} %get-tuple-element.102), channel_id=1, source_target_pairs={{0,2},{1,3},{2,0},{3,1},{4,6},{5,7},{6,4},{7,5}} | collective-permute-start | bytes 8650760 | tf_op jit(solution)/shard_map/ppermute | solution.py:348
  39.7 185.7 %collective-permute-start.7 = (bf16[256,5632]{1,0:T(8,128)(2,1)}, bf16[256,5632]{1,0:T(8,128)(2,1)}, u32[]{:S(2)}, u32[]{:S(2)}) collective-permute-start(bf16[256,5632]{1,0:T(8,128)(2,1)} %get-tuple-element.103), channel_id=1, source_target_pairs={{0,3},{1,2},{2,1},{3,0},{4,7},{5,6},{6,5},{7,4}} | collective-permute-start | bytes 8650760 | tf_op jit(solution)/shard_map/ppermute | solution.py:348
  40.1 190.6 %collective-permute-start.8 = (bf16[256,5632]{1,0:T(8,128)(2,1)}, bf16[256,5632]{1,0:T(8,128)(2,1)}, u32[]{:S(2)}, u32[]{:S(2)}) collective-permute-start(bf16[256,5632]{1,0:T(8,128)(2,1)} %get-tuple-element.100), channel_id=1, source_target_pairs={{0,4},{1,5},{2,6},{3,7},{4,0},{5,1},{6,2},{7,3}} | collective-permute-start | bytes 8650760 | tf_op jit(solution)/shard_map/ppermute | solution.py:348
  40.5 160.7 %copy-start.8 = (f32[1,2,8,128]{3,1,2,0:T(2,128)}, f32[1,2,8,128]{3,1,2,0:T(2,128)S(1)}, u32[]{:S(2)}) copy-start(f32[1,2,8,128]{3,1,2,0:T(2,128)S(1)} %copy.27) | copy-start | bytes 24580
  40.5 369.5 %collective-permute-start.4 = (bf16[1536,2048]{1,0:T(8,128)(2,1)}, bf16[1536,2048]{1,0:T(8,128)(2,1)}, u32[]{:S(2)}, u32[]{:S(2)}) collective-permute-start(bf16[1536,2048]{1,0:T(8,128)(2,1)} %bitcast.78), channel_id=1, source_target_pairs={{0,1},{1,0},{2,3},{3,2},{4,5},{5,4},{6,7},{7,6}} | collective-permute-start | bytes 18874376 | tf_op jit(solution)/shard_map/ppermute | solution.py:348
  207.9 221.2 %collective-permute-start.3 = (bf16[1536,2048]{1,0:T(8,128)(2,1)}, bf16[1536,2048]{1,0:T(8,128)(2,1)S(1)}, u32[]{:S(2)}, u32[]{:S(2)}) collective-permute-start(bf16[1536,2048]{1,0:T(8,128)(2,1)} %fusion.14), channel_id=1, source_target_pairs={{0,1},{1,0},{2,3},{3,2},{4,5},{5,4},{6,7},{7,6}} | collective-permute-start | bytes 18874376 | tf_op jit(solution)/shard_map/ppermute | solution.py:348
  219.7 65.6 %collective-permute-start.9 = (bf16[256,5632]{1,0:T(8,128)(2,1)}, bf16[256,5632]{1,0:T(8,128)(2,1)S(1)}, u32[]{:S(2)}, u32[]{:S(2)}) collective-permute-start(bf16[256,5632]{1,0:T(8,128)(2,1)} %collective-permute-done.5), channel_id=1, source_target_pairs={{0,4},{1,5},{2,6},{3,7},{4,0},{5,1},{6,2},{7,3}} | collective-permute-start | bytes 8650760 | tf_op jit(solution)/shard_map/ppermute | solution.py:348
  225.5 121.6 %collective-permute-start.10 = (bf16[256,5632]{1,0:T(8,128)(2,1)}, bf16[256,5632]{1,0:T(8,128)(2,1)S(1)}, u32[]{:S(2)}, u32[]{:S(2)}) collective-permute-start(bf16[256,5632]{1,0:T(8,128)(2,1)} %collective-permute-done.6), channel_id=1, source_target_pairs={{0,4},{1,5},{2,6},{3,7},{4,0},{5,1},{6,2},{7,3}} | collective-permute-start | bytes 8650760 | tf_op jit(solution)/shard_map/ppermute | solution.py:348
  230.7 177.5 %collective-permute-start.11 = (bf16[256,5632]{1,0:T(8,128)(2,1)}, bf16[256,5632]{1,0:T(8,128)(2,1)S(1)}, u32[]{:S(2)}, u32[]{:S(2)}) collective-permute-start(bf16[256,5632]{1,0:T(8,128)(2,1)} %collective-permute-done.7), channel_id=1, source_target_pairs={{0,4},{1,5},{2,6},{3,7},{4,0},{5,1},{6,2},{7,3}} | collective-permute-start | bytes 8650760 | tf_op jit(solution)/shard_map/ppermute | solution.py:348
  428.9 137.2 %collective-permute-start.12 = (bf16[1536,2048]{1,0:T(8,128)(2,1)}, bf16[1536,2048]{1,0:T(8,128)(2,1)}, u32[]{:S(2)}, u32[]{:S(2)}) collective-permute-start(bf16[1536,2048]{1,0:T(8,128)(2,1)} %fusion.14), channel_id=1, source_target_pairs={{0,2},{1,3},{2,0},{3,1},{4,6},{5,7},{6,4},{7,5}} | collective-permute-start | bytes 18874376 | tf_op jit(solution)/shard_map/ppermute | solution.py:348
  566.0 10.5 collective-permute-start.13
  566.0 138.2 %collective-permute-start.14 = (bf16[1536,2048]{1,0:T(8,128)(2,1)}, bf16[1536,2048]{1,0:T(8,128)(2,1)}, u32[]{:S(2)}, u32[]{:S(2)}) collective-permute-start(bf16[1536,2048]{1,0:T(8,128)(2,1)} %bitcast.80), channel_id=1, source_target_pairs={{0,2},{1,3},{2,0},{3,1},{4,6},{5,7},{6,4},{7,5}} | collective-permute-start | bytes 18874376 | tf_op jit(solution)/shard_map/ppermute | solution.py:348
  566.3 123.9 %collective-permute-start.15 = (bf16[1376,2048]{1,0:T(8,128)(2,1)}, bf16[1376,2048]{1,0:T(8,128)(2,1)}, u32[]{:S(2)}, u32[]{:S(2)}) collective-permute-start(bf16[1376,2048]{1,0:T(8,128)(2,1)} %param.19), channel_id=1, source_target_pairs={{0,4},{1,5},{2,6},{3,7},{4,0},{5,1},{6,2},{7,3}} | collective-permute-start | bytes 16908296 | tf_op jit(solution)/shard_map/ppermute | solution.py:348
  735.1 23.0 collective-permute-start.17
  735.1 29.4 %collective-permute-start.16 = (bf16[1536,2048]{1,0:T(8,128)(2,1)}, bf16[1536,2048]{1,0:T(8,128)(2,1)}, u32[]{:S(2)}, u32[]{:S(2)}) collective-permute-start(bf16[1536,2048]{1,0:T(8,128)(2,1)} %collective-permute-done.14), channel_id=1, source_target_pairs={{0,1},{1,0},{2,3},{3,2},{4,5},{5,4},{6,7},{7,6}} | collective-permute-start | bytes 18874376 | tf_op jit(solution)/shard_map/ppermute | solution.py:348
  980.9 46.8 %collective-permute-start.18 = (f32[1536,2048]{1,0:T(8,128)}, f32[1536,2048]{1,0:T(8,128)}, u32[]{:S(2)}, u32[]{:S(2)}) collective-permute-start(f32[1536,2048]{1,0:T(8,128)} %fusion.2), channel_id=1, source_target_pairs={{0,1},{1,0},{2,3},{3,2},{4,5},{5,4},{6,7},{7,6}} | collective-permute-start | bytes 37748744 | tf_op jit(solution)/shard_map/ppermute | solution.py:348
  1203.5 273.1 %collective-permute-start.20 = (f32[1536,2048]{1,0:T(8,128)}, f32[1536,2048]{1,0:T(8,128)}, u32[]{:S(2)}, u32[]{:S(2)}) collective-permute-start(f32[1536,2048]{1,0:T(8,128)} %fusion.48), channel_id=1, source_target_pairs={{0,2},{1,3},{2,0},{3,1},{4,6},{5,7},{6,4},{7,5}} | collective-permute-start | bytes 37748744 | tf_op jit(solution)/shard_map/ppermute | solution.py:348
  1248.5 228.1 %copy-start.9 = (f32[1,2,8,128]{3,1,2,0:T(2,128)S(1)}, f32[1,2,8,128]{3,1,2,0:T(2,128)}, u32[]{:S(2)}) copy-start(f32[1,2,8,128]{3,1,2,0:T(2,128)} %copy-done.8) | copy-start | bytes 24580
  1248.5 228.1 %copy-start.11 = (f32[1536]{0:T(1024)S(1)}, f32[1536]{0:T(1024)}, u32[]{:S(2)}) copy-start(f32[1536]{0:T(1024)} %copy-done.10) | copy-start | bytes 18436
  1248.6 228.1 %collective-permute-start.21 = (f32[1536,2048]{1,0:T(8,128)}, f32[1536,2048]{1,0:T(8,128)}, u32[]{:S(2)}, u32[]{:S(2)}) collective-permute-start(f32[1536,2048]{1,0:T(8,128)} %fusion.6), channel_id=1, source_target_pairs={{0,1},{1,0},{2,3},{3,2},{4,5},{5,4},{6,7},{7,6}} | collective-permute-start | bytes 37748744 | tf_op jit(solution)/shard_map/ppermute | solution.py:348
  1293.4 204.5 %copy-start.1 = (bf16[1536,2048]{1,0:T(8,128)(2,1)S(1)}, bf16[1536,2048]{1,0:T(8,128)(2,1)}, u32[]{:S(2)}) copy-start(bf16[1536,2048]{1,0:T(8,128)(2,1)} %copy-done) | copy-start | bytes 18874372
  1293.4 204.5 %copy-start.2 = (bf16[3,512,2048]{2,1,0:T(8,128)(2,1)S(1)}, bf16[3,512,2048]{2,1,0:T(8,128)(2,1)}, u32[]{:S(2)}) copy-start(bf16[3,512,2048]{2,1,0:T(8,128)(2,1)} %param.12) | copy-start | bytes 18874372
  1531.8 943.3 %reduce-scatter.3.cloned.1.call-start = ((), (), s32[]{:S(2)}) async-start(), calls=%async_computation.4 | async-start | bytes 23592960 | tf_op jit(solution)/shard_map/reduce_scatter | solution.py:354
  1531.9 650.5 %collective-permute-start.29 = (f32[512,5632]{1,0:T(8,128)}, f32[512,5632]{1,0:T(8,128)}, u32[]{:S(2)}, u32[]{:S(2)}) collective-permute-start(f32[512,5632]{1,0:T(8,128)} %fusion.53), channel_id=1, source_target_pairs={{0,4},{1,5},{2,6},{3,7},{4,0},{5,1},{6,2},{7,3}} | collective-permute-start | bytes 34603016 | tf_op jit(solution)/shard_map/ppermute | solution.py:348
  1533.8 646.8 %collective-permute-start.22 = (f32[1408,2048]{1,0:T(8,128)}, f32[1408,2048]{1,0:T(8,128)}, u32[]{:S(2)}, u32[]{:S(2)}) collective-permute-start(f32[1408,2048]{1,0:T(8,128)} %fusion.10), channel_id=1, source_target_pairs={{0,4},{1,5},{2,6},{3,7},{4,0},{5,1},{6,2},{7,3}} | collective-permute-start | bytes 34603016 | tf_op jit(solution)/shard_map/ppermute | solution.py:348
  1533.9 788.1 %collective-permute-start.24 = (f32[1536,2048]{1,0:T(8,128)}, f32[1536,2048]{1,0:T(8,128)}, u32[]{:S(2)}, u32[]{:S(2)}) collective-permute-start(f32[1536,2048]{1,0:T(8,128)} %add.224), channel_id=1, source_target_pairs={{0,2},{1,3},{2,0},{3,1},{4,6},{5,7},{6,4},{7,5}} | collective-permute-start | bytes 37748744 | tf_op jit(solution)/shard_map/ppermute | solution.py:348
  1534.4 67.7 %slice-start.5 = ((s8[6291456]{0:T(1024)(128)(4,1)}), s8[2097152]{0:T(1024)(128)(4,1)S(1)}, s32[]{:S(2)}) async-start(s8[6291456]{0:T(1024)(128)(4,1)} %bitcast.85), calls=%async_computation.11 | async-start | bytes 4194304
  1556.1 46.0 %slice-start.6 = ((s8[6291456]{0:T(1024)(128)(4,1)}), s8[4194304]{0:T(1024)(128)(4,1)S(1)}, s32[]{:S(2)}) async-start(s8[6291456]{0:T(1024)(128)(4,1)} %bitcast.85), calls=%async_computation.12 | async-start | bytes 8388608
  2180.7 141.4 %collective-permute-start.23 = (f32[1536,2048]{1,0:T(8,128)}, f32[1536,2048]{1,0:T(8,128)}, u32[]{:S(2)}, u32[]{:S(2)}) collective-permute-start(f32[1536,2048]{1,0:T(8,128)} %fusion.40), channel_id=1, source_target_pairs={{0,1},{1,0},{2,3},{3,2},{4,5},{5,4},{6,7},{7,6}} | collective-permute-start | bytes 37748744 | tf_op jit(solution)/shard_map/ppermute | solution.py:348
  2180.7 250.6 %collective-permute-start.19 = (f32[512,5632]{1,0:T(8,128)}, f32[512,5632]{1,0:T(8,128)}, u32[]{:S(2)}, u32[]{:S(2)}) collective-permute-start(f32[512,5632]{1,0:T(8,128)} %fusion.51), channel_id=1, source_target_pairs={{0,4},{1,5},{2,6},{3,7},{4,0},{5,1},{6,2},{7,3}} | collective-permute-start | bytes 34603016 | tf_op jit(solution)/shard_map/ppermute | solution.py:348
  2195.3 253.8 %collective-permute-start.30 = (f32[256,5632]{1,0:T(8,128)}, f32[256,5632]{1,0:T(8,128)}, u32[]{:S(2)}, u32[]{:S(2)}) collective-permute-start(f32[256,5632]{1,0:T(8,128)} %get-tuple-element.183), channel_id=1, source_target_pairs={{0,2},{1,3},{2,0},{3,1},{4,6},{5,7},{6,4},{7,5}} | collective-permute-start | bytes 17301512 | tf_op jit(solution)/shard_map/ppermute | solution.py:348
  2205.1 55.5 %collective-permute-start.25 = (f32[4,832]{1,0:T(4,128)S(1)}, f32[4,832]{1,0:T(4,128)S(1)}, u32[]{:S(2)}, u32[]{:S(2)}) collective-permute-start(f32[4,832]{1,0:T(4,128)S(1)} %bitcast.93), channel_id=1, source_target_pairs={{0,1},{1,0},{2,3},{3,2},{4,5},{5,4},{6,7},{7,6}} | collective-permute-start | bytes 39944 | tf_op jit(solution)/shard_map/ppermute | solution.py:348
  2260.6 61.4 %slice-start.2 = ((s8[11534336]{0:T(1024)(128)(4,1)}), s8[4194304]{0:T(1024)(128)(4,1)S(1)}, s32[]{:S(2)}) async-start(s8[11534336]{0:T(1024)(128)(4,1)} %bitcast.81), calls=%async_computation.8 | async-start | bytes 8388608
  2260.7 61.4 %slice-start.3 = ((s8[11534336]{0:T(1024)(128)(4,1)}), s8[4194304]{0:T(1024)(128)(4,1)S(1)}, s32[]{:S(2)}) async-start(s8[11534336]{0:T(1024)(128)(4,1)} %bitcast.81), calls=%async_computation.9 | async-start | bytes 8388608
  2260.7 61.4 %slice-start.4 = ((s8[11534336]{0:T(1024)(128)(4,1)}), s8[3145728]{0:T(1024)(128)(4,1)S(1)}, s32[]{:S(2)}) async-start(s8[11534336]{0:T(1024)(128)(4,1)} %bitcast.81), calls=%async_computation.10 | async-start | bytes 6291456
  2260.7 61.4 %collective-permute-start.26 = (f32[2,832]{1,0:T(2,128)S(1)}, f32[2,832]{1,0:T(2,128)S(1)}, u32[]{:S(2)}, u32[]{:S(2)}) collective-permute-start(f32[2,832]{1,0:T(2,128)S(1)} %bitcast.94), channel_id=1, source_target_pairs={{0,2},{1,3},{2,0},{3,1},{4,6},{5,7},{6,4},{7,5}} | collective-permute-start | bytes 19976 | tf_op jit(solution)/shard_map/ppermute | solution.py:348
  2322.0 127.0 %collective-permute-start.31 = (f32[256,5632]{1,0:T(8,128)}, f32[256,5632]{1,0:T(8,128)}, u32[]{:S(2)}, u32[]{:S(2)}) collective-permute-start(f32[256,5632]{1,0:T(8,128)} %get-tuple-element.182), channel_id=1, source_target_pairs={{0,3},{1,2},{2,1},{3,0},{4,7},{5,6},{6,5},{7,4}} | collective-permute-start | bytes 17301512 | tf_op jit(solution)/shard_map/ppermute | solution.py:348
  2322.0 22.9 slice-start
  2444.2 9.8 collective-permute-start.28
  2444.2 3.6 collective-permute-start.27
  (8 other events, 102.7 us)
Sparse Core Ops, SparseCore 0:
  9.8 86.9 all-gather.2
  98.6 83.5 all-gather.4
  1532.0 175.9 reduce-scatter.4
  1711.9 212.4 reduce-scatter.2
